TPU v7x, 128 devices: a whole 4x4x4 slice. The times are simulated.
128 devices in a mesh: table: 32 (over y, x, core), tensor: 4 (over z).
Axes of the slice: x: 4, y: 4, z: 4, core: 2. Of those that a mesh axis runs over, the one named last changes fastest.
Arguments:
- hidden: bfloat16 [1024, 2560], P('table'), may hold values from -16 to 16
- attn_gain: float32 [2560], replicated, may hold values from 0.6 to 1.4
- q_weight: bfloat16 [2560, 2560], P(None, 'tensor'), may hold values from -1 to 1
- kv_weight: bfloat16 [2560, 2, 512], P(None, None, 'tensor'), may hold values from -0.125 to 0.125
- out_weight: bfloat16 [2560, 2560], P('tensor'), may hold values from -0.125 to 0.125
- key_cache: bfloat16 [1024, 256, 512], P('table', None, 'tensor'), may hold values from -256 to 256
- value_cache: bfloat16 [1024, 256, 512], P('table', None, 'tensor'), may hold values from -6 to 6
- cache_lengths: int32 [1024], P('table'), may hold values from 64 to 256
- table: bfloat16 [131072, 1280], P('table'), may hold values from -6 to 6
- key_proj: bfloat16 [1280, 2560], P(None, 'tensor'), may hold values from -0.15625 to 0.15625
- value_proj: bfloat16 [1280, 2560], P(None, 'tensor'), may hold values from -0.15625 to 0.15625
- lookup_ids: int32 [1024, 16], P('table'), may hold values from 0 to 131071, as said below
Outputs:
- mixed: bfloat16 [1024, 2560], P('table', 'tensor')
Inputs may be any that keep to these rules, and one draw needn't show every extreme that they name: `lookup_ids`: within the 32 sequences of one index of table (aligned blocks of rows), at most 32 ids lie in the range of 4096 rows of any one owner (owner = id // 4096); in every draw one owner gets exactly 32 ids from every block.
All inputs are finite; a program needn't handle non-finite values.
Results may differ from a plain program's by a relative error of at most 0.007.
Values may be sent and summed in bfloat16 or wider, within the bound.
No kernel may reach another device: no remote copies, remote signals or barrier semaphores. Data moves between devices by JAX's collectives and lax.ppermute only.
A program may use at most 128 MiB of HBM per device.

v0:
```python
import math

import jax
import jax.numpy as jnp
from jax import lax
from jax.sharding import PartitionSpec as P

HEAD_DIM = 128


epsilon = 1e-06


def copy_for_each(array, axis):
    peers = lax.axis_size(axis)
    return lax.all_to_all(
        jnp.broadcast_to(array[None], (peers, *array.shape)), axis, 0, 0, tiled=True
    )


def taken_together(array, axis):
    everything = copy_for_each(array, axis)
    return jnp.sum(everything, axis=0)


def packed_total(arrays, axis):
    ends = [0]
    for a in arrays:
        ends.append(ends[-1] + a.size)
    so_far = taken_together(jnp.concatenate([a.ravel() for a in arrays]), axis)
    return tuple((so_far[b:e].reshape(a.shape) for a, b, e in zip(arrays, ends, ends[1:])))


def cut_along(array, dim, peers):
    lengths = array.shape
    blocks = array.reshape(*lengths[:dim], peers, lengths[dim] // peers, *lengths[dim + 1 :])
    return jnp.moveaxis(blocks, dim, 0)


def summed_on_arrival(array, axis, dim):
    peers = lax.axis_size(axis)
    blocks = lax.all_to_all(cut_along(array, dim, peers), axis, 0, 0, tiled=True)
    return jnp.sum(blocks.astype(jnp.float32), axis=0)


def local(
    hidden,
    attn_gain,
    q_weight,
    kv_weight,
    out_weight,
    key_cache,
    value_cache,
    cache_lengths,
    table,
    key_proj,
    value_proj,
    lookup_ids,
):
    seq_count, width = hidden.shape
    tensor_count = lax.axis_size("tensor")
    tensor_index = lax.axis_index("tensor")
    slice_width = width // tensor_count
    hidden_f32 = hidden.astype(jnp.float32)
    normed = hidden_f32 * lax.rsqrt(
        jnp.mean(hidden_f32 * hidden_f32, axis=1, keepdims=True) + epsilon
    )
    attn_in = (normed * attn_gain).astype(jnp.bfloat16)
    head_dim = HEAD_DIM
    ctx_len = key_cache.shape[1]
    kv_width = kv_weight.shape[2]
    kv_local = kv_width // head_dim
    group_size = q_weight.shape[1] // kv_width
    inv_scale = 1.0 / math.sqrt(head_dim)
    query_proj = jnp.dot(attn_in, q_weight, preferred_element_type=jnp.float32).astype(jnp.bfloat16)
    new_kv = jnp.dot(
        attn_in, kv_weight.reshape(width, 2 * kv_width), preferred_element_type=jnp.float32
    ).astype(jnp.bfloat16)
    query_heads = query_proj.reshape(seq_count, kv_local, group_size, head_dim)
    new_key = new_kv[:, :kv_width].reshape(seq_count, kv_local, head_dim)
    new_value = new_kv[:, kv_width:].reshape(seq_count, kv_local, head_dim)
    key_blocks = key_cache.reshape(seq_count, ctx_len, kv_local, head_dim)
    value_blocks = value_cache.reshape(seq_count, ctx_len, kv_local, head_dim)
    attention_energies = (
        jnp.einsum("skgh,sckh->skgc", query_heads, key_blocks, preferred_element_type=jnp.float32)
        * inv_scale
    )
    own_score = (
        jnp.einsum("skgh,skh->skg", query_heads, new_key, preferred_element_type=jnp.float32)
        * inv_scale
    )
    valid_mask = jnp.arange(ctx_len, dtype=jnp.int32)[None, :] < cache_lengths[:, None]
    masked = jnp.where(valid_mask[:, None, None, :], attention_energies, -1e30)
    row_max = jnp.maximum(jnp.max(masked, axis=-1), own_score)
    weights = jnp.exp(masked - row_max[..., None])
    own_weight = jnp.exp(own_score - row_max)
    denom_sum = jnp.sum(weights, axis=-1) + own_weight
    weights_bf = (weights / denom_sum[..., None]).astype(jnp.bfloat16)
    own_prob = (own_weight / denom_sum).astype(jnp.bfloat16)
    context = jnp.einsum(
        "skgc,sckh->skgh", weights_bf, value_blocks, preferred_element_type=jnp.float32
    )
    context = (
        context
        + own_prob.astype(jnp.float32)[..., None] * new_value.astype(jnp.float32)[:, :, None, :]
    )
    context = context.reshape(seq_count, -1).astype(jnp.bfloat16)
    attention = jnp.dot(context, out_weight, preferred_element_type=jnp.float32)
    rows_dev, emb_width = table.shape
    table_count = lax.axis_size("table")
    flat_ids = lookup_ids.reshape(-1)
    requests = flat_ids.shape[0]
    capacity = max(2, 2 * requests // table_count)
    owner_of = flat_ids // rows_dev
    local_row = flat_ids - owner_of * rows_dev
    positions = jnp.arange(requests, dtype=jnp.int32)
    earlier = (owner_of[None, :] == owner_of[:, None]) & (positions[None, :] < positions[:, None])
    rank_of = jnp.sum(earlier.astype(jnp.int32), axis=1)
    slot_of = owner_of * capacity + rank_of
    outgoing = jnp.full((table_count * capacity,), -1, jnp.int32).at[slot_of].set(local_row)
    outgoing = outgoing.reshape(table_count, capacity)
    wanted = jnp.take(
        table,
        jnp.maximum(lax.all_to_all(outgoing, "table", split_axis=0, concat_axis=0, tiled=True), 0),
        axis=0,
    )
    replies = lax.all_to_all(wanted, "table", split_axis=0, concat_axis=0, tiled=True)
    mem_rows = jnp.take(replies.reshape(table_count * capacity, replies.shape[2]), slot_of, axis=0)
    lookups = lookup_ids.shape[1]
    mem_key = jnp.dot(mem_rows, key_proj, preferred_element_type=jnp.float32).reshape(
        seq_count, lookups, slice_width
    )
    mem_value = jnp.dot(mem_rows, value_proj, preferred_element_type=jnp.float32).reshape(
        seq_count, lookups, slice_width
    )
    normed_slice = lax.dynamic_slice_in_dim(normed, tensor_index * slice_width, slice_width, 1)
    cross_term = jnp.sum(mem_key * normed_slice[:, None, :], axis=-1)
    square_sum = jnp.sum(mem_key * mem_key, axis=-1)
    cross_term, square_sum = packed_total((cross_term, square_sum), "tensor")
    gating = jax.nn.sigmoid(cross_term * lax.rsqrt(square_sum / width + epsilon) / math.sqrt(width))
    memory = jnp.sum(gating[..., None] * mem_value, axis=1)
    attention_part = summed_on_arrival(attention.astype(jnp.bfloat16), "tensor", 1)
    residual = lax.dynamic_slice_in_dim(hidden_f32, tensor_index * slice_width, slice_width, 1)
    return (residual + attention_part + memory).astype(jnp.bfloat16)


def solution(mesh):
    return jax.shard_map(
        local,
        mesh=mesh,
        in_specs=(
            P("table", None),
            P(),
            P(None, "tensor"),
            P(None, None, "tensor"),
            P("tensor", None),
            P("table", None, "tensor"),
            P("table", None, "tensor"),
            P("table"),
            P("table", None),
            P(None, "tensor"),
            P(None, "tensor"),
            P("table", None),
        ),
        out_specs=P("table", "tensor"),
        check_vma=False,
    )
```

profile of v0, /device:TPU:0, one launch (start us, length us, event | category | flops | bytes accessed | tf_op | source)
XLA Modules:
  0.0 111.3 jit_solution(8740786368264671054)
XLA Ops:
  0.0 0.0 copy-start
  0.0 0.9 copy.27
  0.9 0.1 reshape.327
  1.0 0.1 reshape.328
  1.1 0.2 convert_reduce_fusion
  1.4 0.0 copy-start.3
  1.4 2.4 %scatter_custom_fusion = s32[1024]{0:T(1024)S(1)} fusion(s32[512]{0:T(512)S(1)} %bitcast.51, s32[512]{0:T(512)S(1)} %get-tuple-element.7, s32[]{:T(128)} %constant.77.clone.1), kind=kCustom, calls=%fused_computation.65 | custom fusion | bytes 4100 | tf_op jit(solution)/shard_map/scatter | solution.py:120
  3.8 0.7 all_to_all.17
  4.5 7.6 %all-to-all-start.1 = ((s32[32,1,32]{2,1,0:T(1,128)}), s32[32,1,32]{2,1,0:T(1,128)}, u32[]{:S(2)}, u32[]{:S(2)}) async-start(s32[32,1,32]{2,1,0:T(1,128)} %all_to_all.17), calls=%async_computation.1 | async-start | bytes 32768 | tf_op jit(solution)/shard_map/all_to_all | solution.py:124
  12.1 1.1 multiply_reduce_fusion.2
  13.2 0.0 copy-done.3
  13.2 0.0 copy-start.5
  13.2 0.6 copy-done.5
  13.8 0.0 copy-start.1
  13.8 2.8 %convolution_convert_fusion.1 = bf16[32,640]{1,0:T(8,128)(2,1)S(1)} fusion(bf16[2560,640]{1,0:T(8,128)(2,1)} %param.14, f32[2560]{0:T(1024)} %param.13, f32[32]{0:T(128)S(1)} %add_rsqrt_fusion, bf16[32,2560]{1,0:T(8,128)(2,1)} %param.12), kind=kOutput, calls=%fused_computation.17 | convolution fusion | flops 105205760 | bytes 3491968 | tf_op jit(solution)/shard_map/dot_general | solution.py:75
  16.5 0.1 reshape.324
  16.6 0.0 copy-done.1
  16.6 1.7 %fusion.6 = bf16[32,256]{1,0:T(8,128)(2,1)S(1)} fusion(bf16[320,8,2,128]{3,2,1,0:T(2,128)(2,1)} %bitcast.53, f32[2560]{0:T(1024)} %param.13, f32[32]{0:T(128)} %copy-done.5, bf16[32,2560]{1,0:T(8,128)(2,1)S(1)} %copy-done.1), kind=kOutput, calls=%fused_computation.18 | convolution fusion | flops 42278912 | bytes 1501312 | tf_op jit(solution)/shard_map/dot_general | solution.py:76
  18.3 0.6 slice_convert_fusion
  18.9 0.1 fusion.17
  19.1 0.1 all-to-all-done.1
  19.2 0.7 broadcast_maximum_fusion
  20.0 1.3 %compare_bitcast_fusion = pred[32,32]{1,0:T(8,128)(4,1)} fusion(s32[32,1,32]{2,0,1:T(8,128)} %bitcast.6), kind=kLoop, calls=%fused_computation.42 | loop fusion | flops 2048 | bytes 5120 | tf_op jit(solution)/shard_map/jit(_take)/le | solution.py:122
  21.3 0.1 reshape.339
  21.3 0.0 copy-start.2
  21.4 11.9 %gather_fusion = bf16[1024,1280]{1,0:T(8,128)(2,1)} fusion(bf16[4096,1280]{1,0:T(8,128)(2,1)} %param.20, s32[1024]{0:T(1024)S(1)} %broadcast_clamp_fusion), kind=kCustom, calls=%fused_computation | custom fusion | bytes 5246976 | tf_op jit(solution)/shard_map/jit(_take)/gather | solution.py:122
  33.3 0.0 copy-done.2
  33.3 3.6 %broadcast_select_fusion = bf16[32,32,1280]{2,1,0:T(8,128)(2,1)} fusion(bf16[32,32,1280]{2,1,0:T(8,128)(2,1)} %bitcast.44, pred[32,32]{1,0:T(8,128)(4,1)S(1)} %copy-done.2), kind=kLoop, calls=%fused_computation.4 | loop fusion | flops 1310720 | bytes 5243904 | tf_op jit(solution)/shard_map/jit(_take)/select_n | solution.py:122
  36.9 0.0 copy-start.7
  36.9 7.4 %all-to-all-start.2 = ((bf16[32,32,1280]{2,1,0:T(8,128)(2,1)}), bf16[32,32,1280]{2,1,0:T(8,128)(2,1)}, u32[]{:S(2)}, u32[]{:S(2)}) async-start(bf16[32,32,1280]{2,1,0:T(8,128)(2,1)} %broadcast_select_fusion), calls=%async_computation.2 | async-start | bytes 5242880 | tf_op jit(solution)/shard_map/all_to_all | solution.py:127
  44.3 0.0 copy-done.7
  44.3 0.1 iota_compare_fusion.1
  44.4 0.0 copy-start.8
  44.4 2.5 %fusion.27 = (f32[32,5]{1,0:T(8,128)S(1)}, f32[32,5,256]{2,1,0:T(8,128)S(1)}) fusion(bf16[32,5,128]{2,1,0:T(8,128)(2,1)S(1)} %reshape.324, bf16[32,256,128]{2,1,0:T(8,128)(2,1)} %param.17, pred[32,256]{1,0:T(8,128)(4,1)S(1)} %iota_compare_fusion.1), kind=kOutput, calls=%fused_computation.74 | convolution fusion | flops 10608480 | bytes 2310784 | tf_op jit(solution)/shard_map/skgh,sckh->skgc/dot_general | solution.py:85
  46.9 0.2 fusion.12
  47.1 0.0 copy-done.8
  47.1 1.2 %fusion.5 = bf16[32,5,128]{2,1,0:T(8,128)(2,1)S(1)} fusion(bf16[32,256,128]{2,1,0:T(8,128)(2,1)S(1)} %copy-done.8, f32[32,5,256]{2,1,0:T(8,128)S(1)} %get-tuple-element.14, f32[32,5]{1,0:T(8,128)S(1)} %get-tuple-element.10, f32[32,5]{1,0:T(8,128)S(1)} %multiply_maximum_fusion, f32[32,128]{1,0:T(8,128)} %get-tuple-element.11, f32[32,5]{1,0:T(8,128)S(1)} %get-tuple-element.9), kind=kOutput, calls=%fused_computation.16 | convolution fusion | flops 10670080 | bytes 2320256 | tf_op jit(solution)/shard_map/skgc,sckh->skgh/dot_general | solution.py:100
  48.3 0.0 copy-done
  48.3 0.0 copy-start.6
  48.3 0.0 copy-start.4
  48.3 0.7 convolution_convert_fusion
  49.0 0.7 copy.52
  49.6 0.0 copy-done.6
  49.6 0.1 broadcast_multiply_fusion
  49.8 30.7 %all-to-all-done.2 = bf16[32,32,1280]{2,1,0:T(8,128)(2,1)} async-done(((bf16[32,32,1280]{2,1,0:T(8,128)(2,1)}), bf16[32,32,1280]{2,1,0:T(8,128)(2,1)}, u32[]{:S(2)}, u32[]{:S(2)}) %all-to-all-start.2) | async-done | bytes 2621472 | tf_op jit(solution)/shard_map/all_to_all | solution.py:127
  80.5 5.3 %all-to-all-start = ((bf16[4,32,640]{2,1,0:T(8,128)(2,1)}), bf16[4,32,640]{2,1,0:T(8,128)(2,1)}, u32[]{:S(2)}, u32[]{:S(2)}) async-start(bf16[4,32,640]{2,1,0:T(8,128)(2,1)} %bitcast.45), calls=%async_computation | async-start | bytes 327680 | tf_op jit(solution)/shard_map/all_to_all | solution.py:42
  85.8 0.0 copy-done.4
  85.8 0.7 convert_element_type.46
  86.5 6.0 %gather_fusion.1 = bf16[512,1280]{1,0:T(8,128)(2,1)} fusion(bf16[1024,1280]{1,0:T(8,128)(2,1)} %bitcast.9, s32[1024]{0:T(1024)S(1)} %pad_clamp_fusion), kind=kCustom, calls=%fused_computation.1 | custom fusion | bytes 2623488 | tf_op jit(solution)/shard_map/jit(_take)/gather | solution.py:128
  92.5 3.2 %fusion.3 = (f32[512]{0:T(512)S(1)}, f32[512]{0:T(512)S(1)}) fusion(f32[32,640]{1,0:T(8,128)S(1)} %constant_dynamic-slice_fusion, bf16[1280,640]{1,0:T(8,128)(2,1)} %param.21, bf16[512,1280]{1,0:T(8,128)(2,1)} %gather_fusion.1, pred[512]{0:T(512)(128)(4,1)S(1)} %compare_and_fusion), kind=kOutput, calls=%fused_computation.9 | convolution fusion | flops 840825856 | bytes 3035648 | tf_op jit(solution)/shard_map/dot_general | solution.py:130
  95.7 0.0 all-to-all-done
  95.7 0.6 broadcast_in_dim.64
  96.3 4.8 %all-to-all-start.3 = ((f32[4,1,1024]{2,1,0:T(1,128)}), f32[4,1,1024]{2,1,0:T(1,128)S(1)}, u32[]{:S(2)}, u32[]{:S(2)}) async-start(f32[4,1,1024]{2,1,0:T(1,128)} %broadcast_in_dim.64), calls=%async_computation.3 | async-start | bytes 32768 | tf_op jit(solution)/shard_map/all_to_all | solution.py:16
  101.1 0.9 convert_reduce_fusion.1
  102.1 4.4 %all-to-all-done.3 = f32[4,1,1024]{2,1,0:T(1,128)S(1)} async-done(((f32[4,1,1024]{2,1,0:T(1,128)}), f32[4,1,1024]{2,1,0:T(1,128)S(1)}, u32[]{:S(2)}, u32[]{:S(2)}) %all-to-all-start.3) | async-done | bytes 16416 | tf_op jit(solution)/shard_map/all_to_all | solution.py:16
  106.5 0.1 reshape.362
  106.6 3.1 %multiply_reduce_fusion = f32[32,640]{1,0:T(8,128)S(1)} fusion(f32[32,16]{1,0:T(8,128)S(1)} %reshape.362, bf16[1280,640]{1,0:T(8,128)(2,1)} %param.22, bf16[512,1280]{1,0:T(8,128)(2,1)} %gather_fusion.1, pred[512]{0:T(512)(128)(4,1)S(1)} %compare_and_fusion), kind=kOutput, calls=%fused_computation.10 | convolution fusion | flops 840151040 | bytes 3033600 | tf_op jit(solution)/shard_map/dot_general | solution.py:133
  109.7 1.5 %add_convert_fusion = bf16[32,640]{1,0:T(8,128)(2,1)} fusion(f32[32,640]{1,0:T(8,128)S(1)} %multiply_reduce_fusion, f32[32,640]{1,0:T(8,128)S(1)} %convert_reduce_fusion.1, f32[32,2560]{1,0:T(8,128)} %convert_element_type.46, s32[]{:T(128)S(6)} %select_n.59), kind=kLoop, calls=%fused_computation.34 | loop fusion | flops 61440 | bytes 286724 | tf_op jit(solution)/shard_map/convert_element_type | solution.py:144
  (12 shorter events, 0.1 us)
Async XLA Ops:
  0.0 48.3 %copy-start = (bf16[640,2560]{1,0:T(8,128)(2,1)S(1)}, bf16[640,2560]{1,0:T(8,128)(2,1)}, u32[]{:S(2)}) copy-start(bf16[640,2560]{1,0:T(8,128)(2,1)} %param.16) | copy-start | bytes 9830404
  1.4 11.8 %copy-start.3 = (s32[512,1]{0,1:T(1,128)}, s32[512,1]{0,1:T(1,128)S(1)}, u32[]{:S(2)}) copy-start(s32[512,1]{0,1:T(1,128)S(1)} %compare_select_fusion) | copy-start | bytes 6148
  4.5 14.7 %all-to-all-start.1 = ((s32[32,1,32]{2,1,0:T(1,128)}), s32[32,1,32]{2,1,0:T(1,128)}, u32[]{:S(2)}, u32[]{:S(2)}) async-start(s32[32,1,32]{2,1,0:T(1,128)} %all_to_all.17), calls=%async_computation.1 | async-start | bytes 32768 | tf_op jit(solution)/shard_map/all_to_all | solution.py:124
  13.2 0.6 copy-start.5
  13.8 2.9 %copy-start.1 = (bf16[32,2560]{1,0:T(8,128)(2,1)S(1)}, bf16[32,2560]{1,0:T(8,128)(2,1)}, u32[]{:S(2)}) copy-start(bf16[32,2560]{1,0:T(8,128)(2,1)} %param.12) | copy-start | bytes 491524
  21.3 11.9 %copy-start.2 = (pred[32,32]{1,0:T(8,128)(4,1)S(1)}, pred[32,32]{1,0:T(8,128)(4,1)}, u32[]{:S(2)}) copy-start(pred[32,32]{1,0:T(8,128)(4,1)} %compare_bitcast_fusion) | copy-start | bytes 3076
  36.9 7.4 %copy-start.7 = (s32[32]{0:T(128)S(1)}, s32[32]{0:T(128)}, u32[]{:S(2)}) copy-start(s32[32]{0:T(128)} %param.19) | copy-start | bytes 388
  36.9 43.6 %all-to-all-start.2 = ((bf16[32,32,1280]{2,1,0:T(8,128)(2,1)}), bf16[32,32,1280]{2,1,0:T(8,128)(2,1)}, u32[]{:S(2)}, u32[]{:S(2)}) async-start(bf16[32,32,1280]{2,1,0:T(8,128)(2,1)} %broadcast_select_fusion), calls=%async_computation.2 | async-start | bytes 5242880 | tf_op jit(solution)/shard_map/all_to_all | solution.py:127
  44.4 2.7 %copy-start.8 = (bf16[32,256,128]{2,1,0:T(8,128)(2,1)S(1)}, bf16[32,256,128]{2,1,0:T(8,128)(2,1)}, u32[]{:S(2)}) copy-start(bf16[32,256,128]{2,1,0:T(8,128)(2,1)} %param.18) | copy-start | bytes 6291460
  48.3 1.4 %copy-start.6 = (f32[32]{0:T(128)S(1)}, f32[32]{0:T(128)}, u32[]{:S(2)}) copy-start(f32[32]{0:T(128)} %copy-done.5) | copy-start | bytes 388
  48.3 37.5 %copy-start.4 = (s32[512,1]{0,1:T(1,128)S(1)}, s32[512,1]{0,1:T(1,128)}, u32[]{:S(2)}) copy-start(s32[512,1]{0,1:T(1,128)} %copy-done.3) | copy-start | bytes 6148
  80.5 15.2 %all-to-all-start = ((bf16[4,32,640]{2,1,0:T(8,128)(2,1)}), bf16[4,32,640]{2,1,0:T(8,128)(2,1)}, u32[]{:S(2)}, u32[]{:S(2)}) async-start(bf16[4,32,640]{2,1,0:T(8,128)(2,1)} %bitcast.45), calls=%async_computation | async-start | bytes 327680 | tf_op jit(solution)/shard_map/all_to_all | solution.py:42
  96.3 10.2 %all-to-all-start.3 = ((f32[4,1,1024]{2,1,0:T(1,128)}), f32[4,1,1024]{2,1,0:T(1,128)S(1)}, u32[]{:S(2)}, u32[]{:S(2)}) async-start(f32[4,1,1024]{2,1,0:T(1,128)} %broadcast_in_dim.64), calls=%async_computation.3 | async-start | bytes 32768 | tf_op jit(solution)/shard_map/all_to_all | solution.py:16
where the time goes:
time: 112 us; the launch traced here: 111 us
  waiting for transfers between devices  35.3 us (32%)
  starting transfers between devices  25.1 us (22%)
  local copies, waits for them, and re-layouts  24.2 us (22%)
  matrix products  15.2 us (14%)
  other arithmetic  11.2 us (10%)
    all_to_all x1, waiting for transfers between devices, local(): lax.all_to_all(wanted, 'table', split_axis=0, concat_axis=0, tiled=True)  30.7 us
    gather x1, local copies, waits for them, and re-layouts, local(): jnp.take(table, jnp.maximum(lax.all_to_all(outgoing, 'table', split_axis=...  11.9 us
    all_to_all x1, starting transfers between devices, local(): lax.all_to_all(outgoing, 'table', split_axis=0, concat_axis=0, tiled=True)  7.56 us
    all_to_all x1, starting transfers between devices, local(): lax.all_to_all(wanted, 'table', split_axis=0, concat_axis=0, tiled=True)  7.43 us
    gather x1, local copies, waits for them, and re-layouts, local(): jnp.take(replies.reshape(table_count * capacity, replies.shape[2]), slot_...  5.98 us
    all_to_all x1, starting transfers between devices, summed_on_arrival(): lax.all_to_all(cut_along(array, dim, peers), axis, 0, 0, tiled=True)  5.3 us
    all_to_all x1, starting transfers between devices, copy_for_each(): lax.all_to_all(jnp.broadcast_to(array[None], (peers, *array.shape)), axis...  4.8 us
    all_to_all x1, waiting for transfers between devices, copy_for_each(): lax.all_to_all(jnp.broadcast_to(array[None], (peers, *array.shape)), axis...  4.41 us
  transfers between devices with their start and end apart: 4, of which 3 were waited for; matrix products, arithmetic and copies ran while one was open for 20% of the time, Pallas kernels for 0%

commit v1 on v0

v1 whole, which is shorter than its diff:
```python
import math

import jax
import jax.numpy as jnp
from jax import lax
from jax.experimental import pallas as pl
from jax.experimental.pallas import tpu as pltpu
from jax.sharding import PartitionSpec as P

HEAD_DIM = 128
EPS = 1e-06
LANES = 128
F32 = jnp.float32
BF16 = jnp.bfloat16
I32 = jnp.int32


def iota(shape, dim):
    return lax.broadcasted_iota(I32, shape, dim)


def ones_where(mask):
    return jnp.where(mask, 1.0, 0.0).astype(BF16)


def mm(a, b):
    return lax.dot_general(a, b, (((1,), (0,)), ((), ())), preferred_element_type=F32)


def mm_nt(a, b):
    return lax.dot_general(a, b, (((1,), (1,)), ((), ())), preferred_element_type=F32)


def mm_tn(a, b):
    return lax.dot_general(a, b, (((0,), (0,)), ((), ())), preferred_element_type=F32)


def two_parts(x):
    high = x.astype(BF16)
    return high, (x - high.astype(F32)).astype(BF16)


def three_parts(x):
    high = x.astype(BF16)
    rest = x - high.astype(F32)
    mid = rest.astype(BF16)
    return high, mid, (rest - mid.astype(F32)).astype(BF16)


def exact_int_mm(left, value):
    return 64.0 * mm(left, (value >> 6).astype(F32).astype(BF16)) + mm(
        left, (value & 63).astype(F32).astype(BF16)
    )


def send_ids_kernel(ids_ref, out_ref):
    peers = out_ref.shape[0]
    out_ref[...] = jnp.broadcast_to(ids_ref[...][None], (peers, *ids_ref.shape))


def slot_map_kernel(first_ref, ids_ref, map_ref, *, rows_dev, owners, seqs, lookups, slots):
    requests = seqs * lookups
    owner = ids_ref[...] // rows_dev
    hit = ones_where(iota((owners, requests), 0) == owner)
    before = ones_where(iota((requests, requests), 0) < iota((requests, requests), 1))
    count = mm(hit, before)
    rank = jnp.sum(count * hit.astype(F32), axis=0, keepdims=True).astype(I32)
    rel = rank - first_ref[0]
    slot = jnp.where((rel >= 0) & (rel < slots), owner * slots + rel, -1)
    placed = ones_where(iota((owners * slots, requests), 0) == slot)
    of_seq = ones_where(iota((seqs, requests), 1) // lookups == iota((seqs, requests), 0))
    map_ref[...] = mm_nt(placed, of_seq).astype(BF16)


def squares_kernel(table_ref, key_ref, out_ref):
    keys = mm(table_ref[...], key_ref[...])
    width = keys.shape[1]
    folded = keys[:, :LANES] * keys[:, :LANES]
    for c in range(LANES, width, LANES):
        part = keys[:, c : c + LANES]
        folded = folded + part * part
    for g in range(keys.shape[0] // LANES):
        block = folded[g * LANES : (g + 1) * LANES, :]
        out_ref[0, g : g + 1, :] = jnp.sum(block.T, axis=0, keepdims=True)


def gather_kernel(
    where_ref, got_ref, table_ref, rows_ref, ids_ref, col_ref, acc_ref, *, rows_dev, askers, slots
):
    step = pl.program_id(0)
    per = got_ref.shape[0] // askers
    total = got_ref.shape[0]
    n_slots = askers * slots

    @pl.when(step == 0)
    def _():
        local = got_ref[...] - where_ref[0] * rows_dev
        mine = (local >= 0) & (local < rows_dev)
        hit = ones_where(mine)
        before = ones_where(iota((LANES, LANES), 0) < iota((LANES, LANES), 1))
        r, c = iota((total, total), 0), iota((total, total), 1)
        earlier = ones_where((r // per == c // per) & (c < r))
        rank = mm(hit, before) + jnp.sum(mm(earlier, hit), axis=1, keepdims=True)
        rel = jnp.where(mine, rank.astype(I32) - where_ref[1], -1)
        lane = iota((total, LANES), 1)
        picked = jnp.zeros((total, LANES), I32)
        for k in range(slots):
            one = jnp.sum(jnp.where(rel == k, local, 0).astype(F32), axis=1, keepdims=True)
            picked = jnp.where(lane == k, one.astype(I32), picked)
        same = ones_where(
            iota((n_slots, total), 1) // per == iota((n_slots, total), 0) // slots
        )
        spread = exact_int_mm(same, picked)
        keep = iota((n_slots, LANES), 1) == iota((n_slots, LANES), 0) % slots
        col = jnp.sum(jnp.where(keep, spread, 0.0), axis=1, keepdims=True).astype(I32)
        col_ref[...] = jnp.broadcast_to(col, (n_slots, LANES))
        ids_ref[...] = jnp.broadcast_to(col, (n_slots, LANES))
        acc_ref[...] = jnp.zeros_like(acc_ref)

    block = table_ref.shape[0]
    col = col_ref[:, :1] - step * block
    chosen = ones_where(iota((n_slots, block), 1) == col)
    acc_ref[...] += mm(chosen, table_ref[...])

    @pl.when(step == pl.num_programs(0) - 1)
    def _():
        rows_ref[...] = acc_ref[...].astype(BF16)


def pick_squares_kernel(ids_ref, sq_ref, out_ref, *, slots):
    ids = ids_ref[...]
    n_slots = ids.shape[0]
    groups = sq_ref.shape[0]
    rowsel = ones_where(iota((n_slots, groups), 1) == ids[:, :1] // LANES)
    high, mid, low = three_parts(sq_ref[...])
    wide = mm(rowsel, high) + (mm(rowsel, mid) + mm(rowsel, low))
    lane = iota((n_slots, LANES), 1)
    value = jnp.sum(jnp.where(lane == ids % LANES, wide, 0.0), axis=1, keepdims=True)
    placed = jnp.where(lane == iota((n_slots, LANES), 0) % slots, value, 0.0)
    out_ref[...] = jnp.sum(placed.reshape(n_slots // slots, slots, LANES), axis=1)


def mix_kernel(rows_ref, map_ref, u_ref, sq_ref, attn_ref, out_ref, *, slots, width):
    rows = rows_ref[...]
    n_slots = rows.shape[0]
    of_seq = map_ref[...].astype(F32)
    u_high, u_low = two_parts(u_ref[...])
    cross_all = mm_nt(rows, u_high) + mm_nt(rows, u_low)
    cross = jnp.sum(cross_all * of_seq, axis=1, keepdims=True)
    owners = sq_ref.shape[0]
    spread = jnp.broadcast_to(sq_ref[...][:, None, :], (owners, slots, LANES)).reshape(n_slots, LANES)
    keep = iota((n_slots, LANES), 1) == iota((n_slots, LANES), 0) % slots
    square = jnp.sum(jnp.where(keep, spread, 0.0), axis=1, keepdims=True)
    gate = jax.nn.sigmoid(cross * lax.rsqrt(square / width + EPS) / math.sqrt(width))
    g_high, g_low = two_parts(of_seq * gate)
    mixed = (mm_tn(g_high, rows) + mm_tn(g_low, rows)).astype(BF16)
    peers, _, out_width = out_ref.shape
    part = width // peers
    for p in range(peers):
        out_ref[p, :, :part] = attn_ref[:, p * part : (p + 1) * part]
        out_ref[p, :, part:] = mixed


def final_kernel(got_ref, value_ref, hidden_ref, out_ref):
    part = out_ref.shape[1]
    total = got_ref[0].astype(F32)
    for p in range(1, got_ref.shape[0]):
        total = total + got_ref[p].astype(F32)
    high, low = two_parts(total[:, part:])
    memory = mm(high, value_ref[...]) + mm(low, value_ref[...])
    out_ref[...] = (hidden_ref[...].astype(F32) + total[:, :part] + memory).astype(BF16)


def whole(shape):
    return pl.BlockSpec(shape, lambda *_: (0,) * len(shape))


def butterfly(x, axis):
    peers = lax.axis_size(axis)
    step = 1
    while step < peers:
        x = x + lax.ppermute(x, axis, [(i, i ^ step) for i in range(peers)])
        step *= 2
    return x


def attention_part(hidden_f32, normed, attn_gain, q_weight, kv_weight, out_weight, key_cache, value_cache, cache_lengths):
    seq_count, width = hidden_f32.shape
    attn_in = (normed * attn_gain).astype(BF16)
    ctx_len = key_cache.shape[1]
    kv_width = kv_weight.shape[2]
    kv_local = kv_width // HEAD_DIM
    group_size = q_weight.shape[1] // kv_width
    inv_scale = 1.0 / math.sqrt(HEAD_DIM)
    query_proj = jnp.dot(attn_in, q_weight, preferred_element_type=F32).astype(BF16)
    new_kv = jnp.dot(
        attn_in, kv_weight.reshape(width, 2 * kv_width), preferred_element_type=F32
    ).astype(BF16)
    query_heads = query_proj.reshape(seq_count, kv_local, group_size, HEAD_DIM)
    new_key = new_kv[:, :kv_width].reshape(seq_count, kv_local, HEAD_DIM)
    new_value = new_kv[:, kv_width:].reshape(seq_count, kv_local, HEAD_DIM)
    key_blocks = key_cache.reshape(seq_count, ctx_len, kv_local, HEAD_DIM)
    value_blocks = value_cache.reshape(seq_count, ctx_len, kv_local, HEAD_DIM)
    energies = (
        jnp.einsum("skgh,sckh->skgc", query_heads, key_blocks, preferred_element_type=F32)
        * inv_scale
    )
    own_score = (
        jnp.einsum("skgh,skh->skg", query_heads, new_key, preferred_element_type=F32) * inv_scale
    )
    valid = jnp.arange(ctx_len, dtype=I32)[None, :] < cache_lengths[:, None]
    masked = jnp.where(valid[:, None, None, :], energies, -1e30)
    row_max = jnp.maximum(jnp.max(masked, axis=-1), own_score)
    weights = jnp.exp(masked - row_max[..., None])
    own_weight = jnp.exp(own_score - row_max)
    denom = jnp.sum(weights, axis=-1) + own_weight
    weights_bf = (weights / denom[..., None]).astype(BF16)
    own_prob = (own_weight / denom).astype(BF16)
    context = jnp.einsum("skgc,sckh->skgh", weights_bf, value_blocks, preferred_element_type=F32)
    context = context + own_prob.astype(F32)[..., None] * new_value.astype(F32)[:, :, None, :]
    context = context.reshape(seq_count, -1).astype(BF16)
    return jnp.dot(context, out_weight, preferred_element_type=F32).astype(BF16)


def local(
    hidden,
    attn_gain,
    q_weight,
    kv_weight,
    out_weight,
    key_cache,
    value_cache,
    cache_lengths,
    table,
    key_proj,
    value_proj,
    lookup_ids,
):
    seqs, width = hidden.shape
    lookups = lookup_ids.shape[1]
    requests = seqs * lookups
    rows_dev, emb = table.shape
    owners = lax.axis_size("table")
    tensor = lax.axis_size("tensor")
    me_table, me_tensor = lax.axis_index("table"), lax.axis_index("tensor")
    part = width // tensor
    capacity = 2 * requests // owners
    slots = capacity // tensor
    n_slots = owners * slots
    per = requests // LANES

    ids_flat = lookup_ids.reshape(requests)
    send = pl.pallas_call(
        send_ids_kernel,
        out_shape=jax.ShapeDtypeStruct((owners, per, LANES), I32),
        name="send_ids",
    )(ids_flat.reshape(per, LANES))
    got_ids = lax.all_to_all(send, "table", 0, 0, tiled=True)

    first = (me_tensor * slots).astype(I32)
    slot_map = pl.pallas_call(
        lambda *refs: slot_map_kernel(
            *refs, rows_dev=rows_dev, owners=owners, seqs=seqs, lookups=lookups, slots=slots
        ),
        out_shape=jax.ShapeDtypeStruct((n_slots, seqs), BF16),
        in_specs=[pl.BlockSpec(memory_space=pltpu.SMEM), pl.BlockSpec(memory_space=pltpu.VMEM)],
        name="slot_map",
    )(first.reshape(1), ids_flat.reshape(1, requests))

    hidden_f32 = hidden.astype(F32)
    normed = hidden_f32 * lax.rsqrt(jnp.mean(hidden_f32 * hidden_f32, axis=1, keepdims=True) + EPS)
    normed_slice = lax.dynamic_slice_in_dim(normed, me_tensor * part, part, 1)
    n_high, n_low = two_parts(normed_slice)
    u = mm_nt(n_high, key_proj) + mm_nt(n_low, key_proj)
    u = butterfly(u, "tensor")

    block = 512
    squares = pl.pallas_call(
        squares_kernel,
        grid=(rows_dev // block,),
        in_specs=[pl.BlockSpec((block, emb), lambda i: (i, 0)), whole(key_proj.shape)],
        out_specs=pl.BlockSpec((1, block // LANES, LANES), lambda i: (i, 0, 0)),
        out_shape=jax.ShapeDtypeStruct((rows_dev // block, block // LANES, LANES), F32),
        name="squares",
    )(table, key_proj)
    squares = butterfly(squares.reshape(rows_dev // LANES, LANES), "tensor")

    rows, row_ids = pl.pallas_call(
        lambda *refs: gather_kernel(*refs, rows_dev=rows_dev, askers=owners, slots=slots),
        grid=(rows_dev // block,),
        in_specs=[
            pl.BlockSpec(memory_space=pltpu.SMEM),
            whole((owners * per, LANES)),
            pl.BlockSpec((block, emb), lambda i: (i, 0)),
        ],
        out_specs=[whole((n_slots, emb)), whole((n_slots, LANES))],
        out_shape=[
            jax.ShapeDtypeStruct((n_slots, emb), BF16),
            jax.ShapeDtypeStruct((n_slots, LANES), I32),
        ],
        scratch_shapes=[pltpu.VMEM((n_slots, LANES), I32), pltpu.VMEM((n_slots, emb), F32)],
        name="gather_rows",
    )(jnp.stack([me_table.astype(I32), first]), got_ids.reshape(owners * per, LANES), table)
    got_rows = lax.all_to_all(rows.reshape(owners, slots, emb), "table", 0, 0, tiled=True)

    picked = pl.pallas_call(
        lambda *refs: pick_squares_kernel(*refs, slots=slots),
        out_shape=jax.ShapeDtypeStruct((owners, LANES), F32),
        name="pick_squares",
    )(row_ids, squares)
    got_squares = lax.all_to_all(picked.reshape(owners, 1, LANES), "table", 0, 0, tiled=True)

    attention = attention_part(
        hidden_f32, normed, attn_gain, q_weight, kv_weight, out_weight, key_cache, value_cache, cache_lengths
    )

    mixes = pl.pallas_call(
        lambda *refs: mix_kernel(*refs, slots=slots, width=width),
        out_shape=jax.ShapeDtypeStruct((tensor, seqs, part + emb), BF16),
        name="mix",
    )(got_rows.reshape(n_slots, emb), slot_map, u, got_squares.reshape(owners, LANES), attention)
    got_mixes = lax.all_to_all(mixes, "tensor", 0, 0, tiled=True)

    hidden_slice = lax.dynamic_slice_in_dim(hidden, me_tensor * part, part, 1)
    return pl.pallas_call(
        final_kernel,
        out_shape=jax.ShapeDtypeStruct((seqs, part), BF16),
        name="final",
    )(got_mixes, value_proj, hidden_slice)


def solution(mesh):
    return jax.shard_map(
        local,
        mesh=mesh,
        in_specs=(
            P("table", None),
            P(),
            P(None, "tensor"),
            P(None, None, "tensor"),
            P("tensor", None),
            P("table", None, "tensor"),
            P("table", None, "tensor"),
            P("table"),
            P("table", None),
            P(None, "tensor"),
            P(None, "tensor"),
            P("table", None),
        ),
        out_specs=P("table", "tensor"),
        check_vma=False,
    )
```

time: 112 us -> 117 us (1.045)
  Pallas kernels: 0 us -> 33.7 us
  local copies, waits for them, and re-layouts: 24.2 us -> 4.24 us
  waiting for transfers between devices: 35.3 us -> 18.4 us
  starting transfers between devices: 25.1 us -> 33.6 us
  other arithmetic: 11.2 us -> 9.63 us
    pallas_call x0 -> x7, Pallas kernels: none -> 33.7 us  [the longest x1 12.7 us: local(): pl.pallas_call(squares_kernel, grid=(rows_dev // block,), in_specs=[pl.Bl...]
    all_to_all x4, waiting for transfers between devices: 35.3 us -> 14.2 us  [the longest x1 8 us: local(): got_mixes = lax.all_to_all(mixes, 'tensor', 0, 0, tiled=True)]
    gather x2 -> x0, local copies, waits for them, and re-layouts: 17.9 us -> none  [the longest x1 11.9 us: local(): jnp.take(table, jnp.maximum(lax.all_to_all(outgoing, 'table', split_axis=...]
    ppermute x0 -> x4, starting transfers between devices: none -> 9.51 us  [butterfly(): x = x + lax.ppermute(x, axis, [(i, i ^ step) for i in range(peers)])]
    ppermute x0 -> x4, waiting for transfers between devices: none -> 4.2 us  [butterfly(): x = x + lax.ppermute(x, axis, [(i, i ^ step) for i in range(peers)])]
    select_n x2 -> x0, other arithmetic: 3.6 us -> none  [the longest x1 3.58 us: local(): jnp.take(table, jnp.maximum(lax.all_to_all(outgoing, 'table', split_axis=...]
    add x0 -> x4, other arithmetic: none -> 3.02 us  [butterfly(): x = x + lax.ppermute(x, axis, [(i, i ^ step) for i in range(peers)])]
    scatter x1 -> x0, local copies, waits for them, and re-layouts: 2.45 us -> none  [local(): jnp.full((table_count * capacity,), -1, jnp.int32).at[slot_of]]
  transfers between devices with their start and end apart: 4 -> 8, of which waited for: 3 -> 4; matrix products, arithmetic and copies ran while one was open for 20% -> 24% of each run, Pallas kernels for 0% -> 23%
where the time goes in v1:
time: 117 us; the launch traced here: 116 us
  Pallas kernels  33.7 us (29%)
  starting transfers between devices  33.6 us (29%)
  waiting for transfers between devices  18.4 us (16%)
  matrix products  16.1 us (14%)
  other arithmetic  9.63 us (8%)
  local copies, waits for them, and re-layouts  4.24 us (4%)
    pallas_call x1, Pallas kernels, local(): pl.pallas_call(squares_kernel, grid=(rows_dev // block,), in_specs=[pl.Bl...  12.7 us
    pallas_call x1, Pallas kernels, local(): pl.pallas_call(lambda *refs: gather_kernel(*refs, rows_dev=rows_dev, aske...  10.2 us
    ppermute x4, starting transfers between devices, butterfly(): x = x + lax.ppermute(x, axis, [(i, i ^ step) for i in range(peers)])  9.51 us
    all_to_all x1, waiting for transfers between devices, local(): got_mixes = lax.all_to_all(mixes, 'tensor', 0, 0, tiled=True)  8 us
    all_to_all x1, starting transfers between devices, local(): got_ids = lax.all_to_all(send, 'table', 0, 0, tiled=True)  7.43 us
    all_to_all x1, starting transfers between devices, local(): lax.all_to_all(picked.reshape(owners, 1, LANES), 'table', 0, 0, tiled=True)  7.38 us
    all_to_all x1, waiting for transfers between devices, local(): lax.all_to_all(picked.reshape(owners, 1, LANES), 'table', 0, 0, tiled=True)  6.23 us
    all_to_all x1, starting transfers between devices, local(): got_mixes = lax.all_to_all(mixes, 'tensor', 0, 0, tiled=True)  4.68 us
  transfers between devices with their start and end apart: 8, of which 4 were waited for; matrix products, arithmetic and copies ran while one was open for 24% of the time, Pallas kernels for 23%

profile of v1, /device:TPU:0, one launch (start us, length us, event | category | flops | bytes accessed | tf_op | source)
XLA Modules:
  0.0 115.9 jit_solution(17444264937253148185)
XLA Ops:
  0.0 0.0 copy-start
  0.0 0.9 copy.17
  0.9 0.0 copy-start.4
  0.9 0.7 reshape_reshape.6.ids_ref
  1.6 1.3 %send_ids.1 = s32[32,4,128]{2,1,0:T(4,128)} custom-call(s32[4,128]{1,0:T(4,128)} %reshape_reshape.6.ids_ref), custom_call_target="tpu_custom_call" | custom-call | tf_op jit(solution)/shard_map/send_ids/pallas_call | solution.py:253
  2.9 7.4 %all-to-all-start = ((s32[32,4,128]{2,1,0:T(4,128)}), s32[32,4,128]{2,1,0:T(4,128)S(1)}, u32[]{:S(2)}, u32[]{:S(2)}) async-start(s32[32,4,128]{2,1,0:T(4,128)} %send_ids.1), calls=%async_computation | async-start | bytes 131072 | tf_op jit(solution)/shard_map/all_to_all | solution.py:258
  10.3 1.1 fusion.8
  11.4 1.7 %convert_multiply_fusion = f32[32,2560]{1,0:T(8,128)} fusion(bf16[32,2560]{1,0:T(8,128)(2,1)} %param.12, f32[32]{0:T(128)S(1)} %add_rsqrt_fusion), kind=kLoop, calls=%fused_computation.11 | loop fusion | flops 163840 | bytes 491648 | tf_op jit(solution)/shard_map/mul | solution.py:271
  13.1 0.0 copy-done.4
  13.2 0.0 copy-start.1
  13.2 2.1 %fusion.16 = f32[32,1280]{1,0:T(8,128)S(1)} fusion(bf16[1280,640]{1,0:T(8,128)(2,1)} %key_ref.1, f32[32,2560]{1,0:T(8,128)} %convert_multiply_fusion, s32[]{:T(128)S(6)} %select_n.9), kind=kOutput, calls=%fused_computation.29 | convolution fusion | flops 52428800 | bytes 1843204 | tf_op jit(solution)/shard_map/dot_general | solution.py:31
  15.3 0.0 copy-done.1
  15.3 2.2 %convolution_add_fusion = f32[32,1280]{1,0:T(8,128)} fusion(f32[32,1280]{1,0:T(8,128)S(1)} %fusion.16, bf16[1280,640]{1,0:T(8,128)(2,1)S(1)} %copy-done.1, f32[32,2560]{1,0:T(8,128)} %convert_multiply_fusion, s32[]{:T(128)S(6)} %select_n.9), kind=kOutput, calls=%fused_computation.1 | convolution fusion | flops 52551680 | bytes 2048004 | tf_op jit(solution)/shard_map/dot_general | solution.py:31
  17.5 1.9 %collective-permute-start = (f32[32,1280]{1,0:T(8,128)}, f32[32,1280]{1,0:T(8,128)}, u32[]{:S(2)}, u32[]{:S(2)}) collective-permute-start(f32[32,1280]{1,0:T(8,128)} %convolution_add_fusion), channel_id=1, source_target_pairs={{0,1},{1,0},{2,3},{3,2},{4,5},{5,4},{6,7},{7,6},{8,9},{9,8},{10,11... | collective-permute-start | bytes 491528 | tf_op jit(solution)/shard_map/ppermute | solution.py:182
  19.4 12.7 %squares.1 = f32[8,4,128]{2,1,0:T(4,128)} custom-call(bf16[4096,1280]{1,0:T(8,128)(2,1)} %table_ref.1, bf16[1280,640]{1,0:T(8,128)(2,1)} %key_ref.1), custom_call_target="tpu_custom_call" | custom-call | tf_op jit(solution)/shard_map/squares/pallas_call | solution.py:278
  32.1 0.0 copy-start.9
  32.1 0.1 collective-permute-start.2
  32.2 0.0 copy-done.2
  32.2 2.6 %convolution_convert_fusion.1 = bf16[32,640]{1,0:T(8,128)(2,1)S(1)} fusion(bf16[2560,640]{1,0:T(8,128)(2,1)} %param.14, f32[2560]{0:T(1024)} %param.13, bf16[32,2560]{1,0:T(8,128)(2,1)S(1)} %copy-done.2, f32[32]{0:T(128)S(1)} %add_rsqrt_fusion), kind=kOutput, calls=%fused_computation.9 | convolution fusion | flops 105205760 | bytes 3491968 | tf_op jit(solution)/shard_map/dot_general | solution.py:195
  34.9 0.7 reshape.120
  35.6 0.0 copy-done.9
  35.6 0.1 iota_compare_fusion
  35.7 0.0 copy-start.6
  35.7 1.7 %fusion.5 = bf16[32,256]{1,0:T(8,128)(2,1)S(1)} fusion(bf16[320,8,2,128]{3,2,1,0:T(2,128)(2,1)} %bitcast.41, f32[2560]{0:T(1024)} %param.13, bf16[32,2560]{1,0:T(8,128)(2,1)S(1)} %copy-done.2, f32[32]{0:T(128)S(1)} %add_rsqrt_fusion), kind=kOutput, calls=%fused_computation.10 | convolution fusion | flops 42278912 | bytes 1501312 | tf_op jit(solution)/shard_map/dot_general | solution.py:196
  37.4 0.6 slice_convert_fusion
  38.0 1.0 fusion.14
  39.0 0.0 copy-start.8
  39.0 3.0 %fusion.21 = (f32[32,5]{1,0:T(8,128)S(1)}, f32[32,5,256]{2,1,0:T(8,128)}) fusion(bf16[32,5,128]{2,1,0:T(8,128)(2,1)} %reshape.120, bf16[32,256,128]{2,1,0:T(8,128)(2,1)} %param.17, pred[32,256]{1,0:T(8,128)(4,1)S(1)} %iota_compare_fusion), kind=kOutput, calls=%fused_computation.40 | convolution fusion | flops 10608480 | bytes 2310784 | tf_op jit(solution)/shard_map/skgh,sckh->skgc/dot_general | solution.py:205
  42.0 0.0 copy-done.8
  42.0 0.0 collective-permute-done.2
  42.0 0.0 copy-done.6
  42.0 0.7 add.44
  42.8 3.9 %collective-permute-start.3 = (f32[32,128]{1,0:T(8,128)S(1)}, f32[32,128]{1,0:T(8,128)S(1)}, u32[]{:S(2)}, u32[]{:S(2)}) collective-permute-start(f32[32,128]{1,0:T(8,128)S(1)} %add.44), channel_id=1, source_target_pairs={{0,2},{1,3},{2,0},{3,1},{4,6},{5,7},{6,4},{7,5},{8,10},{9,11},{10,... | collective-permute-start | bytes 49160 | tf_op jit(solution)/shard_map/ppermute | solution.py:182
  46.6 0.7 pad_add_fusion.refs_0_
  47.3 1.1 collective-permute-done.3
  48.3 0.6 add.45.refs_1_
  48.9 0.0 all-to-all-done
  49.0 0.0 copy-start.3
  49.0 0.6 copy-done.3
  49.6 10.2 %gather_rows.1 = (bf16[256,1280]{1,0:T(8,128)(2,1)}, s32[256,128]{1,0:T(8,128)}) custom-call(s32[2]{0:T(128)} %pad_add_fusion.refs_0_, s32[128,128]{1,0:T(8,128)} %bitcast.33, bf16[4096,1280]{1,0:T(8,128)(2,1)} %table_ref.1), custom_call_target="tpu_custom_call" | custom-call | tf_op jit(solution)/shard_map/gather_rows/pallas_call | solution.py:288
  59.7 1.9 %pick_squares.1 = f32[32,128]{1,0:T(8,128)} custom-call(s32[256,128]{1,0:T(8,128)} %get-tuple-element.8.refs_0_, f32[32,128]{1,0:T(8,128)} %add.45.refs_1_), custom_call_target="tpu_custom_call" | custom-call | tf_op jit(solution)/shard_map/pick_squares/pallas_call | solution.py:306
  61.6 7.4 %all-to-all-start.2 = ((f32[32,1,128]{2,1,0:T(1,128)}), f32[32,1,128]{2,1,0:T(1,128)S(1)}, u32[]{:S(2)}, u32[]{:S(2)}) async-start(f32[32,1,128]{2,1,0:T(1,128)} %bitcast.39), calls=%async_computation.2 | async-start | bytes 32768 | tf_op jit(solution)/shard_map/all_to_all | solution.py:311
  69.0 1.1 fusion.9
  70.2 6.2 %all-to-all-done.2 = f32[32,1,128]{2,1,0:T(1,128)S(1)} async-done(((f32[32,1,128]{2,1,0:T(1,128)}), f32[32,1,128]{2,1,0:T(1,128)S(1)}, u32[]{:S(2)}, u32[]{:S(2)}) %all-to-all-start.2) | async-done | bytes 16416 | tf_op jit(solution)/shard_map/all_to_all | solution.py:311
  76.4 4.6 %all-to-all-start.1 = ((bf16[32,8,1280]{2,1,0:T(8,128)(2,1)}), bf16[32,8,1280]{2,1,0:T(8,128)(2,1)}, u32[]{:S(2)}, u32[]{:S(2)}) async-start(bf16[32,8,1280]{2,1,0:T(8,128)(2,1)} %bitcast.32), calls=%async_computation.1 | async-start | bytes 1310720 | tf_op jit(solution)/shard_map/all_to_all | solution.py:304
  81.0 1.3 %fusion.17 = (f32[32,5]{1,0:T(8,128)}, f32[32,5]{1,0:T(8,128)}) fusion(f32[32,5]{1,0:T(8,128)} %bitcast.38, f32[32,5]{1,0:T(8,128)S(1)} %fusion.9, f32[32,5]{1,0:T(8,128)S(1)} %get-tuple-element.13), kind=kLoop, calls=%fused_computation.31 | loop fusion | flops 1120 | bytes 3200 | tf_op jit(solution)/shard_map/convert_element_type | solution.py:220
  82.4 0.0 copy-done.5
  82.4 0.7 reshape_reshape.7.refs_1_
  83.0 1.7 %slot_map.1.refs_1_ = bf16[256,32]{1,0:T(8,128)(2,1)} custom-call(s32[1]{0:T(128)} %bitcast.1.refs_0_, s32[1,512]{1,0:T(1,128)} %reshape_reshape.7.refs_1_), custom_call_target="tpu_custom_call" | custom-call | tf_op jit(solution)/shard_map/slot_map/pallas_call | solution.py:261
  84.8 2.2 %fusion.4 = bf16[32,5,128]{2,1,0:T(8,128)(2,1)S(1)} fusion(bf16[32,256,128]{2,1,0:T(8,128)(2,1)} %param.18, f32[32,5,256]{2,1,0:T(8,128)} %get-tuple-element.14, f32[32,5]{1,0:T(8,128)} %get-tuple-element.10, f32[32,5]{1,0:T(8,128)S(1)} %multiply_maximum_fusion, f32[32,128]{1,0:T(8,128)} %get-tuple-element.11, f32[32,5]{1,0:T(8,128)} %get-tuple-element.9), kind=kOutput, calls=%fused_computation.8 | convolution fusion | flops 10670080 | bytes 2320256 | tf_op jit(solution)/shard_map/skgc,sckh->skgh/dot_general | solution.py:219
  86.9 0.0 collective-permute-done
  86.9 1.0 add.42
  87.9 0.0 copy-done.7
  88.0 3.6 %collective-permute-start.1 = (f32[32,1280]{1,0:T(8,128)S(1)}, f32[32,1280]{1,0:T(8,128)S(1)}, u32[]{:S(2)}, u32[]{:S(2)}) collective-permute-start(f32[32,1280]{1,0:T(8,128)S(1)} %add.42), channel_id=1, source_target_pairs={{0,2},{1,3},{2,0},{3,1},{4,6},{5,7},{6,4},{7,5},{8,10},{9,11},{10,... | collective-permute-start | bytes 491528 | tf_op jit(solution)/shard_map/ppermute | solution.py:182
  91.6 0.0 copy-done
  91.6 1.3 %convolution_convert_fusion.refs_4_ = bf16[32,2560]{1,0:T(8,128)(2,1)} fusion(bf16[640,2560]{1,0:T(8,128)(2,1)S(1)} %copy-done, bf16[4,8,5,128]{3,2,1,0:T(8,128)(2,1)S(1)} %bitcast.40), kind=kOutput, calls=%fused_computation | convolution fusion | flops 104939520 | bytes 3481600 | tf_op jit(solution)/shard_map/dot_general | solution.py:222
  92.9 3.1 %collective-permute-done.1 = f32[32,1280]{1,0:T(8,128)S(1)} collective-permute-done((f32[32,1280]{1,0:T(8,128)S(1)}, f32[32,1280]{1,0:T(8,128)S(1)}, u32[]{:S(2)}, u32[]{:S(2)}) %collective-permute-start.1) | collective-permute-done | bytes 163872 | tf_op jit(solution)/shard_map/ppermute | solution.py:182
  96.0 0.7 add.43.refs_2_
  96.7 0.0 all-to-all-done.1
  96.7 3.2 %mix.1 = bf16[4,32,1920]{2,1,0:T(8,128)(2,1)} custom-call(bf16[256,1280]{1,0:T(8,128)(2,1)} %bitcast.4.refs_0_, bf16[256,32]{1,0:T(8,128)(2,1)} %slot_map.1.refs_1_, f32[32,1280]{1,0:T(8,128)} %add.43.refs_2_, f32[32,128]{1,0:T(8,128)} %bitcast.36, bf16[32,2560]{1,0:T(8,128)(2,1)} %convolution_convert_fusion.refs_4_), custom_call_target="tpu_custom_call" | custom-call | tf_op jit(solution)/shard_map/mix/pallas_call | solution.py:317
  99.9 4.7 %all-to-all-start.3 = ((bf16[4,32,1920]{2,1,0:T(8,128)(2,1)}), bf16[4,32,1920]{2,1,0:T(8,128)(2,1)}, u32[]{:S(2)}, u32[]{:S(2)}) async-start(bf16[4,32,1920]{2,1,0:T(8,128)(2,1)} %mix.1), calls=%async_computation.3 | async-start | bytes 983040 | tf_op jit(solution)/shard_map/all_to_all | solution.py:322
  104.6 0.6 constant_dynamic-slice_fusion.hidden_ref
  105.2 8.0 %all-to-all-done.3.got_ref = bf16[4,32,1920]{2,1,0:T(8,128)(2,1)} async-done(((bf16[4,32,1920]{2,1,0:T(8,128)(2,1)}), bf16[4,32,1920]{2,1,0:T(8,128)(2,1)}, u32[]{:S(2)}, u32[]{:S(2)}) %all-to-all-start.3) | async-done | bytes 491552 | tf_op jit(solution)/shard_map/all_to_all | solution.py:322
  113.2 2.7 %final.1 = bf16[32,640]{1,0:T(8,128)(2,1)} custom-call(bf16[4,32,1920]{2,1,0:T(8,128)(2,1)} %all-to-all-done.3.got_ref, bf16[1280,640]{1,0:T(8,128)(2,1)} %value_ref.1, bf16[32,640]{1,0:T(8,128)(2,1)} %constant_dynamic-slice_fusion.hidden_ref), custom_call_target="tpu_custom_call" | custom-call | tf_op jit(solution)/shard_map/final/pallas_call | solution.py:325
  (5 shorter events, 0.0 us)
Async XLA Ops:
  0.0 91.6 %copy-start = (bf16[640,2560]{1,0:T(8,128)(2,1)S(1)}, bf16[640,2560]{1,0:T(8,128)(2,1)}, u32[]{:S(2)}) copy-start(bf16[640,2560]{1,0:T(8,128)(2,1)} %param.16) | copy-start | bytes 9830404
  0.9 12.2 %copy-start.4 = (s32[32,16]{1,0:T(8,128)}, s32[32,16]{1,0:T(8,128)S(1)}, u32[]{:S(2)}) copy-start(s32[32,16]{1,0:T(8,128)S(1)} %copy.17) | copy-start | bytes 6148
  2.9 46.0 %all-to-all-start = ((s32[32,4,128]{2,1,0:T(4,128)}), s32[32,4,128]{2,1,0:T(4,128)S(1)}, u32[]{:S(2)}, u32[]{:S(2)}) async-start(s32[32,4,128]{2,1,0:T(4,128)} %send_ids.1), calls=%async_computation | async-start | bytes 131072 | tf_op jit(solution)/shard_map/all_to_all | solution.py:258
  13.2 2.2 %copy-start.1 = (bf16[1280,640]{1,0:T(8,128)(2,1)S(1)}, bf16[1280,640]{1,0:T(8,128)(2,1)}, u32[]{:S(2)}) copy-start(bf16[1280,640]{1,0:T(8,128)(2,1)} %key_ref.1) | copy-start | bytes 4915204
  17.5 14.8 %copy-start.2 = (bf16[32,2560]{1,0:T(8,128)(2,1)S(1)}, bf16[32,2560]{1,0:T(8,128)(2,1)}, u32[]{:S(2)}) copy-start(bf16[32,2560]{1,0:T(8,128)(2,1)} %param.12) | copy-start | bytes 491524
  17.5 69.4 %collective-permute-start = (f32[32,1280]{1,0:T(8,128)}, f32[32,1280]{1,0:T(8,128)}, u32[]{:S(2)}, u32[]{:S(2)}) collective-permute-start(f32[32,1280]{1,0:T(8,128)} %convolution_add_fusion), channel_id=1, source_target_pairs={{0,1},{1,0},{2,3},{3,2},{4,5},{5,4},{6,7},{7,6},{8,9},{9,8},{10,11... | collective-permute-start | bytes 491528 | tf_op jit(solution)/shard_map/ppermute | solution.py:182
  32.1 3.5 %copy-start.9 = (s32[32]{0:T(128)S(1)}, s32[32]{0:T(128)}, u32[]{:S(2)}) copy-start(s32[32]{0:T(128)} %param.19) | copy-start | bytes 388
  32.1 9.9 %collective-permute-start.2 = (f32[32,128]{1,0:T(8,128)}, f32[32,128]{1,0:T(8,128)}, u32[]{:S(2)}, u32[]{:S(2)}) collective-permute-start(f32[32,128]{1,0:T(8,128)} %bitcast.34), channel_id=1, source_target_pairs={{0,1},{1,0},{2,3},{3,2},{4,5},{5,4},{6,7},{7,6},{8,9},{9,8},{10,11... | collective-permute-start | bytes 49160 | tf_op jit(solution)/shard_map/ppermute | solution.py:182
  35.7 6.4 %copy-start.6 = (f32[8,4,128]{2,1,0:T(4,128)S(1)}, f32[8,4,128]{2,1,0:T(4,128)}, u32[]{:S(2)}) copy-start(f32[8,4,128]{2,1,0:T(4,128)} %squares.1) | copy-start | bytes 49156
  39.0 3.0 %copy-start.8 = (f32[32,1,5]{2,1,0:T(1,128)}, f32[32,1,5]{2,1,0:T(1,128)S(1)}, u32[]{:S(2)}) copy-start(f32[32,1,5]{2,1,0:T(1,128)S(1)} %fusion.14) | copy-start | bytes 1924
  42.8 5.6 %collective-permute-start.3 = (f32[32,128]{1,0:T(8,128)S(1)}, f32[32,128]{1,0:T(8,128)S(1)}, u32[]{:S(2)}, u32[]{:S(2)}) collective-permute-start(f32[32,128]{1,0:T(8,128)S(1)} %add.44), channel_id=1, source_target_pairs={{0,2},{1,3},{2,0},{3,1},{4,6},{5,7},{6,4},{7,5},{8,10},{9,11},{10,... | collective-permute-start | bytes 49160 | tf_op jit(solution)/shard_map/ppermute | solution.py:182
  49.0 0.6 copy-start.3
  49.6 32.8 %copy-start.5 = (s32[32,16]{1,0:T(8,128)S(1)}, s32[32,16]{1,0:T(8,128)}, u32[]{:S(2)}) copy-start(s32[32,16]{1,0:T(8,128)} %copy-done.4) | copy-start | bytes 6148
  61.6 14.8 %all-to-all-start.2 = ((f32[32,1,128]{2,1,0:T(1,128)}), f32[32,1,128]{2,1,0:T(1,128)S(1)}, u32[]{:S(2)}, u32[]{:S(2)}) async-start(f32[32,1,128]{2,1,0:T(1,128)} %bitcast.39), calls=%async_computation.2 | async-start | bytes 32768 | tf_op jit(solution)/shard_map/all_to_all | solution.py:311
  76.4 11.5 %copy-start.7 = (f32[32,1,128]{2,1,0:T(1,128)}, f32[32,1,128]{2,1,0:T(1,128)S(1)}, u32[]{:S(2)}) copy-start(f32[32,1,128]{2,1,0:T(1,128)S(1)} %all-to-all-done.2) | copy-start | bytes 49156
  76.4 20.3 %all-to-all-start.1 = ((bf16[32,8,1280]{2,1,0:T(8,128)(2,1)}), bf16[32,8,1280]{2,1,0:T(8,128)(2,1)}, u32[]{:S(2)}, u32[]{:S(2)}) async-start(bf16[32,8,1280]{2,1,0:T(8,128)(2,1)} %bitcast.32), calls=%async_computation.1 | async-start | bytes 1310720 | tf_op jit(solution)/shard_map/all_to_all | solution.py:304
  88.0 8.1 %collective-permute-start.1 = (f32[32,1280]{1,0:T(8,128)S(1)}, f32[32,1280]{1,0:T(8,128)S(1)}, u32[]{:S(2)}, u32[]{:S(2)}) collective-permute-start(f32[32,1280]{1,0:T(8,128)S(1)} %add.42), channel_id=1, source_target_pairs={{0,2},{1,3},{2,0},{3,1},{4,6},{5,7},{6,4},{7,5},{8,10},{9,11},{10,... | collective-permute-start | bytes 491528 | tf_op jit(solution)/shard_map/ppermute | solution.py:182
  99.9 13.3 %all-to-all-start.3 = ((bf16[4,32,1920]{2,1,0:T(8,128)(2,1)}), bf16[4,32,1920]{2,1,0:T(8,128)(2,1)}, u32[]{:S(2)}, u32[]{:S(2)}) async-start(bf16[4,32,1920]{2,1,0:T(8,128)(2,1)} %mix.1), calls=%async_computation.3 | async-start | bytes 983040 | tf_op jit(solution)/shard_map/all_to_all | solution.py:322

commit v2 on v1

v2 whole, which is shorter than its diff:
```python
import math

import jax
import jax.numpy as jnp
from jax import lax
from jax.experimental import pallas as pl
from jax.experimental.pallas import tpu as pltpu
from jax.sharding import PartitionSpec as P


HEAD_DIM = 128
EPS = 1e-06
LANES = 128
F32 = jnp.float32
BF16 = jnp.bfloat16
I32 = jnp.int32


def iota(shape, dim):
    return lax.broadcasted_iota(I32, shape, dim)


def ones_where(mask):
    return jnp.where(mask, 1.0, 0.0).astype(BF16)


def mm(a, b):
    return lax.dot_general(a, b, (((1,), (0,)), ((), ())), preferred_element_type=F32)


def mm_nt(a, b):
    return lax.dot_general(a, b, (((1,), (1,)), ((), ())), preferred_element_type=F32)


def mm_tn(a, b):
    return lax.dot_general(a, b, (((0,), (0,)), ((), ())), preferred_element_type=F32)


def two_parts(x):
    high = x.astype(BF16)
    return high, (x - high.astype(F32)).astype(BF16)


def three_parts(x):
    high = x.astype(BF16)
    rest = x - high.astype(F32)
    mid = rest.astype(BF16)
    return high, mid, (rest - mid.astype(F32)).astype(BF16)


def send_ids_kernel(ids_ref, out_ref):
    _, per, _ = out_ref.shape
    _, seqs = ids_ref.shape
    fit = LANES // seqs
    flat = [
        jnp.concatenate([ids_ref[j * fit + q : j * fit + q + 1, :] for q in range(fit)], axis=1)
        for j in range(per)
    ]
    flat = jnp.concatenate(flat, axis=0)
    out_ref[...] = jnp.broadcast_to(flat[None], out_ref.shape)


def slot_map_kernel(first_ref, ids_ref, map_ref, *, rows_dev, owners, seqs, lookups, slots):
    requests = seqs * lookups
    ids = jnp.concatenate([ids_ref[j : j + 1, :] for j in range(lookups)], axis=1)
    owner = ids // rows_dev
    hit = ones_where(iota((owners, requests), 0) == owner)
    before = ones_where(iota((requests, requests), 0) < iota((requests, requests), 1))
    count = mm(hit, before)
    rank = jnp.sum(count * hit.astype(F32), axis=0, keepdims=True).astype(I32)
    rel = rank - first_ref[0]
    slot = jnp.where((rel >= 0) & (rel < slots), owner * slots + rel, -1)
    placed = ones_where(iota((owners * slots, requests), 0) == slot)
    of_seq = ones_where(iota((seqs, requests), 1) % seqs == iota((seqs, requests), 0))
    map_ref[...] = mm_nt(placed, of_seq).astype(BF16)


def squares_kernel(
    z_ref, hidden_ref, gain_ref, table_ref, key_ref, order_ref, out_ref, attn_in_ref, u_ref
):
    del order_ref
    sub = 256

    @pl.when(pl.program_id(0) == 0)
    def _():
        part = key_ref.shape[1]
        hidden = hidden_ref[...].astype(F32)
        inv = lax.rsqrt(jnp.mean(hidden * hidden, axis=1, keepdims=True) + EPS)
        attn_in_ref[...] = (hidden * inv * gain_ref[...]).astype(BF16)
        start = pl.multiple_of(z_ref[0] * part, LANES)
        high, low = two_parts(hidden_ref[:, pl.ds(start, part)].astype(F32) * inv)
        u_ref[...] = (mm_nt(high, key_ref[...]) + mm_nt(low, key_ref[...])).astype(BF16)

    for t in range(table_ref.shape[0] // sub):
        keys = mm(table_ref[t * sub : (t + 1) * sub, :], key_ref[...])
        folded = keys[:, :LANES] * keys[:, :LANES]
        for c in range(LANES, keys.shape[1], LANES):
            part = keys[:, c : c + LANES]
            folded = folded + part * part
        for g in range(sub // LANES):
            block = folded[g * LANES : (g + 1) * LANES, :]
            row = t * (sub // LANES) + g
            out_ref[0, row : row + 1, :] = jnp.sum(block.T, axis=0, keepdims=True)


def slot_lanes(row, z, slots):
    askers = row.shape[0]
    lane = iota((askers, LANES), 1)
    own = row if z == 0 else pltpu.roll(row, LANES - z * slots, 1)
    own = jnp.where(lane < slots, own, 0.0)
    step = slots
    while step < LANES:
        own = own + pltpu.roll(own, step, 1)
        step *= 2
    fit = LANES // slots
    own = jnp.where(lane // slots == iota((askers, LANES), 0) % fit, own, 0.0)
    return jnp.sum(own.reshape(askers // fit, fit, LANES), axis=1)


def select_kernel(
    where_ref, got_ref, sq_ref, u_ref, idx_ref, out_ref, *, rows_dev, per, capacity, tensor
):
    groups = sq_ref.shape[0]
    askers = got_ref.shape[0] // per
    seqs = u_ref.shape[0]
    slots = capacity // tensor
    before = ones_where(iota((LANES, LANES), 0) < iota((LANES, LANES), 1))
    lane = iota((askers, LANES), 1)
    seen = jnp.zeros((askers, 1), F32)
    ranks, locals_ = [], []
    for j in range(per):
        local = got_ref[pl.ds(j, askers, stride=per), :] - where_ref[0] * rows_dev
        mine = (local >= 0) & (local < rows_dev)
        rank = mm(ones_where(mine), before) + seen
        seen = seen + jnp.sum(jnp.where(mine, 1.0, 0.0), axis=1, keepdims=True)
        ranks.append(jnp.where(mine, rank, -1.0).astype(I32))
        locals_.append(local.astype(F32))
    row = jnp.zeros((askers, LANES), F32)
    for k in range(capacity):
        one = jnp.where(ranks[0] == k, locals_[0], 0.0)
        for j in range(1, per):
            one = one + jnp.where(ranks[j] == k, locals_[j], 0.0)
        row = jnp.where(lane == k, jnp.sum(one, axis=1, keepdims=True), row)
    idx = jnp.zeros(idx_ref.shape, F32)
    for z in range(tensor):
        idx = jnp.where(where_ref[1] == z, slot_lanes(row, z, slots), idx)
    idx_ref[...] = idx.astype(I32)
    ids = row.astype(I32)
    high, low = ids // LANES, ids % LANES
    value = jnp.zeros((askers, LANES), F32)
    for g in range(groups):
        line = jnp.broadcast_to(sq_ref[g : g + 1, :], (askers, LANES))
        found = jnp.take_along_axis(line, low, axis=1, mode="promise_in_bounds")
        value = jnp.where(high == g, found, value)
    u = u_ref[...]
    for z in range(tensor):
        out_ref[z, :seqs, :] = u
        out_ref[z, seqs:, :] = jnp.zeros((out_ref.shape[1] - seqs, u.shape[1]), BF16)
        lines = slot_lanes(value, z, slots)
        for p, part in enumerate(three_parts(lines)):
            out_ref[z, seqs : seqs + lines.shape[0], p * LANES : (p + 1) * LANES] = part


def pack_kernel(rows_ref, got_ref, out_ref, *, seqs):
    owners, slots, _ = out_ref.shape
    n_slots, emb = rows_ref.shape
    lines = n_slots // LANES
    total = jnp.zeros((lines, LANES), F32)
    for p in range(3):
        for z in range(got_ref.shape[0]):
            total = total + got_ref[z, seqs : seqs + 8, p * LANES : (p + 1) * LANES].astype(F32)[:lines]
    spread = jnp.concatenate(
        [jnp.broadcast_to(total[i : i + 1, :], (LANES, LANES)) for i in range(lines)], axis=0
    )
    lane = iota((n_slots, LANES), 1)
    keep = lane == iota((n_slots, LANES), 0) % LANES
    column = jnp.sum(jnp.where(keep, spread, 0.0), axis=1, keepdims=True)
    extra = jnp.zeros((n_slots, LANES), F32)
    for p, part in enumerate(three_parts(column)):
        extra = jnp.where(lane == p, part.astype(F32), extra)
    out_ref[:, :, :emb] = rows_ref[...].reshape(owners, slots, emb)
    out_ref[:, :, emb:] = extra.astype(BF16).reshape(owners, slots, LANES)


def attention_kernel(
    lens_ref, x_ref, qw_hbm, kvw_hbm, key_hbm, val_hbm, ow_hbm, out_ref,
    qw, kvw, key, val, ow, sems,
):
    seqs, width = x_ref.shape
    ctx_len = key_hbm.shape[1]
    heads = qw_hbm.shape[1] // HEAD_DIM
    pad = 8
    copies = [
        pltpu.make_async_copy(src, dst, sems.at[i])
        for i, (src, dst) in enumerate(
            ((qw_hbm, qw), (kvw_hbm, kvw), (key_hbm, key), (val_hbm, val), (ow_hbm, ow))
        )
    ]
    for copy in copies:
        copy.start()
    x = x_ref[...]
    copies[0].wait()
    query = mm(x, qw[...]).astype(BF16)
    src, dst = iota((HEAD_DIM, 4 * HEAD_DIM), 0), iota((HEAD_DIM, 4 * HEAD_DIM), 1)
    spread = ones_where(dst - jnp.where(dst < 2 * HEAD_DIM, 0, 2 * HEAD_DIM + 1) == 2 * src)
    blocks = width // HEAD_DIM
    stacked = jnp.concatenate(
        [x[:, g * HEAD_DIM : (g + 1) * HEAD_DIM] for g in range(blocks)], axis=0
    )
    wide = mm(stacked, spread).astype(BF16)
    even = jnp.concatenate(
        [wide[g * seqs : (g + 1) * seqs, : 2 * HEAD_DIM] for g in range(blocks)], axis=1
    )
    odd = jnp.concatenate(
        [wide[g * seqs : (g + 1) * seqs, 2 * HEAD_DIM :] for g in range(blocks)], axis=1
    )
    copies[1].wait()
    new_kv = mm(jnp.concatenate([even, odd], axis=0), kvw[...]).astype(BF16)
    rows = seqs * pad
    r, c = iota((rows, seqs), 0), iota((rows, seqs), 1)
    q_rows = jnp.zeros((rows, HEAD_DIM), F32)
    for g in range(heads):
        put = ones_where((r // pad == c) & (r % pad == g))
        q_rows = q_rows + mm(put, query[:, g * HEAD_DIM : (g + 1) * HEAD_DIM])
    rep = ones_where(r // pad == c)
    new_key = mm(rep, new_kv[:seqs, :])
    new_value = mm(rep, new_kv[seqs:, :])
    inv_scale = 1.0 / math.sqrt(HEAD_DIM)
    own = jnp.sum(q_rows * new_key, axis=1, keepdims=True) * inv_scale
    copies[2].wait()
    place = iota((pad, ctx_len), 1)
    energies = []
    for s in range(seqs):
        q_s = q_rows[s * pad : (s + 1) * pad, :].astype(BF16)
        score = mm_nt(q_s, key[s]) * inv_scale
        energies.append(jnp.where(place < lens_ref[s], score, -1e30))
    energies = jnp.concatenate(energies, axis=0)
    top = jnp.maximum(jnp.max(energies, axis=1, keepdims=True), own)
    weights = jnp.exp(energies - top)
    own_weight = jnp.exp(own - top)
    denom = jnp.sum(weights, axis=1, keepdims=True) + own_weight
    probs = weights / denom
    own_prob = (own_weight / denom).astype(BF16).astype(F32)
    copies[3].wait()
    context = []
    for s in range(seqs):
        context.append(mm(probs[s * pad : (s + 1) * pad, :].astype(BF16), val[s]))
    context = (jnp.concatenate(context, axis=0) + own_prob * new_value).astype(BF16)
    r, c = iota((seqs, rows), 0), iota((seqs, rows), 1)
    flat = []
    for g in range(heads):
        take = ones_where((c // pad == r) & (c % pad == g))
        flat.append(mm(take, context).astype(BF16))
    copies[4].wait()
    out_ref[...] = mm(jnp.concatenate(flat, axis=1), ow[...]).astype(BF16)


def mix_kernel(rows_ref, map_ref, got_ref, attn_ref, out_ref, *, width):
    _, seqs = map_ref.shape
    emb = got_ref.shape[2]
    rows = rows_ref[:, :emb]
    of_seq = map_ref[...].astype(F32)
    u = got_ref[0, :seqs, :].astype(F32)
    for z in range(1, got_ref.shape[0]):
        u = u + got_ref[z, :seqs, :].astype(F32)
    u_high, u_low = two_parts(u)
    cross_all = mm_nt(rows, u_high) + mm_nt(rows, u_low)
    cross = jnp.sum(cross_all * of_seq, axis=1, keepdims=True)
    square = jnp.sum(rows_ref[:, emb:].astype(F32), axis=1, keepdims=True)
    gate = jax.nn.sigmoid(cross * lax.rsqrt(square / width + EPS) / math.sqrt(width))
    g_high, g_low = two_parts(of_seq * gate)
    mixed = (mm_tn(g_high, rows) + mm_tn(g_low, rows)).astype(BF16)
    peers, _, _ = out_ref.shape
    part = width // peers
    for p in range(peers):
        out_ref[p, :, :part] = attn_ref[:, p * part : (p + 1) * part]
        out_ref[p, :, part:] = mixed


def final_kernel(got_ref, value_ref, hidden_ref, out_ref):
    part = out_ref.shape[1]
    total = got_ref[0].astype(F32)
    for p in range(1, got_ref.shape[0]):
        total = total + got_ref[p].astype(F32)
    high, low = two_parts(total[:, part:])
    memory = mm(high, value_ref[...]) + mm(low, value_ref[...])
    out_ref[...] = (hidden_ref[...].astype(F32) + total[:, :part] + memory).astype(BF16)


def whole(shape):
    return pl.BlockSpec(shape, lambda *_: (0,) * len(shape))


def body(
    hidden,
    attn_gain,
    q_weight,
    kv_weight,
    out_weight,
    key_cache,
    value_cache,
    cache_lengths,
    table,
    key_proj,
    value_proj,
    lookup_ids,
):
    seqs, width = hidden.shape
    lookups = lookup_ids.shape[1]
    requests = seqs * lookups
    rows_dev, emb = table.shape
    owners = lax.axis_size("table")
    tensor = lax.axis_size("tensor")
    me_table, me_tensor = lax.axis_index("table"), lax.axis_index("tensor")
    part = width // tensor
    capacity = 2 * requests // owners
    slots = capacity // tensor
    n_slots = owners * slots
    per = requests // LANES

    vmem = pl.BlockSpec(memory_space=pltpu.VMEM)
    smem = pl.BlockSpec(memory_space=pltpu.SMEM)
    hbm = pl.BlockSpec(memory_space=pl.ANY)
    ids_t = lookup_ids.T

    send = pl.pallas_call(
        send_ids_kernel,
        out_shape=jax.ShapeDtypeStruct((owners, per, LANES), I32),
        name="send_ids",
    )(ids_t)
    got_ids = lax.all_to_all(send, "table", 0, 0, tiled=True)

    block = 512
    squares, attn_in, u_part = pl.pallas_call(
        squares_kernel,
        grid=(rows_dev // block,),
        in_specs=[
            smem,
            whole(hidden.shape),
            whole((1, width)),
            pl.BlockSpec((block, emb), lambda i: (i, 0)),
            whole(key_proj.shape),
            hbm,
        ],
        out_specs=[
            pl.BlockSpec((1, block // LANES, LANES), lambda i: (i, 0, 0)),
            whole(hidden.shape),
            whole((seqs, emb)),
        ],
        out_shape=[
            jax.ShapeDtypeStruct((rows_dev // block, block // LANES, LANES), F32),
            jax.ShapeDtypeStruct(hidden.shape, BF16),
            jax.ShapeDtypeStruct((seqs, emb), BF16),
        ],
        name="squares",
    )(me_tensor.astype(I32).reshape(1), hidden, attn_gain.reshape(1, width), table, key_proj, send)

    where = jnp.stack([me_table.astype(I32), me_tensor.astype(I32)])
    idx, shares = pl.pallas_call(
        lambda *refs: select_kernel(
            *refs, rows_dev=rows_dev, per=per, capacity=capacity, tensor=tensor
        ),
        in_specs=[smem, vmem, vmem, vmem],
        out_shape=[
            jax.ShapeDtypeStruct((n_slots // LANES, LANES), I32),
            jax.ShapeDtypeStruct((tensor, seqs + 8, emb), BF16),
        ],
        name="select",
    )(where, got_ids.reshape(owners * per, LANES), squares.reshape(rows_dev // LANES, LANES), u_part)
    got_shares = lax.all_to_all(shares, "tensor", 0, 0, tiled=True)
    rows = table.at[idx.reshape(n_slots)].get(mode="promise_in_bounds")

    first = (me_tensor * slots).astype(I32)
    slot_map = pl.pallas_call(
        lambda *refs: slot_map_kernel(
            *refs, rows_dev=rows_dev, owners=owners, seqs=seqs, lookups=lookups, slots=slots
        ),
        out_shape=jax.ShapeDtypeStruct((n_slots, seqs), BF16),
        in_specs=[smem, vmem],
        name="slot_map",
    )(first.reshape(1), ids_t)

    packed = pl.pallas_call(
        lambda *refs: pack_kernel(*refs, seqs=seqs),
        out_shape=jax.ShapeDtypeStruct((owners, slots, emb + LANES), BF16),
        name="pack",
    )(rows, got_shares)
    got_rows = lax.all_to_all(packed, "table", 0, 0, tiled=True)

    _, kv_width = key_cache.shape[1:]
    attention = pl.pallas_call(
        attention_kernel,
        in_specs=[smem, vmem, hbm, hbm, hbm, hbm, hbm],
        out_shape=jax.ShapeDtypeStruct((seqs, width), BF16),
        scratch_shapes=[
            pltpu.VMEM(q_weight.shape, BF16),
            pltpu.VMEM((2 * width, kv_width), BF16),
            pltpu.VMEM(key_cache.shape, BF16),
            pltpu.VMEM(value_cache.shape, BF16),
            pltpu.VMEM(out_weight.shape, BF16),
            pltpu.SemaphoreType.DMA((5,)),
        ],
        name="attention",
    )(
        cache_lengths, attn_in, q_weight, kv_weight.reshape(2 * width, kv_width),
        key_cache, value_cache, out_weight,
    )

    mixes = pl.pallas_call(
        lambda *refs: mix_kernel(*refs, width=width),
        out_shape=jax.ShapeDtypeStruct((tensor, seqs, part + emb), BF16),
        name="mix",
    )(got_rows.reshape(n_slots, emb + LANES), slot_map, got_shares, attention)
    got_mixes = lax.all_to_all(mixes, "tensor", 0, 0, tiled=True)

    hidden_slice = lax.dynamic_slice_in_dim(hidden, me_tensor * part, part, 1)
    return pl.pallas_call(
        final_kernel,
        out_shape=jax.ShapeDtypeStruct((seqs, part), BF16),
        name="final",
    )(got_mixes, value_proj, hidden_slice)


def solution(mesh):
    return jax.shard_map(
        body,
        mesh=mesh,
        in_specs=(
            P("table", None),
            P(),
            P(None, "tensor"),
            P(None, None, "tensor"),
            P("tensor", None),
            P("table", None, "tensor"),
            P("table", None, "tensor"),
            P("table"),
            P("table", None),
            P(None, "tensor"),
            P(None, "tensor"),
            P("table", None),
        ),
        out_specs=P("table", "tensor"),
        check_vma=False,
    )
```

time: 117 us -> 89 us (0.76)
  matrix products: 16.1 us -> 0 us
  local copies, waits for them, and re-layouts: 4.24 us -> 13.7 us
  starting transfers between devices: 33.6 us -> 24.9 us
  other arithmetic: 9.63 us -> 1.27 us
  waiting for transfers between devices: 18.4 us -> 12.9 us
  Pallas kernels: 33.7 us -> 35.4 us
    dot_general x8 -> x0, matrix products: 16.1 us -> none  [the longest x2 4.31 us: mm_nt(): lax.dot_general(a, b, (((1,), (1,)), ((), ())), preferred_element_type=F32)]
    ppermute x4 -> x0, starting transfers between devices: 9.51 us -> none  [butterfly(): x = x + lax.ppermute(x, axis, [(i, i ^ step) for i in range(peers)])]
    gather x0 -> x1, local copies, waits for them, and re-layouts: none -> 7.96 us  [body(): rows = table.at[idx.reshape(n_slots)].get(mode='promise_in_bounds')]
    ppermute x4 -> x0, waiting for transfers between devices: 4.2 us -> none  [butterfly(): x = x + lax.ppermute(x, axis, [(i, i ^ step) for i in range(peers)])]
    add x4 -> x0, other arithmetic: 3.02 us -> none  [butterfly(): x = x + lax.ppermute(x, axis, [(i, i ^ step) for i in range(peers)])]
    reduce_sum x2 -> x0, other arithmetic: 2.19 us -> none  [the longest x1 1.14 us: attention_part(): denom = jnp.sum(weights, axis=-1) + own_weight]
    another operation x3 -> x0, local copies, waits for them, and re-layouts: 2.03 us -> none
    convert_element_type x2 -> x0, other arithmetic: 1.95 us -> none  [the longest x1 1.34 us: attention_part(): own_prob.astype(F32)[..., None] * new_value.astype(F32)[:, :, None, :]]
  transfers between devices with their start and end apart: 8 -> 4, of which waited for: 4 -> 3; matrix products, arithmetic and copies ran while one was open for 24% -> 14% of each run, Pallas kernels for 23% -> 26%
where the time goes in v2:
time: 89 us; the launch traced here: 88.1 us
  Pallas kernels  35.4 us (40%)
  starting transfers between devices  24.9 us (28%)
  local copies, waits for them, and re-layouts  13.7 us (15%)
  waiting for transfers between devices  12.9 us (14%)
  other arithmetic  1.27 us (1%)
    pallas_call x1, Pallas kernels, body(): pl.pallas_call(squares_kernel, grid=(rows_dev // block,), in_specs=[smem,...  14 us
    gather x1, local copies, waits for them, and re-layouts, body(): rows = table.at[idx.reshape(n_slots)].get(mode='promise_in_bounds')  7.96 us
    all_to_all x1, waiting for transfers between devices, body(): got_mixes = lax.all_to_all(mixes, 'tensor', 0, 0, tiled=True)  7.91 us
    all_to_all x1, starting transfers between devices, body(): got_ids = lax.all_to_all(send, 'table', 0, 0, tiled=True)  7.43 us
    all_to_all x1, starting transfers between devices, body(): got_rows = lax.all_to_all(packed, 'table', 0, 0, tiled=True)  7.33 us
    pallas_call x1, Pallas kernels, body(): pl.pallas_call(attention_kernel, in_specs=[smem, vmem, hbm, hbm, hbm, hbm...  7.11 us
    all_to_all x1, starting transfers between devices, body(): got_shares = lax.all_to_all(shares, 'tensor', 0, 0, tiled=True)  5.3 us
    all_to_all x1, waiting for transfers between devices, body(): got_rows = lax.all_to_all(packed, 'table', 0, 0, tiled=True)  4.91 us
  transfers between devices with their start and end apart: 4, of which 3 were waited for; matrix products, arithmetic and copies ran while one was open for 14% of the time, Pallas kernels for 26%

profile of v2, /device:TPU:0, one launch (start us, length us, event | category | flops | bytes accessed | tf_op | source)
XLA Modules:
  0.0 88.1 jit_solution(5500360423666214232)
XLA Ops:
  0.0 1.4 %send_ids.1.order_ref = s32[32,4,128]{2,1,0:T(4,128)} custom-call(s32[16,32]{1,0:T(8,128)} %bitcast.13), custom_call_target="tpu_custom_call" | custom-call | tf_op jit(solution)/shard_map/send_ids/pallas_call | solution.py:326
  1.4 7.4 %all-to-all-start = ((s32[32,4,128]{2,1,0:T(4,128)}), s32[32,4,128]{2,1,0:T(4,128)S(1)}, u32[]{:S(2)}, u32[]{:S(2)}) async-start(s32[32,4,128]{2,1,0:T(4,128)} %send_ids.1.order_ref), calls=%async_computation | async-start | bytes 131072 | tf_op jit(solution)/shard_map/all_to_all | solution.py:331
  8.9 1.3 %reshape.51.gain_ref = f32[1,2560]{1,0:T(1,128)} reshape(f32[2560]{0:T(1024)} %param.13) | data formatting | bytes 20480 | tf_op jit(solution)/shard_map/reshape | solution.py:356
  10.2 14.0 %squares.1 = (f32[8,4,128]{2,1,0:T(4,128)}, bf16[32,2560]{1,0:T(8,128)(2,1)}, bf16[32,1280]{1,0:T(8,128)(2,1)}) custom-call(s32[1]{0:T(128)} %bitcast.1.z_ref, bf16[32,2560]{1,0:T(8,128)(2,1)} %hidden_ref.1, f32[1,2560]{1,0:T(1,128)} %reshape.51.gain_ref, bf16[4096,1280]{1,0:T(8,128)(2,1)} %table_ref.1, bf16[1280,640]{1,0:T(8,128)(2,1)} %key_ref.1, ...), custom_call_target="tpu_custom_call" | custom-call | tf_op jit(solution)/shard_map/squares/pallas_call | solution.py:334
  24.2 0.6 pad_add_fusion.refs_0_
  24.8 0.0 all-to-all-done
  24.8 0.0 copy-start.3
  24.8 0.6 copy-done.3
  25.4 2.9 %select.1 = (s32[2,128]{1,0:T(2,128)}, bf16[4,40,1280]{2,1,0:T(8,128)(2,1)}) custom-call(s32[2]{0:T(128)} %pad_add_fusion.refs_0_, s32[128,128]{1,0:T(8,128)} %bitcast.12, f32[32,128]{1,0:T(8,128)} %bitcast.15, bf16[32,1280]{1,0:T(8,128)(2,1)} %get-tuple-element.11.refs_3_), custom_call_target="tpu_custom_call" | custom-call | tf_op jit(solution)/shard_map/select/pallas_call | solution.py:359
  28.2 5.3 %all-to-all-start.1 = ((bf16[4,40,1280]{2,1,0:T(8,128)(2,1)}), bf16[4,40,1280]{2,1,0:T(8,128)(2,1)S(1)}, u32[]{:S(2)}, u32[]{:S(2)}) async-start(bf16[4,40,1280]{2,1,0:T(8,128)(2,1)} %get-tuple-element.13), calls=%async_computation.1 | async-start | bytes 819200 | tf_op jit(solution)/shard_map/all_to_all | solution.py:370
  33.6 0.7 compare_select_fusion
  34.2 8.0 %gather_fusion = bf16[256,1280]{1,0:T(8,128)(2,1)} fusion(bf16[4096,1280]{1,0:T(8,128)(2,1)} %table_ref.1, s32[1024]{0:T(1024)S(1)} %pad_clamp_fusion), kind=kCustom, calls=%fused_computation | custom fusion | bytes 1311744 | tf_op jit(solution)/shard_map/gather | solution.py:371
  42.2 0.1 all-to-all-done.1.refs_1_.refs_2_
  42.2 0.0 copy-start
  42.2 0.8 copy-done
  43.0 2.2 %pack.1 = bf16[32,8,1408]{2,1,0:T(8,128)(2,1)} custom-call(bf16[256,1280]{1,0:T(8,128)(2,1)} %gather_fusion, bf16[4,40,1280]{2,1,0:T(8,128)(2,1)} %copy-done), custom_call_target="tpu_custom_call" | custom-call | tf_op jit(solution)/shard_map/pack/pallas_call | solution.py:383
  45.2 7.3 %all-to-all-start.2 = ((bf16[32,8,1408]{2,1,0:T(8,128)(2,1)}), bf16[32,8,1408]{2,1,0:T(8,128)(2,1)S(1)}, u32[]{:S(2)}, u32[]{:S(2)}) async-start(bf16[32,8,1408]{2,1,0:T(8,128)(2,1)} %pack.1), calls=%async_computation.2 | async-start | bytes 1441792 | tf_op jit(solution)/shard_map/all_to_all | solution.py:388
  52.5 1.8 %slot_map.1.refs_1_ = bf16[256,32]{1,0:T(8,128)(2,1)} custom-call(s32[1]{0:T(128)} %bitcast.8.refs_0_, s32[16,32]{1,0:T(8,128)} %bitcast.14), custom_call_target="tpu_custom_call" | custom-call | tf_op jit(solution)/shard_map/slot_map/pallas_call | solution.py:374
  54.3 7.1 %attention.1.refs_3_ = bf16[32,2560]{1,0:T(8,128)(2,1)} custom-call(s32[32]{0:T(128)} %lens_ref.1, bf16[32,2560]{1,0:T(8,128)(2,1)} %get-tuple-element.14.x_ref, bf16[2560,640]{1,0:T(8,128)(2,1)} %qw_hbm.1, bf16[5120,128]{1,0:T(8,128)(2,1)} %bitcast.11, bf16[32,256,128]{2,1,0:T(8,128)(2,1)} %key_hbm.1, bf16[32,256,128]{2,1,0:T(8,128)(2,1)} %val_hbm.1, ...), custom_call_target="tpu_custom_call" | custom-call | tf_op jit(solution)/shard_map/attention/pallas_call | solution.py:391
  61.5 4.9 %all-to-all-done.2 = bf16[32,8,1408]{2,1,0:T(8,128)(2,1)S(1)} async-done(((bf16[32,8,1408]{2,1,0:T(8,128)(2,1)}), bf16[32,8,1408]{2,1,0:T(8,128)(2,1)S(1)}, u32[]{:S(2)}, u32[]{:S(2)}) %all-to-all-start.2) | async-done | bytes 720928 | tf_op jit(solution)/shard_map/all_to_all | solution.py:388
  66.4 0.0 copy-start.1
  66.4 0.9 copy-done.1
  67.2 3.3 %mix.1 = bf16[4,32,1920]{2,1,0:T(8,128)(2,1)} custom-call(bf16[256,1408]{1,0:T(8,128)(2,1)} %bitcast.10, bf16[256,32]{1,0:T(8,128)(2,1)} %slot_map.1.refs_1_, bf16[4,40,1280]{2,1,0:T(8,128)(2,1)} %copy-done, bf16[32,2560]{1,0:T(8,128)(2,1)} %attention.1.refs_3_), custom_call_target="tpu_custom_call" | custom-call | tf_op jit(solution)/shard_map/mix/pallas_call | solution.py:409
  70.5 4.8 %all-to-all-start.3 = ((bf16[4,32,1920]{2,1,0:T(8,128)(2,1)}), bf16[4,32,1920]{2,1,0:T(8,128)(2,1)S(1)}, u32[]{:S(2)}, u32[]{:S(2)}) async-start(bf16[4,32,1920]{2,1,0:T(8,128)(2,1)} %mix.1), calls=%async_computation.3 | async-start | bytes 983040 | tf_op jit(solution)/shard_map/all_to_all | solution.py:414
  75.3 1.4 %constant_dynamic-slice_fusion.hidden_ref = bf16[32,640]{1,0:T(8,128)(2,1)} fusion(bf16[32,2560]{1,0:T(8,128)(2,1)} %hidden_ref.1, s32[]{:T(128)S(6)} %select_n.14), kind=kLoop, calls=%fused_computation.4 | loop fusion | bytes 81924 | tf_op jit(solution)/shard_map/dynamic_slice | solution.py:416
  76.7 7.9 %all-to-all-done.3.got_ref = bf16[4,32,1920]{2,1,0:T(8,128)(2,1)S(1)} async-done(((bf16[4,32,1920]{2,1,0:T(8,128)(2,1)}), bf16[4,32,1920]{2,1,0:T(8,128)(2,1)S(1)}, u32[]{:S(2)}, u32[]{:S(2)}) %all-to-all-start.3) | async-done | bytes 491552 | tf_op jit(solution)/shard_map/all_to_all | solution.py:414
  84.6 0.0 copy-start.2
  84.6 0.8 copy-done.2
  85.4 2.7 %final.1 = bf16[32,640]{1,0:T(8,128)(2,1)} custom-call(bf16[4,32,1920]{2,1,0:T(8,128)(2,1)} %copy-done.2, bf16[1280,640]{1,0:T(8,128)(2,1)} %value_ref.1, bf16[32,640]{1,0:T(8,128)(2,1)} %constant_dynamic-slice_fusion.hidden_ref), custom_call_target="tpu_custom_call" | custom-call | tf_op jit(solution)/shard_map/final/pallas_call | solution.py:417
  (1 shorter events, 0.0 us)
Async XLA Ops:
  1.4 23.4 %all-to-all-start = ((s32[32,4,128]{2,1,0:T(4,128)}), s32[32,4,128]{2,1,0:T(4,128)S(1)}, u32[]{:S(2)}, u32[]{:S(2)}) async-start(s32[32,4,128]{2,1,0:T(4,128)} %send_ids.1.order_ref), calls=%async_computation | async-start | bytes 131072 | tf_op jit(solution)/shard_map/all_to_all | solution.py:331
  24.8 0.6 copy-start.3
  28.2 14.0 %all-to-all-start.1 = ((bf16[4,40,1280]{2,1,0:T(8,128)(2,1)}), bf16[4,40,1280]{2,1,0:T(8,128)(2,1)S(1)}, u32[]{:S(2)}, u32[]{:S(2)}) async-start(bf16[4,40,1280]{2,1,0:T(8,128)(2,1)} %get-tuple-element.13), calls=%async_computation.1 | async-start | bytes 819200 | tf_op jit(solution)/shard_map/all_to_all | solution.py:370
  42.2 0.8 copy-start
  45.2 21.2 %all-to-all-start.2 = ((bf16[32,8,1408]{2,1,0:T(8,128)(2,1)}), bf16[32,8,1408]{2,1,0:T(8,128)(2,1)S(1)}, u32[]{:S(2)}, u32[]{:S(2)}) async-start(bf16[32,8,1408]{2,1,0:T(8,128)(2,1)} %pack.1), calls=%async_computation.2 | async-start | bytes 1441792 | tf_op jit(solution)/shard_map/all_to_all | solution.py:388
  66.4 0.9 copy-start.1
  70.5 14.1 %all-to-all-start.3 = ((bf16[4,32,1920]{2,1,0:T(8,128)(2,1)}), bf16[4,32,1920]{2,1,0:T(8,128)(2,1)S(1)}, u32[]{:S(2)}, u32[]{:S(2)}) async-start(bf16[4,32,1920]{2,1,0:T(8,128)(2,1)} %mix.1), calls=%async_computation.3 | async-start | bytes 983040 | tf_op jit(solution)/shard_map/all_to_all | solution.py:414
  84.6 0.8 copy-start.2

commit v3 on v2

--- a/solution.py
+++ b/solution.py
@@ -76,31 +76,53 @@
 
 
 def squares_kernel(
-    z_ref, hidden_ref, gain_ref, table_ref, key_ref, order_ref, out_ref, attn_in_ref, u_ref
+    z_ref, gain_ref, hidden_hbm, key_hbm, table_hbm, order_ref, out_ref, attn_in_ref,
+    hidden_ref, key_ref, table, key_t, squares, sems, *, chunks,
 ):
     del order_ref
     sub = 256
-
-    @pl.when(pl.program_id(0) == 0)
-    def _():
-        part = key_ref.shape[1]
-        hidden = hidden_ref[...].astype(F32)
-        inv = lax.rsqrt(jnp.mean(hidden * hidden, axis=1, keepdims=True) + EPS)
-        attn_in_ref[...] = (hidden * inv * gain_ref[...]).astype(BF16)
-        start = pl.multiple_of(z_ref[0] * part, LANES)
-        high, low = two_parts(hidden_ref[:, pl.ds(start, part)].astype(F32) * inv)
-        u_ref[...] = (mm_nt(high, key_ref[...]) + mm_nt(low, key_ref[...])).astype(BF16)
-
-    for t in range(table_ref.shape[0] // sub):
-        keys = mm(table_ref[t * sub : (t + 1) * sub, :], key_ref[...])
-        folded = keys[:, :LANES] * keys[:, :LANES]
-        for c in range(LANES, keys.shape[1], LANES):
-            part = keys[:, c : c + LANES]
-            folded = folded + part * part
-        for g in range(sub // LANES):
-            block = folded[g * LANES : (g + 1) * LANES, :]
-            row = t * (sub // LANES) + g
-            out_ref[0, row : row + 1, :] = jnp.sum(block.T, axis=0, keepdims=True)
+    early = [
+        pltpu.make_async_copy(hidden_hbm, hidden_ref, sems.at[len(chunks)]),
+        pltpu.make_async_copy(key_hbm, key_ref, sems.at[len(chunks) + 1]),
+    ]
+    for copy in early:
+        copy.start()
+    copies, start = [], 0
+    for i, size in enumerate(chunks):
+        rows = pl.ds(start, size)
+        copies.append(pltpu.make_async_copy(table_hbm.at[rows, :], table.at[rows, :], sems.at[i]))
+        copies[-1].start()
+        start += size
+    part = key_ref.shape[1]
+    seqs = hidden_ref.shape[0]
+    early[0].wait()
+    hidden = hidden_ref[...].astype(F32)
+    inv = lax.rsqrt(jnp.mean(hidden * hidden, axis=1, keepdims=True) + EPS)
+    attn_in_ref[...] = (hidden * inv * gain_ref[...].reshape(1, hidden.shape[1])).astype(BF16)
+    first = pl.multiple_of(z_ref[0] * part, LANES)
+    high, low = two_parts(hidden_ref[:, pl.ds(first, part)].astype(F32) * inv)
+    early[1].wait()
+    key_t[...] = key_ref[...].T
+    u = mm(jnp.concatenate([high, low], axis=0), key_t[...])
+    u = (u[:seqs] + u[seqs:]).astype(BF16)
+    start = 0
+    for copy, size in zip(copies, chunks):
+        copy.wait()
+        for t in range(start, start + size, sub):
+            keys = mm_nt(key_t[...], table[t : t + sub, :])
+            line = jnp.sum(keys * keys, axis=0, keepdims=True)
+            for g in range(sub // LANES):
+                squares[t // LANES + g : t // LANES + g + 1, :] = line[:, g * LANES : (g + 1) * LANES]
+        start += size
+    peers, lines, emb = out_ref.shape
+    tail = lines - seqs
+    parts = three_parts(squares[...])
+    pieces = [p[h : h + tail] for p in parts for h in range(0, squares.shape[0], tail)]
+    rest = emb - LANES * len(pieces)
+    block = jnp.concatenate(pieces + [jnp.zeros((tail, rest), BF16)], axis=1)
+    for p in range(peers):
+        out_ref[p, :seqs, :] = u
+        out_ref[p, seqs:, :] = block
 
 
 def slot_lanes(row, z, slots):
@@ -117,63 +139,84 @@
     return jnp.sum(own.reshape(askers // fit, fit, LANES), axis=1)
 
 
-def select_kernel(
-    where_ref, got_ref, sq_ref, u_ref, idx_ref, out_ref, *, rows_dev, per, capacity, tensor
+def gather_kernel(
+    me_ref, z_ref, got_ref, table_hbm, rows_ref, ids_ref, idx_vmem, idx_smem, groups, sems,
+    *, rows_dev, per, capacity, tensor,
 ):
-    groups = sq_ref.shape[0]
     askers = got_ref.shape[0] // per
-    seqs = u_ref.shape[0]
     slots = capacity // tensor
     before = ones_where(iota((LANES, LANES), 0) < iota((LANES, LANES), 1))
     lane = iota((askers, LANES), 1)
     seen = jnp.zeros((askers, 1), F32)
+    low_rank = z_ref[0] * slots
     ranks, locals_ = [], []
     for j in range(per):
-        local = got_ref[pl.ds(j, askers, stride=per), :] - where_ref[0] * rows_dev
+        local = got_ref[pl.ds(j, askers, stride=per), :] - me_ref[0] * rows_dev
         mine = (local >= 0) & (local < rows_dev)
         rank = mm(ones_where(mine), before) + seen
         seen = seen + jnp.sum(jnp.where(mine, 1.0, 0.0), axis=1, keepdims=True)
-        ranks.append(jnp.where(mine, rank, -1.0).astype(I32))
+        ranks.append(jnp.where(mine, rank.astype(I32) - low_rank, -1))
         locals_.append(local.astype(F32))
     row = jnp.zeros((askers, LANES), F32)
-    for k in range(capacity):
+    for k in range(slots):
         one = jnp.where(ranks[0] == k, locals_[0], 0.0)
         for j in range(1, per):
             one = one + jnp.where(ranks[j] == k, locals_[j], 0.0)
         row = jnp.where(lane == k, jnp.sum(one, axis=1, keepdims=True), row)
-    idx = jnp.zeros(idx_ref.shape, F32)
-    for z in range(tensor):
-        idx = jnp.where(where_ref[1] == z, slot_lanes(row, z, slots), idx)
-    idx_ref[...] = idx.astype(I32)
-    ids = row.astype(I32)
+    ids_ref[...] = row.astype(I32)
+    idx_vmem[...] = slot_lanes(row, 0, slots).astype(I32)
+    to_smem = pltpu.make_async_copy(idx_vmem, idx_smem, sems.at[0])
+    to_smem.start()
+    n_slots = askers * slots
+    spread = jnp.broadcast_to(row.astype(I32)[:, None, :], (askers, slots, LANES))
+    spread = spread.reshape(n_slots, LANES)
+    keep = iota((n_slots, LANES), 1) == iota((n_slots, LANES), 0) % slots
+    column = jnp.sum(jnp.where(keep, spread % 8, 0).astype(F32), axis=1, keepdims=True)
+    to_smem.wait()
+    for h in range(n_slots // LANES):
+        def issue(i, carry):
+            base = pl.multiple_of((idx_smem[h, i] // 8) * 8, 8)
+            place = pl.multiple_of((h * LANES + i) * 8, 8)
+            pltpu.make_async_copy(
+                table_hbm.at[pl.ds(base, 8), :], groups.at[pl.ds(place, 8), :], sems.at[1]
+            ).start()
+            return carry
+
+        lax.fori_loop(0, LANES, issue, 0, unroll=8)
+    pltpu.make_async_copy(table_hbm.at[pl.ds(0, n_slots * 8), :], groups, sems.at[1]).wait()
+    size = 32
+    for b in range(n_slots // size):
+        offset = iota((size, size * 8), 1) - 8 * iota((size, size * 8), 0)
+        pick = ones_where(offset.astype(F32) == column[b * size : (b + 1) * size, :])
+        rows_ref[b * size : (b + 1) * size, :] = mm(
+            pick, groups[b * size * 8 : (b + 1) * size * 8, :]
+        ).astype(BF16)
+
+
+def pack_kernel(rows_ref, ids_ref, got_ref, out_ref, *, seqs):
+    owners, slots, _ = out_ref.shape
+    n_slots, emb = rows_ref.shape
+    tail = got_ref.shape[1] - seqs
+    per_part = 32 // tail
+    halves = []
+    for h in range(per_part):
+        total = jnp.zeros((tail, LANES), F32)
+        for p in range(3):
+            c = (p * per_part + h) * LANES
+            for z in range(got_ref.shape[0]):
+                total = total + got_ref[z, seqs:, c : c + LANES].astype(F32)
+        halves.append(total)
+    squares = jnp.concatenate(halves, axis=0)
+    ids = ids_ref[...]
     high, low = ids // LANES, ids % LANES
-    value = jnp.zeros((askers, LANES), F32)
-    for g in range(groups):
-        line = jnp.broadcast_to(sq_ref[g : g + 1, :], (askers, LANES))
+    value = jnp.zeros(ids.shape, F32)
+    for g in range(squares.shape[0]):
+        line = jnp.broadcast_to(squares[g : g + 1, :], ids.shape)
         found = jnp.take_along_axis(line, low, axis=1, mode="promise_in_bounds")
         value = jnp.where(high == g, found, value)
-    u = u_ref[...]
-    for z in range(tensor):
-        out_ref[z, :seqs, :] = u
-        out_ref[z, seqs:, :] = jnp.zeros((out_ref.shape[1] - seqs, u.shape[1]), BF16)
-        lines = slot_lanes(value, z, slots)
-        for p, part in enumerate(three_parts(lines)):
-            out_ref[z, seqs : seqs + lines.shape[0], p * LANES : (p + 1) * LANES] = part
-
-
-def pack_kernel(rows_ref, got_ref, out_ref, *, seqs):
-    owners, slots, _ = out_ref.shape
-    n_slots, emb = rows_ref.shape
-    lines = n_slots // LANES
-    total = jnp.zeros((lines, LANES), F32)
-    for p in range(3):
-        for z in range(got_ref.shape[0]):
-            total = total + got_ref[z, seqs : seqs + 8, p * LANES : (p + 1) * LANES].astype(F32)[:lines]
-    spread = jnp.concatenate(
-        [jnp.broadcast_to(total[i : i + 1, :], (LANES, LANES)) for i in range(lines)], axis=0
-    )
+    spread = jnp.broadcast_to(value[:, None, :], (owners, slots, LANES)).reshape(n_slots, LANES)
     lane = iota((n_slots, LANES), 1)
-    keep = lane == iota((n_slots, LANES), 0) % LANES
+    keep = lane == iota((n_slots, LANES), 0) % slots
     column = jnp.sum(jnp.where(keep, spread, 0.0), axis=1, keepdims=True)
     extra = jnp.zeros((n_slots, LANES), F32)
     for p, part in enumerate(three_parts(column)):
@@ -183,8 +226,8 @@
 
 
 def attention_kernel(
-    lens_ref, x_ref, qw_hbm, kvw_hbm, key_hbm, val_hbm, ow_hbm, out_ref,
-    qw, kvw, key, val, ow, sems,
+    lens_ref, first_ref, ids_ref, x_ref, qw_hbm, kvw_hbm, key_hbm, val_hbm, ow_hbm,
+    out_ref, map_ref, qw, kvw, key, val, ow, sems, *, mapping,
 ):
     seqs, width = x_ref.shape
     ctx_len = key_hbm.shape[1]
@@ -193,11 +236,18 @@
     copies = [
         pltpu.make_async_copy(src, dst, sems.at[i])
         for i, (src, dst) in enumerate(
-            ((qw_hbm, qw), (kvw_hbm, kvw), (key_hbm, key), (val_hbm, val), (ow_hbm, ow))
+            (
+                (qw_hbm, qw),
+                (kvw_hbm, kvw),
+                (key_hbm, key),
+                (val_hbm, val),
+                (ow_hbm, ow),
+            )
         )
     ]
     for copy in copies:
         copy.start()
+    slot_map_kernel(first_ref, ids_ref, map_ref, **mapping)
     x = x_ref[...]
     copies[0].wait()
     query = mm(x, qw[...]).astype(BF16)
@@ -277,18 +327,27 @@
         out_ref[p, :, part:] = mixed
 
 
-def final_kernel(got_ref, value_ref, hidden_ref, out_ref):
+def fetch_kernel(value_hbm, hidden_hbm, order_ref, value_ref, hidden_ref, sems):
+    del order_ref
+    copies = [
+        pltpu.make_async_copy(value_hbm, value_ref, sems.at[0]),
+        pltpu.make_async_copy(hidden_hbm, hidden_ref, sems.at[1]),
+    ]
+    for copy in copies:
+        copy.start()
+    for copy in copies:
+        copy.wait()
+
+
+def final_kernel(z_ref, got_ref, value_ref, hidden_ref, out_ref):
     part = out_ref.shape[1]
+    first = pl.multiple_of(z_ref[0] * part, LANES)
     total = got_ref[0].astype(F32)
     for p in range(1, got_ref.shape[0]):
         total = total + got_ref[p].astype(F32)
     high, low = two_parts(total[:, part:])
     memory = mm(high, value_ref[...]) + mm(low, value_ref[...])
-    out_ref[...] = (hidden_ref[...].astype(F32) + total[:, :part] + memory).astype(BF16)
-
-
-def whole(shape):
-    return pl.BlockSpec(shape, lambda *_: (0,) * len(shape))
+    out_ref[...] = (hidden_ref[:, pl.ds(first, part)].astype(F32) + total[:, :part] + memory).astype(BF16)
 
 
 def body(
@@ -330,68 +389,68 @@
     )(ids_t)
     got_ids = lax.all_to_all(send, "table", 0, 0, tiled=True)
 
-    block = 512
-    squares, attn_in, u_part = pl.pallas_call(
-        squares_kernel,
-        grid=(rows_dev // block,),
-        in_specs=[
-            smem,
-            whole(hidden.shape),
-            whole((1, width)),
-            pl.BlockSpec((block, emb), lambda i: (i, 0)),
-            whole(key_proj.shape),
-            hbm,
+    def near(x):
+        return pltpu.with_memory_space_constraint(x, pltpu.VMEM)
+
+    me = me_table.astype(I32).reshape(1)
+    z = me_tensor.astype(I32).reshape(1)
+    chunks = (256, 256, 512, 1024, 1024, 1024)
+    shares, attn_in = pl.pallas_call(
+        lambda *refs: squares_kernel(*refs, chunks=chunks),
+        in_specs=[smem, vmem, hbm, hbm, hbm, hbm],
+        out_specs=[vmem, vmem],
+        out_shape=[
+            jax.ShapeDtypeStruct((tensor, seqs + 16, emb), BF16),
+            jax.ShapeDtypeStruct(hidden.shape, BF16),
         ],
-        out_specs=[
-            pl.BlockSpec((1, block // LANES, LANES), lambda i: (i, 0, 0)),
-            whole(hidden.shape),
-            whole((seqs, emb)),
-        ],
-        out_shape=[
-            jax.ShapeDtypeStruct((rows_dev // block, block // LANES, LANES), F32),
-            jax.ShapeDtypeStruct(hidden.shape, BF16),
-            jax.ShapeDtypeStruct((seqs, emb), BF16),
+        scratch_shapes=[
+            pltpu.VMEM(hidden.shape, BF16),
+            pltpu.VMEM(key_proj.shape, BF16),
+            pltpu.VMEM(table.shape, BF16),
+            pltpu.VMEM((part, emb), BF16),
+            pltpu.VMEM((rows_dev // LANES, LANES), F32),
+            pltpu.SemaphoreType.DMA((len(chunks) + 2,)),
         ],
         name="squares",
-    )(me_tensor.astype(I32).reshape(1), hidden, attn_gain.reshape(1, width), table, key_proj, send)
-
-    where = jnp.stack([me_table.astype(I32), me_tensor.astype(I32)])
-    idx, shares = pl.pallas_call(
-        lambda *refs: select_kernel(
+    )(z, attn_gain, hidden, key_proj, table, send)
+    got_shares = lax.all_to_all(shares, "tensor", 0, 0, tiled=True)
+
+    rows, row_ids = pl.pallas_call(
+        lambda *refs: gather_kernel(
             *refs, rows_dev=rows_dev, per=per, capacity=capacity, tensor=tensor
         ),
-        in_specs=[smem, vmem, vmem, vmem],
-        out_shape=[
-            jax.ShapeDtypeStruct((n_slots // LANES, LANES), I32),
-            jax.ShapeDtypeStruct((tensor, seqs + 8, emb), BF16),
+        in_specs=[smem, smem, vmem, hbm],
+        out_specs=[vmem, vmem],
+        out_shape=[pltpu.VMEM((n_slots, emb), BF16), pltpu.VMEM((owners, LANES), I32)],
+        scratch_shapes=[
+            pltpu.VMEM((n_slots // LANES, LANES), I32),
+            pltpu.SMEM((n_slots // LANES, LANES), I32),
+            pltpu.VMEM((n_slots * 8, emb), BF16),
+            pltpu.SemaphoreType.DMA((2,)),
         ],
-        name="select",
-    )(where, got_ids.reshape(owners * per, LANES), squares.reshape(rows_dev // LANES, LANES), u_part)
-    got_shares = lax.all_to_all(shares, "tensor", 0, 0, tiled=True)
-    rows = table.at[idx.reshape(n_slots)].get(mode="promise_in_bounds")
-
-    first = (me_tensor * slots).astype(I32)
-    slot_map = pl.pallas_call(
-        lambda *refs: slot_map_kernel(
-            *refs, rows_dev=rows_dev, owners=owners, seqs=seqs, lookups=lookups, slots=slots
-        ),
-        out_shape=jax.ShapeDtypeStruct((n_slots, seqs), BF16),
-        in_specs=[smem, vmem],
-        name="slot_map",
-    )(first.reshape(1), ids_t)
-
+        name="gather",
+    )(me, z, near(got_ids.reshape(owners * per, LANES)), table)
+
+    near_shares = near(got_shares)
     packed = pl.pallas_call(
         lambda *refs: pack_kernel(*refs, seqs=seqs),
+        in_specs=[vmem] * 3,
+        out_specs=vmem,
         out_shape=jax.ShapeDtypeStruct((owners, slots, emb + LANES), BF16),
         name="pack",
-    )(rows, got_shares)
+    )(near(rows), near(row_ids), near_shares)
     got_rows = lax.all_to_all(packed, "table", 0, 0, tiled=True)
 
     _, kv_width = key_cache.shape[1:]
-    attention = pl.pallas_call(
-        attention_kernel,
-        in_specs=[smem, vmem, hbm, hbm, hbm, hbm, hbm],
-        out_shape=jax.ShapeDtypeStruct((seqs, width), BF16),
+    mapping = dict(rows_dev=rows_dev, owners=owners, seqs=seqs, lookups=lookups, slots=slots)
+    attention, slot_map = pl.pallas_call(
+        lambda *refs: attention_kernel(*refs, mapping=mapping),
+        in_specs=[smem, smem, vmem, vmem, hbm, hbm, hbm, hbm, hbm],
+        out_specs=[vmem, vmem],
+        out_shape=[
+            pltpu.VMEM((seqs, width), BF16),
+            pltpu.VMEM((n_slots, seqs), BF16),
+        ],
         scratch_shapes=[
             pltpu.VMEM(q_weight.shape, BF16),
             pltpu.VMEM((2 * width, kv_width), BF16),
@@ -402,23 +461,35 @@
         ],
         name="attention",
     )(
-        cache_lengths, attn_in, q_weight, kv_weight.reshape(2 * width, kv_width),
-        key_cache, value_cache, out_weight,
+        cache_lengths, z * slots, ids_t, attn_in, q_weight,
+        kv_weight.reshape(2 * width, kv_width), key_cache, value_cache, out_weight,
     )
 
     mixes = pl.pallas_call(
         lambda *refs: mix_kernel(*refs, width=width),
+        in_specs=[vmem] * 4,
+        out_specs=vmem,
         out_shape=jax.ShapeDtypeStruct((tensor, seqs, part + emb), BF16),
         name="mix",
-    )(got_rows.reshape(n_slots, emb + LANES), slot_map, got_shares, attention)
+    )(near(got_rows.reshape(n_slots, emb + LANES)), near(slot_map), near_shares, near(attention))
     got_mixes = lax.all_to_all(mixes, "tensor", 0, 0, tiled=True)
 
-    hidden_slice = lax.dynamic_slice_in_dim(hidden, me_tensor * part, part, 1)
+    value_near, hidden_near = pl.pallas_call(
+        fetch_kernel,
+        in_specs=[hbm] * 3,
+        out_specs=[vmem] * 2,
+        out_shape=[pltpu.VMEM(value_proj.shape, BF16), pltpu.VMEM(hidden.shape, BF16)],
+        scratch_shapes=[pltpu.SemaphoreType.DMA((2,))],
+        name="fetch_value",
+    )(value_proj, hidden, mixes)
+
     return pl.pallas_call(
         final_kernel,
+        in_specs=[smem] + [vmem] * 3,
+        out_specs=vmem,
         out_shape=jax.ShapeDtypeStruct((seqs, part), BF16),
         name="final",
-    )(got_mixes, value_proj, hidden_slice)
+    )(z, near(got_mixes), near(value_near), near(hidden_near))
 
 
 def solution(mesh):

time: 89 us -> 79.1 us (0.89)
  local copies, waits for them, and re-layouts: 13.7 us -> 0 us
  waiting for transfers between devices: 12.9 us -> 19.3 us
  Pallas kernels: 35.4 us -> 32 us
  starting transfers between devices: 24.9 us -> 27.2 us
  other arithmetic: 1.27 us -> 0 us
    gather x1 -> x0, local copies, waits for them, and re-layouts: 7.96 us -> none  [body(): rows = table.at[idx.reshape(n_slots)].get(mode='promise_in_bounds')]
    all_to_all x1, waiting for transfers between devices: 0.05 us -> 4.3 us  [body(): got_shares = lax.all_to_all(shares, 'tensor', 0, 0, tiled=True)]
    pallas_call x7, Pallas kernels: 33.9 us -> 30.5 us  [the longest x1 12.6 us: body(): pl.pallas_call(lambda *refs: squares_kernel(*refs, chunks=chunks), in_spe...]
    unnamed x8 -> x0, local copies, waits for them, and re-layouts: 3.02 us -> none
    all_to_all x1, starting transfers between devices: 4.79 us -> 7.22 us  [body(): got_mixes = lax.all_to_all(mixes, 'tensor', 0, 0, tiled=True)]
    all_to_all x1, waiting for transfers between devices: 4.91 us -> 7.18 us  [body(): got_rows = lax.all_to_all(packed, 'table', 0, 0, tiled=True)]
    dynamic_slice x1 -> x0, local copies, waits for them, and re-layouts: 1.38 us -> none  [body(): hidden_slice = lax.dynamic_slice_in_dim(hidden, me_tensor * part, part, 1)]
    reshape x1 -> x0, local copies, waits for them, and re-layouts: 1.32 us -> none  [body(): attn_gain.reshape(1, width)]
  transfers between devices with their start and end apart: 4 -> 4, of which waited for: 3 -> 3; matrix products, arithmetic and copies ran while one was open for 14% -> 0% of each run, Pallas kernels for 26% -> 33%
where the time goes in v3:
time: 79.1 us; the launch traced here: 78.5 us
  Pallas kernels  32 us (40%)
  starting transfers between devices  27.2 us (34%)
  waiting for transfers between devices  19.3 us (24%)
    pallas_call x1, Pallas kernels, body(): pl.pallas_call(lambda *refs: squares_kernel(*refs, chunks=chunks), in_spe...  12.6 us
    all_to_all x1, waiting for transfers between devices, body(): got_mixes = lax.all_to_all(mixes, 'tensor', 0, 0, tiled=True)  7.83 us
    all_to_all x1, starting transfers between devices, body(): got_ids = lax.all_to_all(send, 'table', 0, 0, tiled=True)  7.43 us
    all_to_all x1, starting transfers between devices, body(): got_rows = lax.all_to_all(packed, 'table', 0, 0, tiled=True)  7.23 us
    all_to_all x1, starting transfers between devices, body(): got_mixes = lax.all_to_all(mixes, 'tensor', 0, 0, tiled=True)  7.22 us
    all_to_all x1, waiting for transfers between devices, body(): got_rows = lax.all_to_all(packed, 'table', 0, 0, tiled=True)  7.18 us
    pallas_call x1, Pallas kernels, body(): pl.pallas_call(lambda *refs: attention_kernel(*refs, mapping=mapping), in...  6.63 us
    all_to_all x1, starting transfers between devices, body(): got_shares = lax.all_to_all(shares, 'tensor', 0, 0, tiled=True)  5.32 us
  transfers between devices with their start and end apart: 4, of which 3 were waited for; matrix products, arithmetic and copies ran while one was open for 0% of the time, Pallas kernels for 33%

profile of v3, /device:TPU:0, one launch (start us, length us, event | category | flops | bytes accessed | tf_op | source)
XLA Modules:
  0.0 78.5 jit_solution(4971044188882615548)
XLA Ops:
  0.0 1.4 %send_ids.1.refs_5_ = s32[32,4,128]{2,1,0:T(4,128)} custom-call(s32[16,32]{1,0:T(8,128)} %bitcast.9), custom_call_target="tpu_custom_call" | custom-call | tf_op jit(solution)/shard_map/send_ids/pallas_call | solution.py:385
  1.4 7.4 %all-to-all-start = ((s32[32,4,128]{2,1,0:T(4,128)}), s32[32,4,128]{2,1,0:T(4,128)S(1)}, u32[]{:S(2)}, u32[]{:S(2)}) async-start(s32[32,4,128]{2,1,0:T(4,128)} %send_ids.1.refs_5_), calls=%async_computation | async-start | bytes 131072 | tf_op jit(solution)/shard_map/all_to_all | solution.py:390
  8.9 12.6 %squares.1 = (bf16[4,48,1280]{2,1,0:T(8,128)(2,1)}, bf16[32,2560]{1,0:T(8,128)(2,1)}) custom-call(s32[1]{0:T(128)} %bitcast.refs_1_.refs_0_.z_ref, f32[2560]{0:T(1024)} %refs_1_.1, bf16[32,2560]{1,0:T(8,128)(2,1)} %hidden_hbm.1, bf16[1280,640]{1,0:T(8,128)(2,1)} %refs_3_.3, bf16[4096,1280]{1,0:T(8,128)(2,1)} %refs_4_.2, s32[32,4,128]{2,1,0:T(4,128)} %send_ids.1.refs_5_), custom_call_target="tpu_custom_call" | custom-call | tf_op jit(solution)/shard_map/squares/pallas_call | solution.py:398
  21.5 0.0 all-to-all-done
  21.5 5.3 %all-to-all-start.1 = ((bf16[4,48,1280]{2,1,0:T(8,128)(2,1)}), bf16[4,48,1280]{2,1,0:T(8,128)(2,1)S(1)}, u32[]{:S(2)}, u32[]{:S(2)}) async-start(bf16[4,48,1280]{2,1,0:T(8,128)(2,1)} %get-tuple-element.15), calls=%async_computation.1 | async-start | bytes 983040 | tf_op jit(solution)/shard_map/all_to_all | solution.py:416
  26.8 5.3 %gather.1 = (bf16[256,1280]{1,0:T(8,128)(2,1)S(1)}, s32[32,128]{1,0:T(8,128)S(1)}) custom-call(s32[1]{0:T(128)} %bitcast.1.refs_0_, s32[1]{0:T(128)} %bitcast.refs_1_.refs_0_.z_ref, s32[128,128]{1,0:T(8,128)S(1)} %bitcast.7, bf16[4096,1280]{1,0:T(8,128)(2,1)} %refs_4_.2), custom_call_target="tpu_custom_call" | custom-call | tf_op jit(solution)/shard_map/gather/pallas_call | solution.py:418
  32.1 4.3 %all-to-all-done.1.refs_2_ = bf16[4,48,1280]{2,1,0:T(8,128)(2,1)S(1)} async-done(((bf16[4,48,1280]{2,1,0:T(8,128)(2,1)}), bf16[4,48,1280]{2,1,0:T(8,128)(2,1)S(1)}, u32[]{:S(2)}, u32[]{:S(2)}) %all-to-all-start.1) | async-done | bytes 491552 | tf_op jit(solution)/shard_map/all_to_all | solution.py:416
  36.4 1.4 %pack.1 = bf16[32,8,1408]{2,1,0:T(8,128)(2,1)} custom-call(bf16[256,1280]{1,0:T(8,128)(2,1)S(1)} %get-tuple-element.13.refs_0_, s32[32,128]{1,0:T(8,128)S(1)} %get-tuple-element.14.refs_1_, bf16[4,48,1280]{2,1,0:T(8,128)(2,1)S(1)} %all-to-all-done.1.refs_2_), custom_call_target="tpu_custom_call" | custom-call | tf_op jit(solution)/shard_map/pack/pallas_call | solution.py:435
  37.8 7.2 %all-to-all-start.2 = ((bf16[32,8,1408]{2,1,0:T(8,128)(2,1)}), bf16[32,8,1408]{2,1,0:T(8,128)(2,1)S(1)}, u32[]{:S(2)}, u32[]{:S(2)}) async-start(bf16[32,8,1408]{2,1,0:T(8,128)(2,1)} %pack.1), calls=%async_computation.2 | async-start | bytes 1441792 | tf_op jit(solution)/shard_map/all_to_all | solution.py:442
  45.0 6.6 %attention.1 = (bf16[32,2560]{1,0:T(8,128)(2,1)S(1)}, bf16[256,32]{1,0:T(8,128)(2,1)S(1)}) custom-call(s32[32]{0:T(128)} %refs_0_.1, s32[1]{0:T(128)S(6)} %mul.3.refs_1_, s32[16,32]{1,0:T(8,128)} %bitcast.10, bf16[32,2560]{1,0:T(8,128)(2,1)} %get-tuple-element.16.refs_3_, bf16[2560,640]{1,0:T(8,128)(2,1)} %refs_4_.3, bf16[5120,128]{1,0:T(8,128)(2,1)} %bitcast.8, ...), custom_call_target="tpu_custom_call" | custom-call | tf_op jit(solution)/shard_map/attention/pallas_call | solution.py:446
  51.7 7.2 %all-to-all-done.2 = bf16[32,8,1408]{2,1,0:T(8,128)(2,1)S(1)} async-done(((bf16[32,8,1408]{2,1,0:T(8,128)(2,1)}), bf16[32,8,1408]{2,1,0:T(8,128)(2,1)S(1)}, u32[]{:S(2)}, u32[]{:S(2)}) %all-to-all-start.2) | async-done | bytes 720928 | tf_op jit(solution)/shard_map/all_to_all | solution.py:442
  58.8 2.0 %mix.1.order_ref = bf16[4,32,1920]{2,1,0:T(8,128)(2,1)} custom-call(bf16[256,1408]{1,0:T(8,128)(2,1)S(1)} %bitcast.6, bf16[256,32]{1,0:T(8,128)(2,1)S(1)} %get-tuple-element.17.refs_1_, bf16[4,48,1280]{2,1,0:T(8,128)(2,1)S(1)} %all-to-all-done.1.refs_2_, bf16[32,2560]{1,0:T(8,128)(2,1)S(1)} %get-tuple-element.18.refs_3_), custom_call_target="tpu_custom_call" | custom-call | tf_op jit(solution)/shard_map/mix/pallas_call | solution.py:468
  60.8 7.2 %all-to-all-start.3 = ((bf16[4,32,1920]{2,1,0:T(8,128)(2,1)}), bf16[4,32,1920]{2,1,0:T(8,128)(2,1)S(1)}, u32[]{:S(2)}, u32[]{:S(2)}) async-start(bf16[4,32,1920]{2,1,0:T(8,128)(2,1)} %mix.1.order_ref), calls=%async_computation.3 | async-start | bytes 983040 | tf_op jit(solution)/shard_map/all_to_all | solution.py:475
  68.0 1.4 %fetch_value.1 = (bf16[1280,640]{1,0:T(8,128)(2,1)S(1)}, bf16[32,2560]{1,0:T(8,128)(2,1)S(1)}) custom-call(bf16[1280,640]{1,0:T(8,128)(2,1)} %value_hbm.1, bf16[32,2560]{1,0:T(8,128)(2,1)} %hidden_hbm.1, bf16[4,32,1920]{2,1,0:T(8,128)(2,1)} %mix.1.order_ref), custom_call_target="tpu_custom_call" | custom-call | tf_op jit(solution)/shard_map/fetch_value/pallas_call | solution.py:477
  69.5 7.8 %all-to-all-done.3.got_ref = bf16[4,32,1920]{2,1,0:T(8,128)(2,1)S(1)} async-done(((bf16[4,32,1920]{2,1,0:T(8,128)(2,1)}), bf16[4,32,1920]{2,1,0:T(8,128)(2,1)S(1)}, u32[]{:S(2)}, u32[]{:S(2)}) %all-to-all-start.3) | async-done | bytes 491552 | tf_op jit(solution)/shard_map/all_to_all | solution.py:475
  77.3 1.2 %final.1 = bf16[32,640]{1,0:T(8,128)(2,1)} custom-call(s32[1]{0:T(128)} %bitcast.refs_1_.refs_0_.z_ref, bf16[4,32,1920]{2,1,0:T(8,128)(2,1)S(1)} %all-to-all-done.3.got_ref, bf16[1280,640]{1,0:T(8,128)(2,1)S(1)} %get-tuple-element.19.value_ref, bf16[32,2560]{1,0:T(8,128)(2,1)S(1)} %get-tuple-element.20.hidden_ref), custom_call_target="tpu_custom_call" | custom-call | tf_op jit(solution)/shard_map/final/pallas_call | solution.py:486
Async XLA Ops:
  1.4 20.1 %all-to-all-start = ((s32[32,4,128]{2,1,0:T(4,128)}), s32[32,4,128]{2,1,0:T(4,128)S(1)}, u32[]{:S(2)}, u32[]{:S(2)}) async-start(s32[32,4,128]{2,1,0:T(4,128)} %send_ids.1.refs_5_), calls=%async_computation | async-start | bytes 131072 | tf_op jit(solution)/shard_map/all_to_all | solution.py:390
  21.5 14.9 %all-to-all-start.1 = ((bf16[4,48,1280]{2,1,0:T(8,128)(2,1)}), bf16[4,48,1280]{2,1,0:T(8,128)(2,1)S(1)}, u32[]{:S(2)}, u32[]{:S(2)}) async-start(bf16[4,48,1280]{2,1,0:T(8,128)(2,1)} %get-tuple-element.15), calls=%async_computation.1 | async-start | bytes 983040 | tf_op jit(solution)/shard_map/all_to_all | solution.py:416
  37.8 21.1 %all-to-all-start.2 = ((bf16[32,8,1408]{2,1,0:T(8,128)(2,1)}), bf16[32,8,1408]{2,1,0:T(8,128)(2,1)S(1)}, u32[]{:S(2)}, u32[]{:S(2)}) async-start(bf16[32,8,1408]{2,1,0:T(8,128)(2,1)} %pack.1), calls=%async_computation.2 | async-start | bytes 1441792 | tf_op jit(solution)/shard_map/all_to_all | solution.py:442
  60.8 16.5 %all-to-all-start.3 = ((bf16[4,32,1920]{2,1,0:T(8,128)(2,1)}), bf16[4,32,1920]{2,1,0:T(8,128)(2,1)S(1)}, u32[]{:S(2)}, u32[]{:S(2)}) async-start(bf16[4,32,1920]{2,1,0:T(8,128)(2,1)} %mix.1.order_ref), calls=%async_computation.3 | async-start | bytes 983040 | tf_op jit(solution)/shard_map/all_to_all | solution.py:475

commit v4 on v3

--- a/solution.py
+++ b/solution.py
@@ -60,24 +60,27 @@
     out_ref[...] = jnp.broadcast_to(flat[None], out_ref.shape)
 
 
-def slot_map_kernel(first_ref, ids_ref, map_ref, *, rows_dev, owners, seqs, lookups, slots):
+def slot_map_kernel(z_ref, ids_ref, map_ref, *, rows_dev, owners, seqs, lookups, capacity, tensor):
     requests = seqs * lookups
+    total, width = map_ref.shape
     ids = jnp.concatenate([ids_ref[j : j + 1, :] for j in range(lookups)], axis=1)
     owner = ids // rows_dev
     hit = ones_where(iota((owners, requests), 0) == owner)
     before = ones_where(iota((requests, requests), 0) < iota((requests, requests), 1))
-    count = mm(hit, before)
-    rank = jnp.sum(count * hit.astype(F32), axis=0, keepdims=True).astype(I32)
-    rel = rank - first_ref[0]
-    slot = jnp.where((rel >= 0) & (rel < slots), owner * slots + rel, -1)
-    placed = ones_where(iota((owners * slots, requests), 0) == slot)
-    of_seq = ones_where(iota((seqs, requests), 1) % seqs == iota((seqs, requests), 0))
-    map_ref[...] = mm_nt(placed, of_seq).astype(BF16)
+    rank = jnp.sum(mm(hit, before) * hit.astype(F32), axis=0, keepdims=True).astype(I32)
+    key = owner * capacity + rank - z_ref[0] * (capacity // tensor)
+    row = iota((total, requests), 0)
+    place = row % capacity
+    placed = ones_where(row - place + (place // 8) * 2 + place % 2 == key)
+    of_seq = ones_where(iota((width, requests), 1) % seqs == iota((width, requests), 0) % seqs)
+    part = (iota((total, width), 0) % 8) // 2
+    known = mm_nt(placed, of_seq)
+    map_ref[...] = jnp.where(part == iota((total, width), 1) // seqs, known, 0.0).astype(BF16)
 
 
 def squares_kernel(
-    z_ref, gain_ref, hidden_hbm, key_hbm, table_hbm, order_ref, out_ref, attn_in_ref,
-    hidden_ref, key_ref, table, key_t, squares, sems, *, chunks,
+    z_ref, gain_ref, hidden_hbm, key_hbm, table_hbm, order_ref, squares, u_ref, attn_in_ref,
+    hidden_ref, key_ref, table, key_t, sems, *, chunks,
 ):
     del order_ref
     sub = 256
@@ -104,7 +107,7 @@
     early[1].wait()
     key_t[...] = key_ref[...].T
     u = mm(jnp.concatenate([high, low], axis=0), key_t[...])
-    u = (u[:seqs] + u[seqs:]).astype(BF16)
+    u_ref[...] = (u[:seqs] + u[seqs:]).astype(BF16)
     start = 0
     for copy, size in zip(copies, chunks):
         copy.wait()
@@ -114,15 +117,6 @@
             for g in range(sub // LANES):
                 squares[t // LANES + g : t // LANES + g + 1, :] = line[:, g * LANES : (g + 1) * LANES]
         start += size
-    peers, lines, emb = out_ref.shape
-    tail = lines - seqs
-    parts = three_parts(squares[...])
-    pieces = [p[h : h + tail] for p in parts for h in range(0, squares.shape[0], tail)]
-    rest = emb - LANES * len(pieces)
-    block = jnp.concatenate(pieces + [jnp.zeros((tail, rest), BF16)], axis=1)
-    for p in range(peers):
-        out_ref[p, :seqs, :] = u
-        out_ref[p, seqs:, :] = block
 
 
 def slot_lanes(row, z, slots):
@@ -140,38 +134,39 @@
 
 
 def gather_kernel(
-    me_ref, z_ref, got_ref, table_hbm, rows_ref, ids_ref, idx_vmem, idx_smem, groups, sems,
+    me_ref, z_ref, got_ref, sq_ref, table_hbm, out_ref, idx_vmem, idx_smem, groups, sems,
     *, rows_dev, per, capacity, tensor,
 ):
     askers = got_ref.shape[0] // per
     slots = capacity // tensor
+    n_slots = askers * slots
     before = ones_where(iota((LANES, LANES), 0) < iota((LANES, LANES), 1))
     lane = iota((askers, LANES), 1)
     seen = jnp.zeros((askers, 1), F32)
-    low_rank = z_ref[0] * slots
     ranks, locals_ = [], []
     for j in range(per):
         local = got_ref[pl.ds(j, askers, stride=per), :] - me_ref[0] * rows_dev
         mine = (local >= 0) & (local < rows_dev)
         rank = mm(ones_where(mine), before) + seen
         seen = seen + jnp.sum(jnp.where(mine, 1.0, 0.0), axis=1, keepdims=True)
-        ranks.append(jnp.where(mine, rank.astype(I32) - low_rank, -1))
+        ranks.append(jnp.where(mine, rank, -1.0).astype(I32))
         locals_.append(local.astype(F32))
     row = jnp.zeros((askers, LANES), F32)
-    for k in range(slots):
+    for k in range(capacity):
         one = jnp.where(ranks[0] == k, locals_[0], 0.0)
         for j in range(1, per):
             one = one + jnp.where(ranks[j] == k, locals_[j], 0.0)
         row = jnp.where(lane == k, jnp.sum(one, axis=1, keepdims=True), row)
-    ids_ref[...] = row.astype(I32)
-    idx_vmem[...] = slot_lanes(row, 0, slots).astype(I32)
+    moved = row
+    for z in range(1, tensor):
+        moved = jnp.where(z_ref[0] == z, pltpu.roll(row, LANES - 2 * z, 1), moved)
+    own = jnp.zeros((askers, LANES), F32)
+    for z in range(tensor):
+        piece = moved if z == 0 else pltpu.roll(moved, LANES - (slots - 2) * z, 1)
+        own = jnp.where(lane // 2 == z, piece, own)
+    idx_vmem[...] = slot_lanes(own, 0, slots).astype(I32)
     to_smem = pltpu.make_async_copy(idx_vmem, idx_smem, sems.at[0])
     to_smem.start()
-    n_slots = askers * slots
-    spread = jnp.broadcast_to(row.astype(I32)[:, None, :], (askers, slots, LANES))
-    spread = spread.reshape(n_slots, LANES)
-    keep = iota((n_slots, LANES), 1) == iota((n_slots, LANES), 0) % slots
-    column = jnp.sum(jnp.where(keep, spread % 8, 0).astype(F32), axis=1, keepdims=True)
     to_smem.wait()
     for h in range(n_slots // LANES):
         def issue(i, carry):
@@ -183,50 +178,56 @@
             return carry
 
         lax.fori_loop(0, LANES, issue, 0, unroll=8)
+    ids = row.astype(I32)
+    high, low = ids // LANES, ids % LANES
+    value = jnp.zeros((askers, LANES), F32)
+    for g in range(sq_ref.shape[0]):
+        line = jnp.broadcast_to(sq_ref[g : g + 1, :], (askers, LANES))
+        found = jnp.take_along_axis(line, low, axis=1, mode="promise_in_bounds")
+        value = jnp.where(high == g, found, value)
+    extra = []
+    for z in range(tensor):
+        piece = value if z == 0 else pltpu.roll(value, LANES - slots * z, 1)
+        line = jnp.zeros((askers, LANES), F32)
+        for p, part in enumerate(three_parts(jnp.where(lane < slots, piece, 0.0))):
+            part = part.astype(F32)
+            line = line + (part if p == 0 else pltpu.roll(part, slots * p, 1))
+        extra.append(jnp.broadcast_to(line[:, None, :], (askers, 8, LANES)))
+    total = n_slots * 4
+    extra = jnp.stack(extra, axis=1).reshape(total, LANES)
+    extra = jnp.where(iota((total, LANES), 0) % 8 == 6, extra, 0.0)
+    spread = jnp.broadcast_to((own.astype(I32) % 8)[:, None, :], (askers, capacity, LANES))
+    spread = spread.reshape(total, LANES).astype(F32)
+    place = iota((total, LANES), 0) % capacity
+    keep = iota((total, LANES), 1) == (place // 8) * 2 + place % 2
+    column = jnp.sum(jnp.where(keep, spread, 0.0), axis=1, keepdims=True)
     pltpu.make_async_copy(table_hbm.at[pl.ds(0, n_slots * 8), :], groups, sems.at[1]).wait()
     size = 32
+    width = out_ref.shape[2]
+    emb = groups.shape[1]
+    r, c = iota((4 * size, 8 * size), 0), iota((4 * size, 8 * size), 1)
+    offset = (c - 8 * (2 * (r // 8) + r % 2)).astype(F32)
+    part_of = (r % 8) // 2
     for b in range(n_slots // size):
-        offset = iota((size, size * 8), 1) - 8 * iota((size, size * 8), 0)
-        pick = ones_where(offset.astype(F32) == column[b * size : (b + 1) * size, :])
-        rows_ref[b * size : (b + 1) * size, :] = mm(
-            pick, groups[b * size * 8 : (b + 1) * size * 8, :]
-        ).astype(BF16)
-
-
-def pack_kernel(rows_ref, ids_ref, got_ref, out_ref, *, seqs):
-    owners, slots, _ = out_ref.shape
-    n_slots, emb = rows_ref.shape
-    tail = got_ref.shape[1] - seqs
-    per_part = 32 // tail
-    halves = []
-    for h in range(per_part):
-        total = jnp.zeros((tail, LANES), F32)
-        for p in range(3):
-            c = (p * per_part + h) * LANES
-            for z in range(got_ref.shape[0]):
-                total = total + got_ref[z, seqs:, c : c + LANES].astype(F32)
-        halves.append(total)
-    squares = jnp.concatenate(halves, axis=0)
-    ids = ids_ref[...]
-    high, low = ids // LANES, ids % LANES
-    value = jnp.zeros(ids.shape, F32)
-    for g in range(squares.shape[0]):
-        line = jnp.broadcast_to(squares[g : g + 1, :], ids.shape)
-        found = jnp.take_along_axis(line, low, axis=1, mode="promise_in_bounds")
-        value = jnp.where(high == g, found, value)
-    spread = jnp.broadcast_to(value[:, None, :], (owners, slots, LANES)).reshape(n_slots, LANES)
-    lane = iota((n_slots, LANES), 1)
-    keep = lane == iota((n_slots, LANES), 0) % slots
-    column = jnp.sum(jnp.where(keep, spread, 0.0), axis=1, keepdims=True)
-    extra = jnp.zeros((n_slots, LANES), F32)
-    for p, part in enumerate(three_parts(column)):
-        extra = jnp.where(lane == p, part.astype(F32), extra)
-    out_ref[:, :, :emb] = rows_ref[...].reshape(owners, slots, emb)
-    out_ref[:, :, emb:] = extra.astype(BF16).reshape(owners, slots, LANES)
+        rows = slice(b * 4 * size, (b + 1) * 4 * size)
+        pick = jnp.where(offset == column[rows], 1.0, 0.0)
+        blocks = []
+        for q in range(4):
+            chosen = jnp.where(part_of == q, pick, 0.0).astype(BF16)
+            end = min(emb, (q + 1) * width)
+            blocks.append(mm(chosen, groups[b * 8 * size : (b + 1) * 8 * size, q * width : end]))
+        full = blocks[0] + blocks[1] + blocks[2]
+        whole_part = jnp.concatenate(
+            [full[:, :LANES] + blocks[3], full[:, LANES : 2 * LANES] + extra[rows], full[:, 2 * LANES :]],
+            axis=1,
+        )
+        out_ref[b * size // 2 : (b + 1) * size // 2] = whole_part.astype(BF16).reshape(
+            size // 2, 8, width
+        )
 
 
 def attention_kernel(
-    lens_ref, first_ref, ids_ref, x_ref, qw_hbm, kvw_hbm, key_hbm, val_hbm, ow_hbm,
+    lens_ref, z_ref, ids_ref, x_ref, qw_hbm, kvw_hbm, key_hbm, val_hbm, ow_hbm,
     out_ref, map_ref, qw, kvw, key, val, ow, sems, *, mapping,
 ):
     seqs, width = x_ref.shape
@@ -247,7 +248,7 @@
     ]
     for copy in copies:
         copy.start()
-    slot_map_kernel(first_ref, ids_ref, map_ref, **mapping)
+    slot_map_kernel(z_ref, ids_ref, map_ref, **mapping)
     x = x_ref[...]
     copies[0].wait()
     query = mm(x, qw[...]).astype(BF16)
@@ -305,26 +306,44 @@
     out_ref[...] = mm(jnp.concatenate(flat, axis=1), ow[...]).astype(BF16)
 
 
-def mix_kernel(rows_ref, map_ref, got_ref, attn_ref, out_ref, *, width):
-    _, seqs = map_ref.shape
-    emb = got_ref.shape[2]
-    rows = rows_ref[:, :emb]
+def mix_kernel(got_ref, map_ref, u_ref, more_u_ref, attn_ref, out_ref, *, width):
+    total, columns = map_ref.shape
+    seqs, emb = u_ref.shape
+    part = got_ref.shape[2]
+    rows = got_ref[...].reshape(total, part)
     of_seq = map_ref[...].astype(F32)
-    u = got_ref[0, :seqs, :].astype(F32)
-    for z in range(1, got_ref.shape[0]):
-        u = u + got_ref[z, :seqs, :].astype(F32)
+    u = u_ref[...].astype(F32) + more_u_ref[...].astype(F32)
+    parts = columns // seqs
+    u = jnp.concatenate([u, jnp.zeros((seqs, parts * part - emb), F32)], axis=1)
+    u = jnp.concatenate([u[:, q * part : (q + 1) * part] for q in range(parts)], axis=0)
     u_high, u_low = two_parts(u)
-    cross_all = mm_nt(rows, u_high) + mm_nt(rows, u_low)
-    cross = jnp.sum(cross_all * of_seq, axis=1, keepdims=True)
-    square = jnp.sum(rows_ref[:, emb:].astype(F32), axis=1, keepdims=True)
+    cross_all = (mm_nt(rows, u_high) + mm_nt(rows, u_low)) * of_seq
+    r, c = iota((LANES, LANES), 0), iota((LANES, LANES), 1)
+    same = ones_where((r // 8 == c // 8) & (r % 2 == c % 2))
+    sums = []
+    for b in range(0, total, LANES):
+        high, mid, low = three_parts(cross_all[b : b + LANES, :])
+        sums.append(mm(same, high) + (mm(same, mid) + mm(same, low)))
+    cross = jnp.sum(jnp.concatenate(sums, axis=0), axis=1, keepdims=True)
+    owners = total // 32
+    row = iota((total, LANES), 0)
+    extra = jnp.where(row % 8 == 6, rows[:, LANES : 2 * LANES].astype(F32), 0.0)
+    extra = jnp.sum(extra.reshape(owners, 32, LANES), axis=1)
+    square = extra + (pltpu.roll(extra, LANES - 8, 1) + pltpu.roll(extra, LANES - 16, 1))
+    spread = jnp.broadcast_to(square[:, None, :], (owners, 32, LANES)).reshape(total, LANES)
+    place = row % 32
+    keep = iota((total, LANES), 1) == (place // 8) * 2 + place % 2
+    square = jnp.sum(jnp.where(keep, spread, 0.0), axis=1, keepdims=True)
     gate = jax.nn.sigmoid(cross * lax.rsqrt(square / width + EPS) / math.sqrt(width))
     g_high, g_low = two_parts(of_seq * gate)
-    mixed = (mm_tn(g_high, rows) + mm_tn(g_low, rows)).astype(BF16)
-    peers, _, _ = out_ref.shape
-    part = width // peers
+    mixed = mm_tn(g_high, rows) + mm_tn(g_low, rows)
+    mixed = jnp.concatenate([mixed[q * seqs : (q + 1) * seqs, :] for q in range(parts)], axis=1)
+    mixed = mixed[:, :emb].astype(BF16)
+    peers = out_ref.shape[0]
+    own = width // peers
     for p in range(peers):
-        out_ref[p, :, :part] = attn_ref[:, p * part : (p + 1) * part]
-        out_ref[p, :, part:] = mixed
+        out_ref[p, :, :own] = attn_ref[:, p * own : (p + 1) * own]
+        out_ref[p, :, own:] = mixed
 
 
 def fetch_kernel(value_hbm, hidden_hbm, order_ref, value_ref, hidden_ref, sems):
@@ -395,12 +414,13 @@
     me = me_table.astype(I32).reshape(1)
     z = me_tensor.astype(I32).reshape(1)
     chunks = (256, 256, 512, 1024, 1024, 1024)
-    shares, attn_in = pl.pallas_call(
+    squares, u, attn_in = pl.pallas_call(
         lambda *refs: squares_kernel(*refs, chunks=chunks),
         in_specs=[smem, vmem, hbm, hbm, hbm, hbm],
-        out_specs=[vmem, vmem],
+        out_specs=[vmem, vmem, vmem],
         out_shape=[
-            jax.ShapeDtypeStruct((tensor, seqs + 16, emb), BF16),
+            pltpu.VMEM((rows_dev // LANES, LANES), F32),
+            jax.ShapeDtypeStruct((seqs, emb), BF16),
             jax.ShapeDtypeStruct(hidden.shape, BF16),
         ],
         scratch_shapes=[
@@ -408,20 +428,22 @@
             pltpu.VMEM(key_proj.shape, BF16),
             pltpu.VMEM(table.shape, BF16),
             pltpu.VMEM((part, emb), BF16),
-            pltpu.VMEM((rows_dev // LANES, LANES), F32),
             pltpu.SemaphoreType.DMA((len(chunks) + 2,)),
         ],
         name="squares",
     )(z, attn_gain, hidden, key_proj, table, send)
-    got_shares = lax.all_to_all(shares, "tensor", 0, 0, tiled=True)
-
-    rows, row_ids = pl.pallas_call(
+
+    def other(x, step):
+        return lax.ppermute(x, "tensor", [(i, i ^ step) for i in range(tensor)])
+
+    more_u = other(u, 1)
+    packed = pl.pallas_call(
         lambda *refs: gather_kernel(
             *refs, rows_dev=rows_dev, per=per, capacity=capacity, tensor=tensor
         ),
-        in_specs=[smem, smem, vmem, hbm],
-        out_specs=[vmem, vmem],
-        out_shape=[pltpu.VMEM((n_slots, emb), BF16), pltpu.VMEM((owners, LANES), I32)],
+        in_specs=[smem, smem, vmem, vmem, hbm],
+        out_specs=vmem,
+        out_shape=jax.ShapeDtypeStruct((owners * tensor, 8, 3 * LANES), BF16),
         scratch_shapes=[
             pltpu.VMEM((n_slots // LANES, LANES), I32),
             pltpu.SMEM((n_slots // LANES, LANES), I32),
@@ -429,27 +451,20 @@
             pltpu.SemaphoreType.DMA((2,)),
         ],
         name="gather",
-    )(me, z, near(got_ids.reshape(owners * per, LANES)), table)
-
-    near_shares = near(got_shares)
-    packed = pl.pallas_call(
-        lambda *refs: pack_kernel(*refs, seqs=seqs),
-        in_specs=[vmem] * 3,
-        out_specs=vmem,
-        out_shape=jax.ShapeDtypeStruct((owners, slots, emb + LANES), BF16),
-        name="pack",
-    )(near(rows), near(row_ids), near_shares)
-    got_rows = lax.all_to_all(packed, "table", 0, 0, tiled=True)
+    )(me, z, near(got_ids.reshape(owners * per, LANES)), near(squares), table)
+    got_rows = lax.all_to_all(packed, ("table", "tensor"), 0, 0, tiled=True)
+    u = (u.astype(F32) + more_u.astype(F32)).astype(BF16)
+    more_u = other(u, 2)
 
     _, kv_width = key_cache.shape[1:]
-    mapping = dict(rows_dev=rows_dev, owners=owners, seqs=seqs, lookups=lookups, slots=slots)
+    mapping = dict(rows_dev=rows_dev, owners=owners, seqs=seqs, lookups=lookups, capacity=capacity, tensor=tensor)
     attention, slot_map = pl.pallas_call(
         lambda *refs: attention_kernel(*refs, mapping=mapping),
         in_specs=[smem, smem, vmem, vmem, hbm, hbm, hbm, hbm, hbm],
         out_specs=[vmem, vmem],
         out_shape=[
             pltpu.VMEM((seqs, width), BF16),
-            pltpu.VMEM((n_slots, seqs), BF16),
+            pltpu.VMEM((4 * n_slots, 4 * seqs), BF16),
         ],
         scratch_shapes=[
             pltpu.VMEM(q_weight.shape, BF16),
@@ -461,17 +476,17 @@
         ],
         name="attention",
     )(
-        cache_lengths, z * slots, ids_t, attn_in, q_weight,
+        cache_lengths, z, ids_t, attn_in, q_weight,
         kv_weight.reshape(2 * width, kv_width), key_cache, value_cache, out_weight,
     )
 
     mixes = pl.pallas_call(
         lambda *refs: mix_kernel(*refs, width=width),
-        in_specs=[vmem] * 4,
+        in_specs=[vmem] * 5,
         out_specs=vmem,
         out_shape=jax.ShapeDtypeStruct((tensor, seqs, part + emb), BF16),
         name="mix",
-    )(near(got_rows.reshape(n_slots, emb + LANES)), near(slot_map), near_shares, near(attention))
+    )(near(got_rows), near(slot_map), near(u), near(more_u), near(attention))
     got_mixes = lax.all_to_all(mixes, "tensor", 0, 0, tiled=True)
 
     value_near, hidden_near = pl.pallas_call(

time: 79.1 us -> 80.9 us (1.023)
  the two profiles are of different devices: /device:TPU:0 before, /device:TPU:10 now
where the time goes in v4:
time: 80.9 us; the launch traced here: 80.4 us
  Pallas kernels  34.1 us (42%)
  starting transfers between devices  28 us (35%)
  waiting for transfers between devices  18.2 us (22%)
    pallas_call x1, Pallas kernels, body(): pl.pallas_call(lambda *refs: squares_kernel(*refs, chunks=chunks), in_spe...  11.8 us
    all_to_all x1, starting transfers between devices, body(): got_rows = lax.all_to_all(packed, ('table', 'tensor'), 0, 0, tiled=True)  11.7 us
    ppermute x2, waiting for transfers between devices, other(): return lax.ppermute(x, 'tensor', [(i, i ^ step) for i in range(tensor)])  10.5 us
    pallas_call x1, Pallas kernels, body(): pl.pallas_call(lambda *refs: gather_kernel(*refs, rows_dev=rows_dev, per=...  9.15 us
    all_to_all x1, waiting for transfers between devices, body(): got_mixes = lax.all_to_all(mixes, 'tensor', 0, 0, tiled=True)  7.64 us
    all_to_all x1, starting transfers between devices, body(): got_ids = lax.all_to_all(send, 'table', 0, 0, tiled=True)  7.51 us
    pallas_call x1, Pallas kernels, body(): pl.pallas_call(lambda *refs: attention_kernel(*refs, mapping=mapping), in...  6.83 us
    ppermute x2, starting transfers between devices, other(): return lax.ppermute(x, 'tensor', [(i, i ^ step) for i in range(tensor)])  5.32 us
  transfers between devices with their start and end apart: 5, of which 2 were waited for; matrix products, arithmetic and copies ran while one was open for 0% of the time, Pallas kernels for 25%

profile of v4, /device:TPU:10, one launch (start us, length us, event | category | flops | bytes accessed | tf_op | source)
XLA Modules:
  0.0 80.4 jit_solution(16016878162770700538)
XLA Ops:
  0.0 1.4 %send_ids.1.refs_5_ = s32[32,4,128]{2,1,0:T(4,128)} custom-call(s32[16,32]{1,0:T(8,128)} %bitcast.7), custom_call_target="tpu_custom_call" | custom-call | tf_op jit(solution)/shard_map/send_ids/pallas_call | solution.py:404
  1.4 7.5 %all-to-all-start = ((s32[32,4,128]{2,1,0:T(4,128)}), s32[32,4,128]{2,1,0:T(4,128)S(1)}, u32[]{:S(2)}, u32[]{:S(2)}) async-start(s32[32,4,128]{2,1,0:T(4,128)} %send_ids.1.refs_5_), calls=%async_computation | async-start | bytes 131072 | tf_op jit(solution)/shard_map/all_to_all | solution.py:409
  8.9 11.8 %squares.1 = (f32[32,128]{1,0:T(8,128)S(1)}, bf16[32,1280]{1,0:T(8,128)(2,1)}, bf16[32,2560]{1,0:T(8,128)(2,1)}) custom-call(s32[1]{0:T(128)} %bitcast.refs_0_.refs_1_.z_ref, f32[2560]{0:T(1024)} %refs_1_.1, bf16[32,2560]{1,0:T(8,128)(2,1)} %hidden_hbm.1, bf16[1280,640]{1,0:T(8,128)(2,1)} %refs_3_.1, bf16[4096,1280]{1,0:T(8,128)(2,1)} %refs_4_.4, ...), custom_call_target="tpu_custom_call" | custom-call | tf_op jit(solution)/shard_map/squares/pallas_call | solution.py:417
  20.8 0.0 all-to-all-done
  20.8 0.0 copy-start
  20.8 9.2 %gather.1 = bf16[128,8,384]{2,1,0:T(8,128)(2,1)} custom-call(s32[1]{0:T(128)} %bitcast.1.refs_0_, s32[1]{0:T(128)} %bitcast.refs_0_.refs_1_.z_ref, s32[128,128]{1,0:T(8,128)S(1)} %bitcast.5, f32[32,128]{1,0:T(8,128)S(1)} %get-tuple-element.12.refs_3_, bf16[4096,1280]{1,0:T(8,128)(2,1)} %refs_4_.4), custom_call_target="tpu_custom_call" | custom-call | tf_op jit(solution)/shard_map/gather/pallas_call | solution.py:440
  29.9 11.7 %all-to-all-start.1 = ((bf16[128,8,384]{2,1,0:T(8,128)(2,1)}), bf16[128,8,384]{2,1,0:T(8,128)(2,1)S(1)}, u32[]{:S(2)}, u32[]{:S(2)}) async-start(bf16[128,8,384]{2,1,0:T(8,128)(2,1)} %gather.1), calls=%async_computation.1 | async-start | bytes 1572864 | tf_op jit(solution)/shard_map/all_to_all | solution.py:455
  41.6 0.0 copy-done
  41.6 1.7 %collective-permute-start = (bf16[32,1280]{1,0:T(8,128)(2,1)S(1)}, bf16[32,1280]{1,0:T(8,128)(2,1)S(1)}, u32[]{:S(2)}, u32[]{:S(2)}) collective-permute-start(bf16[32,1280]{1,0:T(8,128)(2,1)S(1)} %copy-done), channel_id=1, source_target_pairs={{0,1},{1,0},{2,3},{3,2},{4,5},{5,4},{6,7},{7,6},{8,9},{9,8},{10,11... | collective-permute-start | bytes 245768 | tf_op jit(solution)/shard_map/ppermute | solution.py:437
  43.4 10.5 %collective-permute-done = bf16[32,1280]{1,0:T(8,128)(2,1)S(1)} collective-permute-done((bf16[32,1280]{1,0:T(8,128)(2,1)S(1)}, bf16[32,1280]{1,0:T(8,128)(2,1)S(1)}, u32[]{:S(2)}, u32[]{:S(2)}) %collective-permute-start) | collective-permute-done | bytes 81952 | tf_op jit(solution)/shard_map/ppermute | solution.py:437
  54.0 3.6 %collective-permute-start.1 = (bf16[32,1280]{1,0:T(8,128)(2,1)S(1)}, bf16[32,1280]{1,0:T(8,128)(2,1)S(1)}, u32[]{:S(2)}, u32[]{:S(2)}) collective-permute-start(bf16[32,1280]{1,0:T(8,128)(2,1)S(1)} %add_convert_fusion.refs_2_), channel_id=1, source_target_pairs={{0,2},{1,3},{2,0},{3,1},{4,6},{5,7},{6,4},{7,5},{8,10},{9,11},{10,... | collective-permute-start | bytes 245768 | tf_op jit(solution)/shard_map/ppermute | solution.py:437
  57.5 6.8 %attention.1 = (bf16[32,2560]{1,0:T(8,128)(2,1)S(1)}, bf16[1024,128]{1,0:T(8,128)(2,1)S(1)}) custom-call(s32[32]{0:T(128)} %refs_0_.1, s32[1]{0:T(128)} %bitcast.refs_0_.refs_1_.z_ref, s32[16,32]{1,0:T(8,128)} %bitcast.8, bf16[32,2560]{1,0:T(8,128)(2,1)} %get-tuple-element.13.refs_3_, bf16[2560,640]{1,0:T(8,128)(2,1)} %refs_4_.5, bf16[5120,128]{1,0:T(8,128)(2,1)} %bitcast.6, ...), custom_call_target="tpu_custom_call" | custom-call | tf_op jit(solution)/shard_map/attention/pallas_call | solution.py:461
  64.4 0.0 collective-permute-done.1.refs_3_
  64.4 0.0 all-to-all-done.1.refs_0_
  64.4 2.3 %mix.1.order_ref = bf16[4,32,1920]{2,1,0:T(8,128)(2,1)} custom-call(bf16[128,8,384]{2,1,0:T(8,128)(2,1)S(1)} %all-to-all-done.1.refs_0_, bf16[1024,128]{1,0:T(8,128)(2,1)S(1)} %get-tuple-element.14.refs_1_, bf16[32,1280]{1,0:T(8,128)(2,1)S(1)} %add_convert_fusion.refs_2_, bf16[32,1280]{1,0:T(8,128)(2,1)S(1)} %collective-permute-done.1.refs_3_, ...), custom_call_target="tpu_custom_call" | custom-call | tf_op jit(solution)/shard_map/mix/pallas_call | solution.py:483
  66.7 3.5 %all-to-all-start.2 = ((bf16[4,32,1920]{2,1,0:T(8,128)(2,1)}), bf16[4,32,1920]{2,1,0:T(8,128)(2,1)S(1)}, u32[]{:S(2)}, u32[]{:S(2)}) async-start(bf16[4,32,1920]{2,1,0:T(8,128)(2,1)} %mix.1.order_ref), calls=%async_computation.2 | async-start | bytes 983040 | tf_op jit(solution)/shard_map/all_to_all | solution.py:490
  70.1 1.5 %fetch_value.1 = (bf16[1280,640]{1,0:T(8,128)(2,1)S(1)}, bf16[32,2560]{1,0:T(8,128)(2,1)S(1)}) custom-call(bf16[1280,640]{1,0:T(8,128)(2,1)} %value_hbm.1, bf16[32,2560]{1,0:T(8,128)(2,1)} %hidden_hbm.1, bf16[4,32,1920]{2,1,0:T(8,128)(2,1)} %mix.1.order_ref), custom_call_target="tpu_custom_call" | custom-call | tf_op jit(solution)/shard_map/fetch_value/pallas_call | solution.py:492
  71.6 7.6 %all-to-all-done.2.got_ref = bf16[4,32,1920]{2,1,0:T(8,128)(2,1)S(1)} async-done(((bf16[4,32,1920]{2,1,0:T(8,128)(2,1)}), bf16[4,32,1920]{2,1,0:T(8,128)(2,1)S(1)}, u32[]{:S(2)}, u32[]{:S(2)}) %all-to-all-start.2) | async-done | bytes 491552 | tf_op jit(solution)/shard_map/all_to_all | solution.py:490
  79.2 1.2 %final.1 = bf16[32,640]{1,0:T(8,128)(2,1)} custom-call(s32[1]{0:T(128)} %bitcast.refs_0_.refs_1_.z_ref, bf16[4,32,1920]{2,1,0:T(8,128)(2,1)S(1)} %all-to-all-done.2.got_ref, bf16[1280,640]{1,0:T(8,128)(2,1)S(1)} %get-tuple-element.17.value_ref, bf16[32,2560]{1,0:T(8,128)(2,1)S(1)} %get-tuple-element.18.hidden_ref), custom_call_target="tpu_custom_call" | custom-call | tf_op jit(solution)/shard_map/final/pallas_call | solution.py:501
  (1 shorter events, 0.0 us)
Async XLA Ops:
  1.4 19.4 %all-to-all-start = ((s32[32,4,128]{2,1,0:T(4,128)}), s32[32,4,128]{2,1,0:T(4,128)S(1)}, u32[]{:S(2)}, u32[]{:S(2)}) async-start(s32[32,4,128]{2,1,0:T(4,128)} %send_ids.1.refs_5_), calls=%async_computation | async-start | bytes 131072 | tf_op jit(solution)/shard_map/all_to_all | solution.py:409
  20.8 20.9 %copy-start = (bf16[32,1280]{1,0:T(8,128)(2,1)S(1)}, bf16[32,1280]{1,0:T(8,128)(2,1)}, u32[]{:S(2)}) copy-start(bf16[32,1280]{1,0:T(8,128)(2,1)} %get-tuple-element.15) | copy-start | bytes 245764
  29.9 34.4 %all-to-all-start.1 = ((bf16[128,8,384]{2,1,0:T(8,128)(2,1)}), bf16[128,8,384]{2,1,0:T(8,128)(2,1)S(1)}, u32[]{:S(2)}, u32[]{:S(2)}) async-start(bf16[128,8,384]{2,1,0:T(8,128)(2,1)} %gather.1), calls=%async_computation.1 | async-start | bytes 1572864 | tf_op jit(solution)/shard_map/all_to_all | solution.py:455
  41.6 12.3 %collective-permute-start = (bf16[32,1280]{1,0:T(8,128)(2,1)S(1)}, bf16[32,1280]{1,0:T(8,128)(2,1)S(1)}, u32[]{:S(2)}, u32[]{:S(2)}) collective-permute-start(bf16[32,1280]{1,0:T(8,128)(2,1)S(1)} %copy-done), channel_id=1, source_target_pairs={{0,1},{1,0},{2,3},{3,2},{4,5},{5,4},{6,7},{7,6},{8,9},{9,8},{10,11... | collective-permute-start | bytes 245768 | tf_op jit(solution)/shard_map/ppermute | solution.py:437
  54.0 10.4 %collective-permute-start.1 = (bf16[32,1280]{1,0:T(8,128)(2,1)S(1)}, bf16[32,1280]{1,0:T(8,128)(2,1)S(1)}, u32[]{:S(2)}, u32[]{:S(2)}) collective-permute-start(bf16[32,1280]{1,0:T(8,128)(2,1)S(1)} %add_convert_fusion.refs_2_), channel_id=1, source_target_pairs={{0,2},{1,3},{2,0},{3,1},{4,6},{5,7},{6,4},{7,5},{8,10},{9,11},{10,... | collective-permute-start | bytes 245768 | tf_op jit(solution)/shard_map/ppermute | solution.py:437
  66.7 12.6 %all-to-all-start.2 = ((bf16[4,32,1920]{2,1,0:T(8,128)(2,1)}), bf16[4,32,1920]{2,1,0:T(8,128)(2,1)S(1)}, u32[]{:S(2)}, u32[]{:S(2)}) async-start(bf16[4,32,1920]{2,1,0:T(8,128)(2,1)} %mix.1.order_ref), calls=%async_computation.2 | async-start | bytes 983040 | tf_op jit(solution)/shard_map/all_to_all | solution.py:490

commit v5 on v4

--- a/solution.py
+++ b/solution.py
@@ -48,19 +48,45 @@
     return high, mid, (rest - mid.astype(F32)).astype(BF16)
 
 
-def send_ids_kernel(ids_ref, out_ref):
-    _, per, _ = out_ref.shape
+def start_kernel(
+    ids_hbm, gain_hbm, hidden_hbm, key_hbm, send_hbm, u_ref, attn_in_ref, key_t,
+    ids_ref, gain_ref, hidden_ref, key_ref, send_ref, sems,
+):
+    copies = [
+        pltpu.make_async_copy(src, dst, sems.at[i])
+        for i, (src, dst) in enumerate(
+            ((ids_hbm, ids_ref), (hidden_hbm, hidden_ref), (gain_hbm, gain_ref), (key_hbm, key_ref))
+        )
+    ]
+    for copy in copies:
+        copy.start()
+    _, per, _ = send_ref.shape
     _, seqs = ids_ref.shape
     fit = LANES // seqs
+    copies[0].wait()
     flat = [
         jnp.concatenate([ids_ref[j * fit + q : j * fit + q + 1, :] for q in range(fit)], axis=1)
         for j in range(per)
     ]
-    flat = jnp.concatenate(flat, axis=0)
-    out_ref[...] = jnp.broadcast_to(flat[None], out_ref.shape)
-
-
-def slot_map_kernel(z_ref, ids_ref, map_ref, *, rows_dev, owners, seqs, lookups, capacity, tensor):
+    send_ref[...] = jnp.broadcast_to(jnp.concatenate(flat, axis=0)[None], send_ref.shape)
+    out = pltpu.make_async_copy(send_ref, send_hbm, sems.at[4])
+    out.start()
+    copies[1].wait()
+    part = key_ref.shape[1]
+    hidden = hidden_ref[...].astype(F32)
+    inv = lax.rsqrt(jnp.mean(hidden * hidden, axis=1, keepdims=True) + EPS)
+    copies[2].wait()
+    attn_in_ref[...] = (hidden * inv * gain_ref[...].reshape(1, hidden.shape[1])).astype(BF16)
+    first = pl.multiple_of(lax.axis_index("tensor") * part, LANES)
+    high, low = two_parts(hidden_ref[:, pl.ds(first, part)].astype(F32) * inv)
+    copies[3].wait()
+    key_t[...] = key_ref[...].T
+    u = mm(jnp.concatenate([high, low], axis=0), key_t[...])
+    u_ref[...] = (u[:seqs] + u[seqs:]).astype(BF16)
+    out.wait()
+
+
+def slot_map_kernel(ids_ref, map_ref, *, rows_dev, owners, seqs, lookups, capacity, tensor):
     requests = seqs * lookups
     total, width = map_ref.shape
     ids = jnp.concatenate([ids_ref[j : j + 1, :] for j in range(lookups)], axis=1)
@@ -68,7 +94,7 @@
     hit = ones_where(iota((owners, requests), 0) == owner)
     before = ones_where(iota((requests, requests), 0) < iota((requests, requests), 1))
     rank = jnp.sum(mm(hit, before) * hit.astype(F32), axis=0, keepdims=True).astype(I32)
-    key = owner * capacity + rank - z_ref[0] * (capacity // tensor)
+    key = owner * capacity + rank - lax.axis_index("tensor") * (capacity // tensor)
     row = iota((total, requests), 0)
     place = row % capacity
     placed = ones_where(row - place + (place // 8) * 2 + place % 2 == key)
@@ -78,45 +104,39 @@
     map_ref[...] = jnp.where(part == iota((total, width), 1) // seqs, known, 0.0).astype(BF16)
 
 
-def squares_kernel(
-    z_ref, gain_ref, hidden_hbm, key_hbm, table_hbm, order_ref, squares, u_ref, attn_in_ref,
-    hidden_ref, key_ref, table, key_t, sems, *, chunks,
-):
-    del order_ref
-    sub = 256
-    early = [
-        pltpu.make_async_copy(hidden_hbm, hidden_ref, sems.at[len(chunks)]),
-        pltpu.make_async_copy(key_hbm, key_ref, sems.at[len(chunks) + 1]),
-    ]
-    for copy in early:
-        copy.start()
+def fetch_rows(table_hbm, table, sems, first, chunks):
     copies, start = [], 0
     for i, size in enumerate(chunks):
-        rows = pl.ds(start, size)
-        copies.append(pltpu.make_async_copy(table_hbm.at[rows, :], table.at[rows, :], sems.at[i]))
+        copies.append(
+            pltpu.make_async_copy(
+                table_hbm.at[pl.ds(first + start, size), :],
+                table.at[pl.ds(start, size), :],
+                sems.at[i],
+            )
+        )
         copies[-1].start()
         start += size
-    part = key_ref.shape[1]
-    seqs = hidden_ref.shape[0]
-    early[0].wait()
-    hidden = hidden_ref[...].astype(F32)
-    inv = lax.rsqrt(jnp.mean(hidden * hidden, axis=1, keepdims=True) + EPS)
-    attn_in_ref[...] = (hidden * inv * gain_ref[...].reshape(1, hidden.shape[1])).astype(BF16)
-    first = pl.multiple_of(z_ref[0] * part, LANES)
-    high, low = two_parts(hidden_ref[:, pl.ds(first, part)].astype(F32) * inv)
-    early[1].wait()
-    key_t[...] = key_ref[...].T
-    u = mm(jnp.concatenate([high, low], axis=0), key_t[...])
-    u_ref[...] = (u[:seqs] + u[seqs:]).astype(BF16)
-    start = 0
+    return copies
+
+
+def row_squares(key_t, table, squares, copies, first, chunks, between=None):
+    sub, start = 256, 0
     for copy, size in zip(copies, chunks):
         copy.wait()
         for t in range(start, start + size, sub):
+            if between is not None and t == 0:
+                for i in range(sum(chunks) // sub):
+                    between(i)
             keys = mm_nt(key_t[...], table[t : t + sub, :])
             line = jnp.sum(keys * keys, axis=0, keepdims=True)
             for g in range(sub // LANES):
-                squares[t // LANES + g : t // LANES + g + 1, :] = line[:, g * LANES : (g + 1) * LANES]
+                group = (first + t) // LANES + g
+                squares[group : group + 1, :] = line[:, g * LANES : (g + 1) * LANES]
         start += size
+
+
+def squares_kernel(key_t, table_hbm, squares, table, sems, *, chunks):
+    row_squares(key_t, table, squares, fetch_rows(table_hbm, table, sems, 0, chunks), 0, chunks)
 
 
 def slot_lanes(row, z, slots):
@@ -134,50 +154,59 @@
 
 
 def gather_kernel(
-    me_ref, z_ref, got_ref, sq_ref, table_hbm, out_ref, idx_vmem, idx_smem, groups, sems,
-    *, rows_dev, per, capacity, tensor,
+    got_ref, some_ref, key_t, table_hbm, out_hbm,
+    idx_vmem, idx_smem, groups, out_ref, table, sq_ref, sems, table_sems,
+    *, rows_dev, per, capacity, tensor, chunks,
 ):
     askers = got_ref.shape[0] // per
     slots = capacity // tensor
     n_slots = askers * slots
+    me, mine_z = lax.axis_index("table"), lax.axis_index("tensor")
+    done = some_ref.shape[0]
+    copies = fetch_rows(table_hbm, table, table_sems, done * LANES, chunks)
+    sq_ref[:done, :] = some_ref[...]
     before = ones_where(iota((LANES, LANES), 0) < iota((LANES, LANES), 1))
     lane = iota((askers, LANES), 1)
     seen = jnp.zeros((askers, 1), F32)
     ranks, locals_ = [], []
     for j in range(per):
-        local = got_ref[pl.ds(j, askers, stride=per), :] - me_ref[0] * rows_dev
+        local = got_ref[pl.ds(j, askers, stride=per), :] - me * rows_dev
         mine = (local >= 0) & (local < rows_dev)
         rank = mm(ones_where(mine), before) + seen
         seen = seen + jnp.sum(jnp.where(mine, 1.0, 0.0), axis=1, keepdims=True)
         ranks.append(jnp.where(mine, rank, -1.0).astype(I32))
         locals_.append(local.astype(F32))
-    row = jnp.zeros((askers, LANES), F32)
-    for k in range(capacity):
-        one = jnp.where(ranks[0] == k, locals_[0], 0.0)
+
+    def ranked(target):
+        one = jnp.where(ranks[0] == target, locals_[0], 0.0)
         for j in range(1, per):
-            one = one + jnp.where(ranks[j] == k, locals_[j], 0.0)
-        row = jnp.where(lane == k, jnp.sum(one, axis=1, keepdims=True), row)
-    moved = row
-    for z in range(1, tensor):
-        moved = jnp.where(z_ref[0] == z, pltpu.roll(row, LANES - 2 * z, 1), moved)
+            one = one + jnp.where(ranks[j] == target, locals_[j], 0.0)
+        return jnp.sum(one, axis=1, keepdims=True)
+
     own = jnp.zeros((askers, LANES), F32)
-    for z in range(tensor):
-        piece = moved if z == 0 else pltpu.roll(moved, LANES - (slots - 2) * z, 1)
-        own = jnp.where(lane // 2 == z, piece, own)
+    for k in range(slots):
+        own = jnp.where(lane == k, ranked((k // 2) * slots + k % 2 + 2 * mine_z), own)
     idx_vmem[...] = slot_lanes(own, 0, slots).astype(I32)
     to_smem = pltpu.make_async_copy(idx_vmem, idx_smem, sems.at[0])
     to_smem.start()
+    row = jnp.zeros((askers, LANES), F32)
+    for k in range(capacity):
+        row = jnp.where(lane == k, ranked(k), row)
     to_smem.wait()
-    for h in range(n_slots // LANES):
-        def issue(i, carry):
-            base = pl.multiple_of((idx_smem[h, i] // 8) * 8, 8)
-            place = pl.multiple_of((h * LANES + i) * 8, 8)
+    half = n_slots // 2
+    steps = sum(chunks) // 256
+    each = n_slots // steps
+
+    def issue(step):
+        for s in range(step * each, (step + 1) * each):
+            base = pl.multiple_of((idx_smem[s // LANES, s % LANES] // 8) * 8, 8)
             pltpu.make_async_copy(
-                table_hbm.at[pl.ds(base, 8), :], groups.at[pl.ds(place, 8), :], sems.at[1]
+                table_hbm.at[pl.ds(base, 8), :],
+                groups.at[pl.ds(s * 8, 8), :],
+                sems.at[1 + s // half],
             ).start()
-            return carry
-
-        lax.fori_loop(0, LANES, issue, 0, unroll=8)
+
+    row_squares(key_t, table, sq_ref, copies, done * LANES, chunks, issue)
     ids = row.astype(I32)
     high, low = ids // LANES, ids % LANES
     value = jnp.zeros((askers, LANES), F32)
@@ -192,42 +221,51 @@
         for p, part in enumerate(three_parts(jnp.where(lane < slots, piece, 0.0))):
             part = part.astype(F32)
             line = line + (part if p == 0 else pltpu.roll(part, slots * p, 1))
-        extra.append(jnp.broadcast_to(line[:, None, :], (askers, 8, LANES)))
-    total = n_slots * 4
-    extra = jnp.stack(extra, axis=1).reshape(total, LANES)
-    extra = jnp.where(iota((total, LANES), 0) % 8 == 6, extra, 0.0)
-    spread = jnp.broadcast_to((own.astype(I32) % 8)[:, None, :], (askers, capacity, LANES))
-    spread = spread.reshape(total, LANES).astype(F32)
-    place = iota((total, LANES), 0) % capacity
-    keep = iota((total, LANES), 1) == (place // 8) * 2 + place % 2
+        extra.append(line.astype(BF16))
+    extra = jnp.concatenate(extra, axis=0)
+    spread = jnp.broadcast_to((own.astype(I32) % 8)[:, None, :], (askers, slots, LANES))
+    spread = spread.reshape(n_slots, LANES).astype(F32)
+    keep = iota((n_slots, LANES), 1) == iota((n_slots, LANES), 0) % slots
     column = jnp.sum(jnp.where(keep, spread, 0.0), axis=1, keepdims=True)
-    pltpu.make_async_copy(table_hbm.at[pl.ds(0, n_slots * 8), :], groups, sems.at[1]).wait()
     size = 32
     width = out_ref.shape[2]
     emb = groups.shape[1]
-    r, c = iota((4 * size, 8 * size), 0), iota((4 * size, 8 * size), 1)
-    offset = (c - 8 * (2 * (r // 8) + r % 2)).astype(F32)
-    part_of = (r % 8) // 2
-    for b in range(n_slots // size):
-        rows = slice(b * 4 * size, (b + 1) * 4 * size)
-        pick = jnp.where(offset == column[rows], 1.0, 0.0)
-        blocks = []
-        for q in range(4):
-            chosen = jnp.where(part_of == q, pick, 0.0).astype(BF16)
-            end = min(emb, (q + 1) * width)
-            blocks.append(mm(chosen, groups[b * 8 * size : (b + 1) * 8 * size, q * width : end]))
-        full = blocks[0] + blocks[1] + blocks[2]
-        whole_part = jnp.concatenate(
-            [full[:, :LANES] + blocks[3], full[:, LANES : 2 * LANES] + extra[rows], full[:, 2 * LANES :]],
+    offset = (iota((size, 8 * size), 1) - 8 * iota((size, 8 * size), 0)).astype(F32)
+    r, c = iota((4 * size, size), 0), iota((4 * size, size), 1)
+    move = [ones_where((c == 2 * (r // 8) + r % 2) & ((r % 8) // 2 == q)) for q in range(4)]
+    r, c = iota((4 * size, LANES), 0), iota((4 * size, LANES), 1)
+    source = jnp.where(r % 8 == 6, ((r // 8) % tensor) * askers + r // capacity, -LANES)
+    blocks = n_slots // size
+    outs = []
+    for b in range(blocks):
+        if b % (blocks // 2) == 0:
+            h = b // (blocks // 2)
+            pltpu.make_async_copy(
+                table_hbm.at[pl.ds(0, half * 8), :],
+                groups.at[pl.ds(h * half * 8, half * 8), :],
+                sems.at[1 + h],
+            ).wait()
+        pick = ones_where(offset == column[b * size : (b + 1) * size, :])
+        rows = mm(pick, groups[b * 8 * size : (b + 1) * 8 * size, :]).astype(BF16)
+        full = mm(move[0], rows[:, :width])
+        for q in (1, 2):
+            full = full + mm(move[q], rows[:, q * width : (q + 1) * width])
+        tail = mm(move[3], rows[:, 3 * width : emb])
+        squares = mm(ones_where(c == source + b * (size // slots)), extra)
+        full = jnp.concatenate(
+            [full[:, :LANES] + tail, full[:, LANES : 2 * LANES] + squares, full[:, 2 * LANES :]],
             axis=1,
         )
-        out_ref[b * size // 2 : (b + 1) * size // 2] = whole_part.astype(BF16).reshape(
-            size // 2, 8, width
-        )
+        span = pl.ds(b * size // 2, size // 2)
+        out_ref[b * size // 2 : (b + 1) * size // 2] = full.astype(BF16).reshape(size // 2, 8, width)
+        outs.append(pltpu.make_async_copy(out_ref.at[span], out_hbm.at[span], sems.at[3 + b]))
+        outs[-1].start()
+    for out in outs:
+        out.wait()
 
 
 def attention_kernel(
-    lens_ref, z_ref, ids_ref, x_ref, qw_hbm, kvw_hbm, key_hbm, val_hbm, ow_hbm,
+    lens_ref, ids_ref, x_ref, qw_hbm, kvw_hbm, key_hbm, val_hbm, ow_hbm,
     out_ref, map_ref, qw, kvw, key, val, ow, sems, *, mapping,
 ):
     seqs, width = x_ref.shape
@@ -248,7 +286,7 @@
     ]
     for copy in copies:
         copy.start()
-    slot_map_kernel(z_ref, ids_ref, map_ref, **mapping)
+    slot_map_kernel(ids_ref, map_ref, **mapping)
     x = x_ref[...]
     copies[0].wait()
     query = mm(x, qw[...]).astype(BF16)
@@ -358,9 +396,9 @@
         copy.wait()
 
 
-def final_kernel(z_ref, got_ref, value_ref, hidden_ref, out_ref):
+def final_kernel(got_ref, value_ref, hidden_ref, out_ref):
     part = out_ref.shape[1]
-    first = pl.multiple_of(z_ref[0] * part, LANES)
+    first = pl.multiple_of(lax.axis_index("tensor") * part, LANES)
     total = got_ref[0].astype(F32)
     for p in range(1, got_ref.shape[0]):
         total = total + got_ref[p].astype(F32)
@@ -389,7 +427,6 @@
     rows_dev, emb = table.shape
     owners = lax.axis_size("table")
     tensor = lax.axis_size("tensor")
-    me_table, me_tensor = lax.axis_index("table"), lax.axis_index("tensor")
     part = width // tensor
     capacity = 2 * requests // owners
     slots = capacity // tensor
@@ -401,66 +438,78 @@
     hbm = pl.BlockSpec(memory_space=pl.ANY)
     ids_t = lookup_ids.T
 
-    send = pl.pallas_call(
-        send_ids_kernel,
-        out_shape=jax.ShapeDtypeStruct((owners, per, LANES), I32),
-        name="send_ids",
-    )(ids_t)
-    got_ids = lax.all_to_all(send, "table", 0, 0, tiled=True)
-
     def near(x):
         return pltpu.with_memory_space_constraint(x, pltpu.VMEM)
 
-    me = me_table.astype(I32).reshape(1)
-    z = me_tensor.astype(I32).reshape(1)
-    chunks = (256, 256, 512, 1024, 1024, 1024)
-    squares, u, attn_in = pl.pallas_call(
-        lambda *refs: squares_kernel(*refs, chunks=chunks),
-        in_specs=[smem, vmem, hbm, hbm, hbm, hbm],
-        out_specs=[vmem, vmem, vmem],
+    def other(x, step):
+        return lax.ppermute(x, "tensor", [(i, i ^ step) for i in range(tensor)])
+
+    send, u, attn_in, key_t = pl.pallas_call(
+        start_kernel,
+        in_specs=[hbm] * 4,
+        out_specs=[hbm] + [vmem] * 3,
         out_shape=[
-            pltpu.VMEM((rows_dev // LANES, LANES), F32),
-            jax.ShapeDtypeStruct((seqs, emb), BF16),
-            jax.ShapeDtypeStruct(hidden.shape, BF16),
+            jax.ShapeDtypeStruct((owners, per, LANES), I32),
+            pltpu.VMEM((seqs, emb), BF16),
+            pltpu.VMEM(hidden.shape, BF16),
+            pltpu.VMEM((part, emb), BF16),
         ],
         scratch_shapes=[
+            pltpu.VMEM(ids_t.shape, I32),
+            pltpu.VMEM(attn_gain.shape, F32),
             pltpu.VMEM(hidden.shape, BF16),
             pltpu.VMEM(key_proj.shape, BF16),
-            pltpu.VMEM(table.shape, BF16),
-            pltpu.VMEM((part, emb), BF16),
-            pltpu.SemaphoreType.DMA((len(chunks) + 2,)),
+            pltpu.VMEM((owners, per, LANES), I32),
+            pltpu.SemaphoreType.DMA((5,)),
+        ],
+        name="start",
+    )(ids_t, attn_gain, hidden, key_proj)
+    more_u = other(u, 1)
+    got_ids = lax.all_to_all(send, "table", 0, 0, tiled=True)
+
+    u = (u.astype(F32) + more_u.astype(F32)).astype(BF16)
+    more_u = other(u, 2)
+
+    chunks = (256, 256, 512, 1024)
+    more_chunks = (1024, 1024)
+    early_rows = sum(chunks)
+    squares = pl.pallas_call(
+        lambda *refs: squares_kernel(*refs, chunks=chunks),
+        in_specs=[vmem, hbm],
+        out_specs=vmem,
+        out_shape=pltpu.VMEM((early_rows // LANES, LANES), F32),
+        scratch_shapes=[
+            pltpu.VMEM((early_rows, emb), BF16),
+            pltpu.SemaphoreType.DMA((len(chunks),)),
         ],
         name="squares",
-    )(z, attn_gain, hidden, key_proj, table, send)
-
-    def other(x, step):
-        return lax.ppermute(x, "tensor", [(i, i ^ step) for i in range(tensor)])
-
-    more_u = other(u, 1)
+    )(near(key_t), table)
+
     packed = pl.pallas_call(
         lambda *refs: gather_kernel(
-            *refs, rows_dev=rows_dev, per=per, capacity=capacity, tensor=tensor
+            *refs, rows_dev=rows_dev, per=per, capacity=capacity, tensor=tensor, chunks=more_chunks
         ),
-        in_specs=[smem, smem, vmem, vmem, hbm],
-        out_specs=vmem,
+        in_specs=[vmem, vmem, vmem, hbm],
+        out_specs=hbm,
         out_shape=jax.ShapeDtypeStruct((owners * tensor, 8, 3 * LANES), BF16),
         scratch_shapes=[
             pltpu.VMEM((n_slots // LANES, LANES), I32),
             pltpu.SMEM((n_slots // LANES, LANES), I32),
             pltpu.VMEM((n_slots * 8, emb), BF16),
-            pltpu.SemaphoreType.DMA((2,)),
+            pltpu.VMEM((owners * tensor, 8, 3 * LANES), BF16),
+            pltpu.VMEM((rows_dev - early_rows, emb), BF16),
+            pltpu.VMEM((rows_dev // LANES, LANES), F32),
+            pltpu.SemaphoreType.DMA((11,)),
+            pltpu.SemaphoreType.DMA((len(more_chunks),)),
         ],
         name="gather",
-    )(me, z, near(got_ids.reshape(owners * per, LANES)), near(squares), table)
+    )(near(got_ids.reshape(owners * per, LANES)), near(squares), near(key_t), table)
     got_rows = lax.all_to_all(packed, ("table", "tensor"), 0, 0, tiled=True)
-    u = (u.astype(F32) + more_u.astype(F32)).astype(BF16)
-    more_u = other(u, 2)
-
     _, kv_width = key_cache.shape[1:]
     mapping = dict(rows_dev=rows_dev, owners=owners, seqs=seqs, lookups=lookups, capacity=capacity, tensor=tensor)
     attention, slot_map = pl.pallas_call(
         lambda *refs: attention_kernel(*refs, mapping=mapping),
-        in_specs=[smem, smem, vmem, vmem, hbm, hbm, hbm, hbm, hbm],
+        in_specs=[smem, vmem, vmem, hbm, hbm, hbm, hbm, hbm],
         out_specs=[vmem, vmem],
         out_shape=[
             pltpu.VMEM((seqs, width), BF16),
@@ -476,7 +525,7 @@
         ],
         name="attention",
     )(
-        cache_lengths, z, ids_t, attn_in, q_weight,
+        cache_lengths, ids_t, near(attn_in), q_weight,
         kv_weight.reshape(2 * width, kv_width), key_cache, value_cache, out_weight,
     )
 
@@ -500,11 +549,11 @@
 
     return pl.pallas_call(
         final_kernel,
-        in_specs=[smem] + [vmem] * 3,
+        in_specs=[vmem] * 3,
         out_specs=vmem,
         out_shape=jax.ShapeDtypeStruct((seqs, part), BF16),
         name="final",
-    )(z, near(got_mixes), near(value_near), near(hidden_near))
+    )(near(got_mixes), near(value_near), near(hidden_near))
 
 
 def solution(mesh):

time: 80.9 us -> 76 us (0.939)
  Pallas kernels: 34.1 us -> 29.3 us
    pallas_call x1, Pallas kernels: 11.8 us -> 6.14 us  [body(): pl.pallas_call(lambda *refs: squares_kernel(*refs, chunks=chunks), in_spe...]
    pallas_call x2, Pallas kernels: 2.6 us -> 3.43 us  [the longest x1 2.23 us: body(): pl.pallas_call(start_kernel, in_specs=[hbm] * 4, out_specs=[hbm] + [vmem]...]
  transfers between devices with their start and end apart: 5 -> 5, of which waited for: 2 -> 2; matrix products, arithmetic and copies ran while one was open for 0% -> 0% of each run, Pallas kernels for 25% -> 18%
where the time goes in v5:
time: 76 us; the launch traced here: 75.6 us
  Pallas kernels  29.3 us (39%)
  starting transfers between devices  28 us (37%)
  waiting for transfers between devices  18.2 us (24%)
    all_to_all x1, starting transfers between devices, body(): got_rows = lax.all_to_all(packed, ('table', 'tensor'), 0, 0, tiled=True)  11.7 us
    ppermute x2, waiting for transfers between devices, other(): return lax.ppermute(x, 'tensor', [(i, i ^ step) for i in range(tensor)])  10.6 us
    pallas_call x1, Pallas kernels, body(): pl.pallas_call(lambda *refs: gather_kernel(*refs, rows_dev=rows_dev, per=...  9.56 us
    all_to_all x1, waiting for transfers between devices, body(): got_mixes = lax.all_to_all(mixes, 'tensor', 0, 0, tiled=True)  7.65 us
    all_to_all x1, starting transfers between devices, body(): got_ids = lax.all_to_all(send, 'table', 0, 0, tiled=True)  7.52 us
    pallas_call x1, Pallas kernels, body(): pl.pallas_call(lambda *refs: attention_kernel(*refs, mapping=mapping), in...  6.39 us
    pallas_call x1, Pallas kernels, body(): pl.pallas_call(lambda *refs: squares_kernel(*refs, chunks=chunks), in_spe...  6.14 us
    ppermute x2, starting transfers between devices, other(): return lax.ppermute(x, 'tensor', [(i, i ^ step) for i in range(tensor)])  5.32 us
  transfers between devices with their start and end apart: 5, of which 2 were waited for; matrix products, arithmetic and copies ran while one was open for 0% of the time, Pallas kernels for 18%

profile of v5, /device:TPU:10, one launch (start us, length us, event | category | flops | bytes accessed | tf_op | source)
XLA Modules:
  0.0 75.6 jit_solution(12187746702848303401)
XLA Ops:
  0.0 2.2 %start.1 = (s32[32,4,128]{2,1,0:T(4,128)}, bf16[32,1280]{1,0:T(8,128)(2,1)S(1)}, bf16[32,2560]{1,0:T(8,128)(2,1)S(1)}, bf16[640,1280]{1,0:T(8,128)(2,1)S(1)}) custom-call(s32[16,32]{1,0:T(8,128)} %bitcast.5, f32[2560]{0:T(1024)} %gain_hbm.1, bf16[32,2560]{1,0:T(8,128)(2,1)} %hidden_hbm.3, bf16[1280,640]{1,0:T(8,128)(2,1)} %key_hbm.1), custom_call_target="tpu_custom_call" | custom-call | tf_op jit(solution)/shard_map/start/pallas_call | solution.py:447
  2.2 7.5 %all-to-all-start = ((s32[32,4,128]{2,1,0:T(4,128)}), s32[32,4,128]{2,1,0:T(4,128)S(1)}, u32[]{:S(2)}, u32[]{:S(2)}) async-start(s32[32,4,128]{2,1,0:T(4,128)} %get-tuple-element.13), calls=%async_computation | async-start | bytes 131072 | tf_op jit(solution)/shard_map/all_to_all | solution.py:468
  9.8 6.1 %squares.1.refs_1_ = f32[16,128]{1,0:T(8,128)S(1)} custom-call(bf16[640,1280]{1,0:T(8,128)(2,1)S(1)} %get-tuple-element.14.refs_0_.refs_2_, bf16[4096,1280]{1,0:T(8,128)(2,1)} %refs_3_.2), custom_call_target="tpu_custom_call" | custom-call | tf_op jit(solution)/shard_map/squares/pallas_call | solution.py:476
  15.9 0.0 all-to-all-done
  15.9 9.6 %gather.1 = bf16[128,8,384]{2,1,0:T(8,128)(2,1)} custom-call(s32[128,128]{1,0:T(8,128)S(1)} %bitcast.3, f32[16,128]{1,0:T(8,128)S(1)} %squares.1.refs_1_, bf16[640,1280]{1,0:T(8,128)(2,1)S(1)} %get-tuple-element.14.refs_0_.refs_2_, bf16[4096,1280]{1,0:T(8,128)(2,1)} %refs_3_.2), custom_call_target="tpu_custom_call" | custom-call | tf_op jit(solution)/shard_map/gather/pallas_call | solution.py:488
  25.5 11.7 %all-to-all-start.1 = ((bf16[128,8,384]{2,1,0:T(8,128)(2,1)}), bf16[128,8,384]{2,1,0:T(8,128)(2,1)S(1)}, u32[]{:S(2)}, u32[]{:S(2)}) async-start(bf16[128,8,384]{2,1,0:T(8,128)(2,1)} %gather.1), calls=%async_computation.1 | async-start | bytes 1572864 | tf_op jit(solution)/shard_map/all_to_all | solution.py:507
  37.2 1.7 %collective-permute-start = (bf16[32,1280]{1,0:T(8,128)(2,1)S(1)}, bf16[32,1280]{1,0:T(8,128)(2,1)S(1)}, u32[]{:S(2)}, u32[]{:S(2)}) collective-permute-start(bf16[32,1280]{1,0:T(8,128)(2,1)S(1)} %get-tuple-element.17), channel_id=1, source_target_pairs={{0,1},{1,0},{2,3},{3,2},{4,5},{5,4},{6,7},{7,6},{8,9},{9,8},{10,11... | collective-permute-start | bytes 245768 | tf_op jit(solution)/shard_map/ppermute | solution.py:445
  38.9 10.6 %collective-permute-done = bf16[32,1280]{1,0:T(8,128)(2,1)S(1)} collective-permute-done((bf16[32,1280]{1,0:T(8,128)(2,1)S(1)}, bf16[32,1280]{1,0:T(8,128)(2,1)S(1)}, u32[]{:S(2)}, u32[]{:S(2)}) %collective-permute-start) | collective-permute-done | bytes 81952 | tf_op jit(solution)/shard_map/ppermute | solution.py:445
  49.5 3.6 %collective-permute-start.1 = (bf16[32,1280]{1,0:T(8,128)(2,1)S(1)}, bf16[32,1280]{1,0:T(8,128)(2,1)S(1)}, u32[]{:S(2)}, u32[]{:S(2)}) collective-permute-start(bf16[32,1280]{1,0:T(8,128)(2,1)S(1)} %add_convert_fusion.refs_2_), channel_id=1, source_target_pairs={{0,2},{1,3},{2,0},{3,1},{4,6},{5,7},{6,4},{7,5},{8,10},{9,11},{10,... | collective-permute-start | bytes 245768 | tf_op jit(solution)/shard_map/ppermute | solution.py:445
  53.1 6.4 %attention.1 = (bf16[32,2560]{1,0:T(8,128)(2,1)S(1)}, bf16[1024,128]{1,0:T(8,128)(2,1)S(1)}) custom-call(s32[32]{0:T(128)} %refs_0_.1, s32[16,32]{1,0:T(8,128)} %bitcast.6, bf16[32,2560]{1,0:T(8,128)(2,1)S(1)} %get-tuple-element.15.refs_2_, bf16[2560,640]{1,0:T(8,128)(2,1)} %refs_3_.3, bf16[5120,128]{1,0:T(8,128)(2,1)} %bitcast.4, ...), custom_call_target="tpu_custom_call" | custom-call | tf_op jit(solution)/shard_map/attention/pallas_call | solution.py:510
  59.5 0.0 collective-permute-done.1.refs_3_
  59.5 0.0 all-to-all-done.1.refs_0_
  59.5 2.3 %mix.1.order_ref = bf16[4,32,1920]{2,1,0:T(8,128)(2,1)} custom-call(bf16[128,8,384]{2,1,0:T(8,128)(2,1)S(1)} %all-to-all-done.1.refs_0_, bf16[1024,128]{1,0:T(8,128)(2,1)S(1)} %get-tuple-element.16.refs_1_, bf16[32,1280]{1,0:T(8,128)(2,1)S(1)} %add_convert_fusion.refs_2_, bf16[32,1280]{1,0:T(8,128)(2,1)S(1)} %collective-permute-done.1.refs_3_, ...), custom_call_target="tpu_custom_call" | custom-call | tf_op jit(solution)/shard_map/mix/pallas_call | solution.py:532
  61.8 3.5 %all-to-all-start.2 = ((bf16[4,32,1920]{2,1,0:T(8,128)(2,1)}), bf16[4,32,1920]{2,1,0:T(8,128)(2,1)S(1)}, u32[]{:S(2)}, u32[]{:S(2)}) async-start(bf16[4,32,1920]{2,1,0:T(8,128)(2,1)} %mix.1.order_ref), calls=%async_computation.2 | async-start | bytes 983040 | tf_op jit(solution)/shard_map/all_to_all | solution.py:539
  65.3 1.5 %fetch_value.1 = (bf16[1280,640]{1,0:T(8,128)(2,1)S(1)}, bf16[32,2560]{1,0:T(8,128)(2,1)S(1)}) custom-call(bf16[1280,640]{1,0:T(8,128)(2,1)} %value_hbm.1, bf16[32,2560]{1,0:T(8,128)(2,1)} %hidden_hbm.3, bf16[4,32,1920]{2,1,0:T(8,128)(2,1)} %mix.1.order_ref), custom_call_target="tpu_custom_call" | custom-call | tf_op jit(solution)/shard_map/fetch_value/pallas_call | solution.py:541
  66.7 7.6 %all-to-all-done.2.got_ref = bf16[4,32,1920]{2,1,0:T(8,128)(2,1)S(1)} async-done(((bf16[4,32,1920]{2,1,0:T(8,128)(2,1)}), bf16[4,32,1920]{2,1,0:T(8,128)(2,1)S(1)}, u32[]{:S(2)}, u32[]{:S(2)}) %all-to-all-start.2) | async-done | bytes 491552 | tf_op jit(solution)/shard_map/all_to_all | solution.py:539
  74.4 1.2 %final.1 = bf16[32,640]{1,0:T(8,128)(2,1)} custom-call(bf16[4,32,1920]{2,1,0:T(8,128)(2,1)S(1)} %all-to-all-done.2.got_ref, bf16[1280,640]{1,0:T(8,128)(2,1)S(1)} %get-tuple-element.19.value_ref, bf16[32,2560]{1,0:T(8,128)(2,1)S(1)} %get-tuple-element.20.hidden_ref), custom_call_target="tpu_custom_call" | custom-call | tf_op jit(solution)/shard_map/final/pallas_call | solution.py:550
  (1 shorter events, 0.0 us)
Async XLA Ops:
  2.2 13.7 %all-to-all-start = ((s32[32,4,128]{2,1,0:T(4,128)}), s32[32,4,128]{2,1,0:T(4,128)S(1)}, u32[]{:S(2)}, u32[]{:S(2)}) async-start(s32[32,4,128]{2,1,0:T(4,128)} %get-tuple-element.13), calls=%async_computation | async-start | bytes 131072 | tf_op jit(solution)/shard_map/all_to_all | solution.py:468
  25.5 34.0 %all-to-all-start.1 = ((bf16[128,8,384]{2,1,0:T(8,128)(2,1)}), bf16[128,8,384]{2,1,0:T(8,128)(2,1)S(1)}, u32[]{:S(2)}, u32[]{:S(2)}) async-start(bf16[128,8,384]{2,1,0:T(8,128)(2,1)} %gather.1), calls=%async_computation.1 | async-start | bytes 1572864 | tf_op jit(solution)/shard_map/all_to_all | solution.py:507
  37.2 12.3 %collective-permute-start = (bf16[32,1280]{1,0:T(8,128)(2,1)S(1)}, bf16[32,1280]{1,0:T(8,128)(2,1)S(1)}, u32[]{:S(2)}, u32[]{:S(2)}) collective-permute-start(bf16[32,1280]{1,0:T(8,128)(2,1)S(1)} %get-tuple-element.17), channel_id=1, source_target_pairs={{0,1},{1,0},{2,3},{3,2},{4,5},{5,4},{6,7},{7,6},{8,9},{9,8},{10,11... | collective-permute-start | bytes 245768 | tf_op jit(solution)/shard_map/ppermute | solution.py:445
  49.5 10.0 %collective-permute-start.1 = (bf16[32,1280]{1,0:T(8,128)(2,1)S(1)}, bf16[32,1280]{1,0:T(8,128)(2,1)S(1)}, u32[]{:S(2)}, u32[]{:S(2)}) collective-permute-start(bf16[32,1280]{1,0:T(8,128)(2,1)S(1)} %add_convert_fusion.refs_2_), channel_id=1, source_target_pairs={{0,2},{1,3},{2,0},{3,1},{4,6},{5,7},{6,4},{7,5},{8,10},{9,11},{10,... | collective-permute-start | bytes 245768 | tf_op jit(solution)/shard_map/ppermute | solution.py:445
  61.8 12.6 %all-to-all-start.2 = ((bf16[4,32,1920]{2,1,0:T(8,128)(2,1)}), bf16[4,32,1920]{2,1,0:T(8,128)(2,1)S(1)}, u32[]{:S(2)}, u32[]{:S(2)}) async-start(bf16[4,32,1920]{2,1,0:T(8,128)(2,1)} %mix.1.order_ref), calls=%async_computation.2 | async-start | bytes 983040 | tf_op jit(solution)/shard_map/all_to_all | solution.py:539

commit v6 on v5

--- a/solution.py
+++ b/solution.py
@@ -199,10 +199,10 @@
 
     def issue(step):
         for s in range(step * each, (step + 1) * each):
-            base = pl.multiple_of((idx_smem[s // LANES, s % LANES] // 8) * 8, 8)
+            base = pl.multiple_of((idx_smem[s // LANES, s % LANES] // 2) * 2, 2)
             pltpu.make_async_copy(
-                table_hbm.at[pl.ds(base, 8), :],
-                groups.at[pl.ds(s * 8, 8), :],
+                table_hbm.at[pl.ds(base, 2), :],
+                groups.at[pl.ds(s * 2, 2), :],
                 sems.at[1 + s // half],
             ).start()
 
@@ -223,14 +223,14 @@
             line = line + (part if p == 0 else pltpu.roll(part, slots * p, 1))
         extra.append(line.astype(BF16))
     extra = jnp.concatenate(extra, axis=0)
-    spread = jnp.broadcast_to((own.astype(I32) % 8)[:, None, :], (askers, slots, LANES))
+    spread = jnp.broadcast_to((own.astype(I32) % 2)[:, None, :], (askers, slots, LANES))
     spread = spread.reshape(n_slots, LANES).astype(F32)
     keep = iota((n_slots, LANES), 1) == iota((n_slots, LANES), 0) % slots
     column = jnp.sum(jnp.where(keep, spread, 0.0), axis=1, keepdims=True)
-    size = 32
+    size = 64
     width = out_ref.shape[2]
     emb = groups.shape[1]
-    offset = (iota((size, 8 * size), 1) - 8 * iota((size, 8 * size), 0)).astype(F32)
+    offset = (iota((size, 2 * size), 1) - 2 * iota((size, 2 * size), 0)).astype(F32)
     r, c = iota((4 * size, size), 0), iota((4 * size, size), 1)
     move = [ones_where((c == 2 * (r // 8) + r % 2) & ((r % 8) // 2 == q)) for q in range(4)]
     r, c = iota((4 * size, LANES), 0), iota((4 * size, LANES), 1)
@@ -241,12 +241,12 @@
         if b % (blocks // 2) == 0:
             h = b // (blocks // 2)
             pltpu.make_async_copy(
-                table_hbm.at[pl.ds(0, half * 8), :],
-                groups.at[pl.ds(h * half * 8, half * 8), :],
+                table_hbm.at[pl.ds(0, half * 2), :],
+                groups.at[pl.ds(h * half * 2, half * 2), :],
                 sems.at[1 + h],
             ).wait()
         pick = ones_where(offset == column[b * size : (b + 1) * size, :])
-        rows = mm(pick, groups[b * 8 * size : (b + 1) * 8 * size, :]).astype(BF16)
+        rows = mm(pick, groups[b * 2 * size : (b + 1) * 2 * size, :]).astype(BF16)
         full = mm(move[0], rows[:, :width])
         for q in (1, 2):
             full = full + mm(move[q], rows[:, q * width : (q + 1) * width])
@@ -495,7 +495,7 @@
         scratch_shapes=[
             pltpu.VMEM((n_slots // LANES, LANES), I32),
             pltpu.SMEM((n_slots // LANES, LANES), I32),
-            pltpu.VMEM((n_slots * 8, emb), BF16),
+            pltpu.VMEM((n_slots * 2, emb), BF16),
             pltpu.VMEM((owners * tensor, 8, 3 * LANES), BF16),
             pltpu.VMEM((rows_dev - early_rows, emb), BF16),
             pltpu.VMEM((rows_dev // LANES, LANES), F32),

time: 76 us -> 75.2 us (0.989)
  Pallas kernels: 29.3 us -> 28.4 us
    pallas_call x1, Pallas kernels: 9.56 us -> 8.75 us  [body(): pl.pallas_call(lambda *refs: gather_kernel(*refs, rows_dev=rows_dev, per=...]
  transfers between devices with their start and end apart: 5 -> 5, of which waited for: 2 -> 2; matrix products, arithmetic and copies ran while one was open for 0% -> 0% of each run, Pallas kernels for 18% -> 19%
where the time goes in v6:
time: 75.2 us; the launch traced here: 74.8 us
  Pallas kernels  28.4 us (38%)
  starting transfers between devices  28 us (37%)
  waiting for transfers between devices  18.2 us (24%)
    all_to_all x1, starting transfers between devices, body(): got_rows = lax.all_to_all(packed, ('table', 'tensor'), 0, 0, tiled=True)  11.7 us
    ppermute x2, waiting for transfers between devices, other(): return lax.ppermute(x, 'tensor', [(i, i ^ step) for i in range(tensor)])  10.6 us
    pallas_call x1, Pallas kernels, body(): pl.pallas_call(lambda *refs: gather_kernel(*refs, rows_dev=rows_dev, per=...  8.75 us
    all_to_all x1, waiting for transfers between devices, body(): got_mixes = lax.all_to_all(mixes, 'tensor', 0, 0, tiled=True)  7.64 us
    all_to_all x1, starting transfers between devices, body(): got_ids = lax.all_to_all(send, 'table', 0, 0, tiled=True)  7.52 us
    pallas_call x1, Pallas kernels, body(): pl.pallas_call(lambda *refs: attention_kernel(*refs, mapping=mapping), in...  6.39 us
    pallas_call x1, Pallas kernels, body(): pl.pallas_call(lambda *refs: squares_kernel(*refs, chunks=chunks), in_spe...  6.14 us
    ppermute x2, starting transfers between devices, other(): return lax.ppermute(x, 'tensor', [(i, i ^ step) for i in range(tensor)])  5.32 us
  transfers between devices with their start and end apart: 5, of which 2 were waited for; matrix products, arithmetic and copies ran while one was open for 0% of the time, Pallas kernels for 19%

profile of v6, /device:TPU:10, one launch (start us, length us, event | category | flops | bytes accessed | tf_op | source)
XLA Modules:
  0.0 74.8 jit_solution(6908066486513688079)
XLA Ops:
  0.0 2.2 %start.1 = (s32[32,4,128]{2,1,0:T(4,128)}, bf16[32,1280]{1,0:T(8,128)(2,1)S(1)}, bf16[32,2560]{1,0:T(8,128)(2,1)S(1)}, bf16[640,1280]{1,0:T(8,128)(2,1)S(1)}) custom-call(s32[16,32]{1,0:T(8,128)} %bitcast.5, f32[2560]{0:T(1024)} %gain_hbm.1, bf16[32,2560]{1,0:T(8,128)(2,1)} %hidden_hbm.3, bf16[1280,640]{1,0:T(8,128)(2,1)} %key_hbm.1), custom_call_target="tpu_custom_call" | custom-call | tf_op jit(solution)/shard_map/start/pallas_call | solution.py:447
  2.2 7.5 %all-to-all-start = ((s32[32,4,128]{2,1,0:T(4,128)}), s32[32,4,128]{2,1,0:T(4,128)S(1)}, u32[]{:S(2)}, u32[]{:S(2)}) async-start(s32[32,4,128]{2,1,0:T(4,128)} %get-tuple-element.13), calls=%async_computation | async-start | bytes 131072 | tf_op jit(solution)/shard_map/all_to_all | solution.py:468
  9.8 6.1 %squares.1.refs_1_ = f32[16,128]{1,0:T(8,128)S(1)} custom-call(bf16[640,1280]{1,0:T(8,128)(2,1)S(1)} %get-tuple-element.14.refs_0_.refs_2_, bf16[4096,1280]{1,0:T(8,128)(2,1)} %refs_3_.2), custom_call_target="tpu_custom_call" | custom-call | tf_op jit(solution)/shard_map/squares/pallas_call | solution.py:476
  15.9 0.0 all-to-all-done
  15.9 8.8 %gather.1 = bf16[128,8,384]{2,1,0:T(8,128)(2,1)} custom-call(s32[128,128]{1,0:T(8,128)S(1)} %bitcast.3, f32[16,128]{1,0:T(8,128)S(1)} %squares.1.refs_1_, bf16[640,1280]{1,0:T(8,128)(2,1)S(1)} %get-tuple-element.14.refs_0_.refs_2_, bf16[4096,1280]{1,0:T(8,128)(2,1)} %refs_3_.2), custom_call_target="tpu_custom_call" | custom-call | tf_op jit(solution)/shard_map/gather/pallas_call | solution.py:488
  24.7 11.7 %all-to-all-start.1 = ((bf16[128,8,384]{2,1,0:T(8,128)(2,1)}), bf16[128,8,384]{2,1,0:T(8,128)(2,1)S(1)}, u32[]{:S(2)}, u32[]{:S(2)}) async-start(bf16[128,8,384]{2,1,0:T(8,128)(2,1)} %gather.1), calls=%async_computation.1 | async-start | bytes 1572864 | tf_op jit(solution)/shard_map/all_to_all | solution.py:507
  36.4 1.7 %collective-permute-start = (bf16[32,1280]{1,0:T(8,128)(2,1)S(1)}, bf16[32,1280]{1,0:T(8,128)(2,1)S(1)}, u32[]{:S(2)}, u32[]{:S(2)}) collective-permute-start(bf16[32,1280]{1,0:T(8,128)(2,1)S(1)} %get-tuple-element.17), channel_id=1, source_target_pairs={{0,1},{1,0},{2,3},{3,2},{4,5},{5,4},{6,7},{7,6},{8,9},{9,8},{10,11... | collective-permute-start | bytes 245768 | tf_op jit(solution)/shard_map/ppermute | solution.py:445
  38.1 10.6 %collective-permute-done = bf16[32,1280]{1,0:T(8,128)(2,1)S(1)} collective-permute-done((bf16[32,1280]{1,0:T(8,128)(2,1)S(1)}, bf16[32,1280]{1,0:T(8,128)(2,1)S(1)}, u32[]{:S(2)}, u32[]{:S(2)}) %collective-permute-start) | collective-permute-done | bytes 81952 | tf_op jit(solution)/shard_map/ppermute | solution.py:445
  48.7 3.6 %collective-permute-start.1 = (bf16[32,1280]{1,0:T(8,128)(2,1)S(1)}, bf16[32,1280]{1,0:T(8,128)(2,1)S(1)}, u32[]{:S(2)}, u32[]{:S(2)}) collective-permute-start(bf16[32,1280]{1,0:T(8,128)(2,1)S(1)} %add_convert_fusion.refs_2_), channel_id=1, source_target_pairs={{0,2},{1,3},{2,0},{3,1},{4,6},{5,7},{6,4},{7,5},{8,10},{9,11},{10,... | collective-permute-start | bytes 245768 | tf_op jit(solution)/shard_map/ppermute | solution.py:445
  52.3 6.4 %attention.1 = (bf16[32,2560]{1,0:T(8,128)(2,1)S(1)}, bf16[1024,128]{1,0:T(8,128)(2,1)S(1)}) custom-call(s32[32]{0:T(128)} %refs_0_.1, s32[16,32]{1,0:T(8,128)} %bitcast.6, bf16[32,2560]{1,0:T(8,128)(2,1)S(1)} %get-tuple-element.15.refs_2_, bf16[2560,640]{1,0:T(8,128)(2,1)} %refs_3_.3, bf16[5120,128]{1,0:T(8,128)(2,1)} %bitcast.4, ...), custom_call_target="tpu_custom_call" | custom-call | tf_op jit(solution)/shard_map/attention/pallas_call | solution.py:510
  58.7 0.0 collective-permute-done.1.refs_3_
  58.7 0.0 all-to-all-done.1.refs_0_
  58.7 2.3 %mix.1.order_ref = bf16[4,32,1920]{2,1,0:T(8,128)(2,1)} custom-call(bf16[128,8,384]{2,1,0:T(8,128)(2,1)S(1)} %all-to-all-done.1.refs_0_, bf16[1024,128]{1,0:T(8,128)(2,1)S(1)} %get-tuple-element.16.refs_1_, bf16[32,1280]{1,0:T(8,128)(2,1)S(1)} %add_convert_fusion.refs_2_, bf16[32,1280]{1,0:T(8,128)(2,1)S(1)} %collective-permute-done.1.refs_3_, ...), custom_call_target="tpu_custom_call" | custom-call | tf_op jit(solution)/shard_map/mix/pallas_call | solution.py:532
  61.0 3.5 %all-to-all-start.2 = ((bf16[4,32,1920]{2,1,0:T(8,128)(2,1)}), bf16[4,32,1920]{2,1,0:T(8,128)(2,1)S(1)}, u32[]{:S(2)}, u32[]{:S(2)}) async-start(bf16[4,32,1920]{2,1,0:T(8,128)(2,1)} %mix.1.order_ref), calls=%async_computation.2 | async-start | bytes 983040 | tf_op jit(solution)/shard_map/all_to_all | solution.py:539
  64.5 1.5 %fetch_value.1 = (bf16[1280,640]{1,0:T(8,128)(2,1)S(1)}, bf16[32,2560]{1,0:T(8,128)(2,1)S(1)}) custom-call(bf16[1280,640]{1,0:T(8,128)(2,1)} %value_hbm.1, bf16[32,2560]{1,0:T(8,128)(2,1)} %hidden_hbm.3, bf16[4,32,1920]{2,1,0:T(8,128)(2,1)} %mix.1.order_ref), custom_call_target="tpu_custom_call" | custom-call | tf_op jit(solution)/shard_map/fetch_value/pallas_call | solution.py:541
  65.9 7.6 %all-to-all-done.2.got_ref = bf16[4,32,1920]{2,1,0:T(8,128)(2,1)S(1)} async-done(((bf16[4,32,1920]{2,1,0:T(8,128)(2,1)}), bf16[4,32,1920]{2,1,0:T(8,128)(2,1)S(1)}, u32[]{:S(2)}, u32[]{:S(2)}) %all-to-all-start.2) | async-done | bytes 491552 | tf_op jit(solution)/shard_map/all_to_all | solution.py:539
  73.6 1.2 %final.1 = bf16[32,640]{1,0:T(8,128)(2,1)} custom-call(bf16[4,32,1920]{2,1,0:T(8,128)(2,1)S(1)} %all-to-all-done.2.got_ref, bf16[1280,640]{1,0:T(8,128)(2,1)S(1)} %get-tuple-element.19.value_ref, bf16[32,2560]{1,0:T(8,128)(2,1)S(1)} %get-tuple-element.20.hidden_ref), custom_call_target="tpu_custom_call" | custom-call | tf_op jit(solution)/shard_map/final/pallas_call | solution.py:550
  (1 shorter events, 0.0 us)
Async XLA Ops:
  2.2 13.7 %all-to-all-start = ((s32[32,4,128]{2,1,0:T(4,128)}), s32[32,4,128]{2,1,0:T(4,128)S(1)}, u32[]{:S(2)}, u32[]{:S(2)}) async-start(s32[32,4,128]{2,1,0:T(4,128)} %get-tuple-element.13), calls=%async_computation | async-start | bytes 131072 | tf_op jit(solution)/shard_map/all_to_all | solution.py:468
  24.7 34.0 %all-to-all-start.1 = ((bf16[128,8,384]{2,1,0:T(8,128)(2,1)}), bf16[128,8,384]{2,1,0:T(8,128)(2,1)S(1)}, u32[]{:S(2)}, u32[]{:S(2)}) async-start(bf16[128,8,384]{2,1,0:T(8,128)(2,1)} %gather.1), calls=%async_computation.1 | async-start | bytes 1572864 | tf_op jit(solution)/shard_map/all_to_all | solution.py:507
  36.4 12.3 %collective-permute-start = (bf16[32,1280]{1,0:T(8,128)(2,1)S(1)}, bf16[32,1280]{1,0:T(8,128)(2,1)S(1)}, u32[]{:S(2)}, u32[]{:S(2)}) collective-permute-start(bf16[32,1280]{1,0:T(8,128)(2,1)S(1)} %get-tuple-element.17), channel_id=1, source_target_pairs={{0,1},{1,0},{2,3},{3,2},{4,5},{5,4},{6,7},{7,6},{8,9},{9,8},{10,11... | collective-permute-start | bytes 245768 | tf_op jit(solution)/shard_map/ppermute | solution.py:445
  48.7 10.0 %collective-permute-start.1 = (bf16[32,1280]{1,0:T(8,128)(2,1)S(1)}, bf16[32,1280]{1,0:T(8,128)(2,1)S(1)}, u32[]{:S(2)}, u32[]{:S(2)}) collective-permute-start(bf16[32,1280]{1,0:T(8,128)(2,1)S(1)} %add_convert_fusion.refs_2_), channel_id=1, source_target_pairs={{0,2},{1,3},{2,0},{3,1},{4,6},{5,7},{6,4},{7,5},{8,10},{9,11},{10,... | collective-permute-start | bytes 245768 | tf_op jit(solution)/shard_map/ppermute | solution.py:445
  61.0 12.6 %all-to-all-start.2 = ((bf16[4,32,1920]{2,1,0:T(8,128)(2,1)}), bf16[4,32,1920]{2,1,0:T(8,128)(2,1)S(1)}, u32[]{:S(2)}, u32[]{:S(2)}) async-start(bf16[4,32,1920]{2,1,0:T(8,128)(2,1)} %mix.1.order_ref), calls=%async_computation.2 | async-start | bytes 983040 | tf_op jit(solution)/shard_map/all_to_all | solution.py:539

commit v7 on v6

--- a/solution.py
+++ b/solution.py
@@ -125,7 +125,7 @@
         copy.wait()
         for t in range(start, start + size, sub):
             if between is not None and t == 0:
-                for i in range(sum(chunks) // sub):
+                for i in range(4):
                     between(i)
             keys = mm_nt(key_t[...], table[t : t + sub, :])
             line = jnp.sum(keys * keys, axis=0, keepdims=True)
@@ -194,7 +194,7 @@
         row = jnp.where(lane == k, ranked(k), row)
     to_smem.wait()
     half = n_slots // 2
-    steps = sum(chunks) // 256
+    steps = 4
     each = n_slots // steps
 
     def issue(step):
@@ -360,8 +360,8 @@
     same = ones_where((r // 8 == c // 8) & (r % 2 == c % 2))
     sums = []
     for b in range(0, total, LANES):
-        high, mid, low = three_parts(cross_all[b : b + LANES, :])
-        sums.append(mm(same, high) + (mm(same, mid) + mm(same, low)))
+        high, low = two_parts(cross_all[b : b + LANES, :])
+        sums.append(mm(same, high) + mm(same, low))
     cross = jnp.sum(jnp.concatenate(sums, axis=0), axis=1, keepdims=True)
     owners = total // 32
     row = iota((total, LANES), 0)
@@ -470,8 +470,8 @@
     u = (u.astype(F32) + more_u.astype(F32)).astype(BF16)
     more_u = other(u, 2)
 
-    chunks = (256, 256, 512, 1024)
-    more_chunks = (1024, 1024)
+    chunks = (256, 512, 768)
+    more_chunks = (1024, 1536)
     early_rows = sum(chunks)
     squares = pl.pallas_call(
         lambda *refs: squares_kernel(*refs, chunks=chunks),

time: 75.2 us -> 74.1 us (0.985)
  starting transfers between devices: 28 us -> 26.9 us
    all_to_all x1, starting transfers between devices: 11.7 us -> 10.6 us  [body(): got_rows = lax.all_to_all(packed, ('table', 'tensor'), 0, 0, tiled=True)]
    pallas_call x1, Pallas kernels: 6.14 us -> 5.1 us  [body(): pl.pallas_call(lambda *refs: squares_kernel(*refs, chunks=chunks), in_spe...]
    pallas_call x1, Pallas kernels: 8.75 us -> 9.58 us  [body(): pl.pallas_call(lambda *refs: gather_kernel(*refs, rows_dev=rows_dev, per=...]
  transfers between devices with their start and end apart: 5 -> 5, of which waited for: 2 -> 3; matrix products, arithmetic and copies ran while one was open for 0% -> 0% of each run, Pallas kernels for 19% -> 18%
where the time goes in v7:
time: 74.1 us; the launch traced here: 73.7 us
  Pallas kernels  28.1 us (38%)
  starting transfers between devices  26.9 us (36%)
  waiting for transfers between devices  18.5 us (25%)
    all_to_all x1, starting transfers between devices, body(): got_rows = lax.all_to_all(packed, ('table', 'tensor'), 0, 0, tiled=True)  10.6 us
    ppermute x2, waiting for transfers between devices, other(): return lax.ppermute(x, 'tensor', [(i, i ^ step) for i in range(tensor)])  10.6 us
    pallas_call x1, Pallas kernels, body(): pl.pallas_call(lambda *refs: gather_kernel(*refs, rows_dev=rows_dev, per=...  9.58 us
    all_to_all x1, waiting for transfers between devices, body(): got_mixes = lax.all_to_all(mixes, 'tensor', 0, 0, tiled=True)  7.64 us
    all_to_all x1, starting transfers between devices, body(): got_ids = lax.all_to_all(send, 'table', 0, 0, tiled=True)  7.52 us
    pallas_call x1, Pallas kernels, body(): pl.pallas_call(lambda *refs: attention_kernel(*refs, mapping=mapping), in...  6.39 us
    ppermute x2, starting transfers between devices, other(): return lax.ppermute(x, 'tensor', [(i, i ^ step) for i in range(tensor)])  5.32 us
    pallas_call x1, Pallas kernels, body(): pl.pallas_call(lambda *refs: squares_kernel(*refs, chunks=chunks), in_spe...  5.1 us
  transfers between devices with their start and end apart: 5, of which 3 were waited for; matrix products, arithmetic and copies ran while one was open for 0% of the time, Pallas kernels for 18%

profile of v7, /device:TPU:10, one launch (start us, length us, event | category | flops | bytes accessed | tf_op | source)
XLA Modules:
  0.0 73.7 jit_solution(4876025394342633861)
XLA Ops:
  0.0 2.2 %start.1 = (s32[32,4,128]{2,1,0:T(4,128)}, bf16[32,1280]{1,0:T(8,128)(2,1)S(1)}, bf16[32,2560]{1,0:T(8,128)(2,1)S(1)}, bf16[640,1280]{1,0:T(8,128)(2,1)S(1)}) custom-call(s32[16,32]{1,0:T(8,128)} %bitcast.5, f32[2560]{0:T(1024)} %gain_hbm.1, bf16[32,2560]{1,0:T(8,128)(2,1)} %hidden_hbm.3, bf16[1280,640]{1,0:T(8,128)(2,1)} %key_hbm.1), custom_call_target="tpu_custom_call" | custom-call | tf_op jit(solution)/shard_map/start/pallas_call | solution.py:447
  2.2 7.5 %all-to-all-start = ((s32[32,4,128]{2,1,0:T(4,128)}), s32[32,4,128]{2,1,0:T(4,128)S(1)}, u32[]{:S(2)}, u32[]{:S(2)}) async-start(s32[32,4,128]{2,1,0:T(4,128)} %get-tuple-element.13), calls=%async_computation | async-start | bytes 131072 | tf_op jit(solution)/shard_map/all_to_all | solution.py:468
  9.8 5.1 %squares.1.refs_1_ = f32[12,128]{1,0:T(8,128)S(1)} custom-call(bf16[640,1280]{1,0:T(8,128)(2,1)S(1)} %get-tuple-element.14.refs_0_.refs_2_, bf16[4096,1280]{1,0:T(8,128)(2,1)} %refs_3_.2), custom_call_target="tpu_custom_call" | custom-call | tf_op jit(solution)/shard_map/squares/pallas_call | solution.py:476
  14.9 0.3 all-to-all-done
  15.2 9.6 %gather.1 = bf16[128,8,384]{2,1,0:T(8,128)(2,1)} custom-call(s32[128,128]{1,0:T(8,128)S(1)} %bitcast.3, f32[12,128]{1,0:T(8,128)S(1)} %squares.1.refs_1_, bf16[640,1280]{1,0:T(8,128)(2,1)S(1)} %get-tuple-element.14.refs_0_.refs_2_, bf16[4096,1280]{1,0:T(8,128)(2,1)} %refs_3_.2), custom_call_target="tpu_custom_call" | custom-call | tf_op jit(solution)/shard_map/gather/pallas_call | solution.py:488
  24.8 10.6 %all-to-all-start.1 = ((bf16[128,8,384]{2,1,0:T(8,128)(2,1)}), bf16[128,8,384]{2,1,0:T(8,128)(2,1)S(1)}, u32[]{:S(2)}, u32[]{:S(2)}) async-start(bf16[128,8,384]{2,1,0:T(8,128)(2,1)} %gather.1), calls=%async_computation.1 | async-start | bytes 1572864 | tf_op jit(solution)/shard_map/all_to_all | solution.py:507
  35.4 1.7 %collective-permute-start = (bf16[32,1280]{1,0:T(8,128)(2,1)S(1)}, bf16[32,1280]{1,0:T(8,128)(2,1)S(1)}, u32[]{:S(2)}, u32[]{:S(2)}) collective-permute-start(bf16[32,1280]{1,0:T(8,128)(2,1)S(1)} %get-tuple-element.17), channel_id=1, source_target_pairs={{0,1},{1,0},{2,3},{3,2},{4,5},{5,4},{6,7},{7,6},{8,9},{9,8},{10,11... | collective-permute-start | bytes 245768 | tf_op jit(solution)/shard_map/ppermute | solution.py:445
  37.2 10.6 %collective-permute-done = bf16[32,1280]{1,0:T(8,128)(2,1)S(1)} collective-permute-done((bf16[32,1280]{1,0:T(8,128)(2,1)S(1)}, bf16[32,1280]{1,0:T(8,128)(2,1)S(1)}, u32[]{:S(2)}, u32[]{:S(2)}) %collective-permute-start) | collective-permute-done | bytes 81952 | tf_op jit(solution)/shard_map/ppermute | solution.py:445
  47.7 3.6 %collective-permute-start.1 = (bf16[32,1280]{1,0:T(8,128)(2,1)S(1)}, bf16[32,1280]{1,0:T(8,128)(2,1)S(1)}, u32[]{:S(2)}, u32[]{:S(2)}) collective-permute-start(bf16[32,1280]{1,0:T(8,128)(2,1)S(1)} %add_convert_fusion.refs_2_), channel_id=1, source_target_pairs={{0,2},{1,3},{2,0},{3,1},{4,6},{5,7},{6,4},{7,5},{8,10},{9,11},{10,... | collective-permute-start | bytes 245768 | tf_op jit(solution)/shard_map/ppermute | solution.py:445
  51.3 6.4 %attention.1 = (bf16[32,2560]{1,0:T(8,128)(2,1)S(1)}, bf16[1024,128]{1,0:T(8,128)(2,1)S(1)}) custom-call(s32[32]{0:T(128)} %refs_0_.1, s32[16,32]{1,0:T(8,128)} %bitcast.6, bf16[32,2560]{1,0:T(8,128)(2,1)S(1)} %get-tuple-element.15.refs_2_, bf16[2560,640]{1,0:T(8,128)(2,1)} %refs_3_.3, bf16[5120,128]{1,0:T(8,128)(2,1)} %bitcast.4, ...), custom_call_target="tpu_custom_call" | custom-call | tf_op jit(solution)/shard_map/attention/pallas_call | solution.py:510
  57.7 0.0 collective-permute-done.1.refs_3_
  57.7 0.0 all-to-all-done.1.refs_0_
  57.7 2.2 %mix.1.order_ref = bf16[4,32,1920]{2,1,0:T(8,128)(2,1)} custom-call(bf16[128,8,384]{2,1,0:T(8,128)(2,1)S(1)} %all-to-all-done.1.refs_0_, bf16[1024,128]{1,0:T(8,128)(2,1)S(1)} %get-tuple-element.16.refs_1_, bf16[32,1280]{1,0:T(8,128)(2,1)S(1)} %add_convert_fusion.refs_2_, bf16[32,1280]{1,0:T(8,128)(2,1)S(1)} %collective-permute-done.1.refs_3_, ...), custom_call_target="tpu_custom_call" | custom-call | tf_op jit(solution)/shard_map/mix/pallas_call | solution.py:532
  59.9 3.5 %all-to-all-start.2 = ((bf16[4,32,1920]{2,1,0:T(8,128)(2,1)}), bf16[4,32,1920]{2,1,0:T(8,128)(2,1)S(1)}, u32[]{:S(2)}, u32[]{:S(2)}) async-start(bf16[4,32,1920]{2,1,0:T(8,128)(2,1)} %mix.1.order_ref), calls=%async_computation.2 | async-start | bytes 983040 | tf_op jit(solution)/shard_map/all_to_all | solution.py:539
  63.4 1.5 %fetch_value.1 = (bf16[1280,640]{1,0:T(8,128)(2,1)S(1)}, bf16[32,2560]{1,0:T(8,128)(2,1)S(1)}) custom-call(bf16[1280,640]{1,0:T(8,128)(2,1)} %value_hbm.1, bf16[32,2560]{1,0:T(8,128)(2,1)} %hidden_hbm.3, bf16[4,32,1920]{2,1,0:T(8,128)(2,1)} %mix.1.order_ref), custom_call_target="tpu_custom_call" | custom-call | tf_op jit(solution)/shard_map/fetch_value/pallas_call | solution.py:541
  64.9 7.6 %all-to-all-done.2.got_ref = bf16[4,32,1920]{2,1,0:T(8,128)(2,1)S(1)} async-done(((bf16[4,32,1920]{2,1,0:T(8,128)(2,1)}), bf16[4,32,1920]{2,1,0:T(8,128)(2,1)S(1)}, u32[]{:S(2)}, u32[]{:S(2)}) %all-to-all-start.2) | async-done | bytes 491552 | tf_op jit(solution)/shard_map/all_to_all | solution.py:539
  72.5 1.2 %final.1 = bf16[32,640]{1,0:T(8,128)(2,1)} custom-call(bf16[4,32,1920]{2,1,0:T(8,128)(2,1)S(1)} %all-to-all-done.2.got_ref, bf16[1280,640]{1,0:T(8,128)(2,1)S(1)} %get-tuple-element.19.value_ref, bf16[32,2560]{1,0:T(8,128)(2,1)S(1)} %get-tuple-element.20.hidden_ref), custom_call_target="tpu_custom_call" | custom-call | tf_op jit(solution)/shard_map/final/pallas_call | solution.py:550
  (1 shorter events, 0.0 us)
Async XLA Ops:
  2.2 13.0 %all-to-all-start = ((s32[32,4,128]{2,1,0:T(4,128)}), s32[32,4,128]{2,1,0:T(4,128)S(1)}, u32[]{:S(2)}, u32[]{:S(2)}) async-start(s32[32,4,128]{2,1,0:T(4,128)} %get-tuple-element.13), calls=%async_computation | async-start | bytes 131072 | tf_op jit(solution)/shard_map/all_to_all | solution.py:468
  24.8 32.9 %all-to-all-start.1 = ((bf16[128,8,384]{2,1,0:T(8,128)(2,1)}), bf16[128,8,384]{2,1,0:T(8,128)(2,1)S(1)}, u32[]{:S(2)}, u32[]{:S(2)}) async-start(bf16[128,8,384]{2,1,0:T(8,128)(2,1)} %gather.1), calls=%async_computation.1 | async-start | bytes 1572864 | tf_op jit(solution)/shard_map/all_to_all | solution.py:507
  35.4 12.3 %collective-permute-start = (bf16[32,1280]{1,0:T(8,128)(2,1)S(1)}, bf16[32,1280]{1,0:T(8,128)(2,1)S(1)}, u32[]{:S(2)}, u32[]{:S(2)}) collective-permute-start(bf16[32,1280]{1,0:T(8,128)(2,1)S(1)} %get-tuple-element.17), channel_id=1, source_target_pairs={{0,1},{1,0},{2,3},{3,2},{4,5},{5,4},{6,7},{7,6},{8,9},{9,8},{10,11... | collective-permute-start | bytes 245768 | tf_op jit(solution)/shard_map/ppermute | solution.py:445
  47.7 10.0 %collective-permute-start.1 = (bf16[32,1280]{1,0:T(8,128)(2,1)S(1)}, bf16[32,1280]{1,0:T(8,128)(2,1)S(1)}, u32[]{:S(2)}, u32[]{:S(2)}) collective-permute-start(bf16[32,1280]{1,0:T(8,128)(2,1)S(1)} %add_convert_fusion.refs_2_), channel_id=1, source_target_pairs={{0,2},{1,3},{2,0},{3,1},{4,6},{5,7},{6,4},{7,5},{8,10},{9,11},{10,... | collective-permute-start | bytes 245768 | tf_op jit(solution)/shard_map/ppermute | solution.py:445
  59.9 12.6 %all-to-all-start.2 = ((bf16[4,32,1920]{2,1,0:T(8,128)(2,1)}), bf16[4,32,1920]{2,1,0:T(8,128)(2,1)S(1)}, u32[]{:S(2)}, u32[]{:S(2)}) async-start(bf16[4,32,1920]{2,1,0:T(8,128)(2,1)} %mix.1.order_ref), calls=%async_computation.2 | async-start | bytes 983040 | tf_op jit(solution)/shard_map/all_to_all | solution.py:539
